TPU v7x, 32 devices: a whole 2x2x4 slice. The times are simulated.
32 devices in a mesh: gx: 4 (over x, core), gy: 4 (over z), gz: 2 (over y).
Axes of the slice: x: 2, y: 2, z: 4, core: 2. Of those that a mesh axis runs over, the one named last changes fastest.
Arguments:
- relative_placements: float32 [3, 12, 12, 8, 128], P(None, 'gx', 'gy', 'gz'), may hold values from 0 to 1
- mass_per_density: float32 [12, 12, 8, 128], P('gx', 'gy', 'gz'), may hold values from 0.004 to 0.04
- opening_heat_level: float32 [12, 12, 8, 128], P('gx', 'gy', 'gz'), may hold values from 0.5 to 2
- bin_fill_counts: int32 [12, 12, 8], P('gx', 'gy', 'gz'), may hold values from 16 to 128
Outputs:
- final_temp: float32 [12, 12, 8, 128], P('gx', 'gy', 'gz')
Inputs may be any that keep to these rules, and one draw needn't show every extreme that they name: Tile cell t holds particles in slots 0 to bin_fill_counts[t] - 1; the other slots are empty and are no source.
All inputs are finite; a program needn't handle non-finite values.
Results may differ from a plain program's by a relative error of at most 0.0003.
Values sent between devices are 32-bit elements; how exact they have to be, the bound alone decides.
No kernel may reach another device: no remote copies, remote signals or barrier semaphores. Data moves between devices by JAX's collectives and lax.ppermute only.
A program may use at most 64 MiB of HBM per device.

v0:
```python
import jax
import jax.numpy as jnp
from jax import lax
from jax.sharding import PartitionSpec as P

step_factor = 2.0


def shifted(block, axis, distance):
    devices = range(lax.axis_size(axis))
    route = [((i - distance) % len(devices), i) for i in devices]
    return lax.ppermute(block, axis, route)


def with_halo(value, sides, width):
    for axis, dim in sides:
        size, length = (lax.axis_size(axis), value.shape[dim])
        up = [(i, (i + 1) % size) for i in range(size)]
        down = [(j, i) for i, j in up]
        last = lax.slice_in_dim(value, length - width, length, axis=dim)
        leading = lax.slice_in_dim(value, 0, width, axis=dim)
        before = lax.ppermute(last, axis, up)
        after = lax.ppermute(leading, axis, down)
        value = jnp.concatenate([before, value, after], axis=dim)
    return value


def paired(fields, periodic_enclosure):
    extent_x, extent_y, extent_z = periodic_enclosure
    bin_dimensions = fields.shape[-1]
    forward = [(0, 0, 0)] + [
        (sx, sy, sz)
        for sx in (-1, 0, 1)
        for sy in (-1, 0, 1)
        for sz in (-1, 0, 1)
        if (sx, sy, sz) > (0, 0, 0)
    ]

    def visit(column, totals):
        col_x = column // extent_y
        col_y = column % extent_y

        def column_at(shift_x, shift_y):
            column_part = lax.dynamic_slice_in_dim(fields, col_x + 1 + shift_x, 1, 1)
            column_part = lax.dynamic_slice_in_dim(column_part, col_y + 1 + shift_y, 1, 2)
            return column_part[:, 0, 0]

        target = column_at(0, 0)[:, 1 : 1 + extent_z]
        own_part = jnp.zeros((2, extent_z, bin_dimensions), jnp.float32)
        for shift_x, shift_y, shift_z in forward:
            source = column_at(shift_x, shift_y)[:, 1 + shift_z : 1 + shift_z + extent_z]
            dist_sq = (float(shift_x) + source[0][:, None, :] - target[0][:, :, None]) ** 2
            dist_sq = (
                dist_sq + (float(shift_y) + source[1][:, None, :] - target[1][:, :, None]) ** 2
            )
            dist_sq = (
                dist_sq + (float(shift_z) + source[2][:, None, :] - target[2][:, :, None]) ** 2
            )
            kernel = jnp.maximum(1.0 - jnp.sqrt(dist_sq), 0.0) ** 3
            shared = kernel * (target[5][:, :, None] + source[5][:, None, :])
            spread = source[4][:, None, :] - target[4][:, :, None]
            toward_target = shared * source[3][:, None, :]
            own_part = own_part + jnp.stack(
                [jnp.sum(toward_target * spread, axis=2), jnp.sum(toward_target, axis=2)]
            )
            if (shift_x, shift_y, shift_z) != (0, 0, 0):
                toward_source = shared * target[3][:, :, None]
                returned = jnp.stack(
                    [-jnp.sum(toward_source * spread, axis=1), jnp.sum(toward_source, axis=1)]
                )
                corner = (0, col_x + 1 + shift_x, col_y + 1 + shift_y, 1 + shift_z, 0)
                window = lax.dynamic_slice(totals, corner, (2, 1, 1, extent_z, bin_dimensions))
                totals = lax.dynamic_update_slice(
                    totals, window + returned.reshape((2, 1, 1, extent_z, bin_dimensions)), corner
                )
        corner = (0, col_x + 1, col_y + 1, 1, 0)
        window = lax.dynamic_slice(totals, corner, (2, 1, 1, extent_z, bin_dimensions))
        return lax.dynamic_update_slice(
            totals, window + own_part.reshape((2, 1, 1, extent_z, bin_dimensions)), corner
        )

    totals = jnp.zeros((2, extent_x + 2, extent_y + 2, extent_z + 2, bin_dimensions), jnp.float32)
    return lax.fori_loop(0, extent_x * extent_y, visit, totals)


def fold_back(totals):
    for shift_by in (1, -1):
        rim = totals[:, -1] if shift_by == 1 else totals[:, 0]
        arrived = shifted(rim, "gx", shift_by)
        if shift_by == 1:
            totals = totals.at[:, 1].add(arrived)
        else:
            totals = totals.at[:, -2].add(arrived)
    totals = totals[:, 1:-1]
    for shift_by in (1, -1):
        rim = totals[:, :, -1] if shift_by == 1 else totals[:, :, 0]
        arrived = shifted(rim, "gy", shift_by)
        if shift_by == 1:
            totals = totals.at[:, :, 1].add(arrived)
        else:
            totals = totals.at[:, :, -2].add(arrived)
    totals = totals[:, :, 1:-1]
    for shift_by in (1, -1):
        rim = totals[:, :, :, -1] if shift_by == 1 else totals[:, :, :, 0]
        arrived = shifted(rim, "gz", shift_by)
        if shift_by == 1:
            totals = totals.at[:, :, :, 1].add(arrived)
        else:
            totals = totals.at[:, :, :, -2].add(arrived)
    totals = totals[:, :, :, 1:-1]
    return (totals[0], totals[1])


def with_temp(fields, temp):
    return jnp.concatenate([fields[:4], temp[None], fields[5:6]], axis=0)


def step_size(row_sums):
    largest = lax.pmax(jnp.max(row_sums), ("gx", "gy", "gz"))
    return step_factor / largest


def section_halo(temp):
    return with_halo(temp, (("gx", 0), ("gy", 1), ("gz", 2)), 1)


def local(relative_placements, mass_per_density, opening_heat_level, bin_fill_counts):
    bin_dimensions = opening_heat_level.shape[-1]
    occupied = (
        jnp.arange(bin_dimensions, dtype=jnp.int32)[None, None, None, :]
        < bin_fill_counts[..., None]
    ).astype(jnp.float32)
    smoothed_particle_measure = mass_per_density * occupied
    layered_buffers = jnp.concatenate(
        [relative_placements, smoothed_particle_measure[None], opening_heat_level[None]], axis=0
    )
    periodic_enclosure = opening_heat_level.shape[:3]
    near = with_halo(layered_buffers, (("gx", 1), ("gy", 2), ("gz", 3)), 1)
    fields = jnp.concatenate([near, (near[4] ** 2.5)[None]], axis=0)

    def flows(section_fields):
        return fold_back(paired(section_fields, periodic_enclosure))

    reference_heat_rate, row_sums = flows(fields)
    super_interval_length = step_size(row_sums * occupied)
    leading_subset = opening_heat_level + 2.0 / 15.0 * super_interval_length * reference_heat_rate
    initial_flow, unused_one = flows(with_temp(fields, section_halo(leading_subset)))
    second = (
        1.5 * leading_subset
        - 0.5 * opening_heat_level
        + 0.6 * super_interval_length * initial_flow
        - 0.4 * super_interval_length * reference_heat_rate
    )
    flow_second, unused_two = flows(with_temp(fields, section_halo(second)))
    final_temp = (
        25.0 / 12.0 * second
        - 5.0 / 6.0 * leading_subset
        - 0.25 * opening_heat_level
        + 5.0 / 6.0 * super_interval_length * flow_second
        - 5.0 / 9.0 * super_interval_length * reference_heat_rate
    )
    return final_temp


def solution(mesh):
    in_specs = (
        P(None, "gx", "gy", "gz", None),
        P("gx", "gy", "gz", None),
        P("gx", "gy", "gz", None),
        P("gx", "gy", "gz"),
    )
    out_specs = P("gx", "gy", "gz", None)
    return jax.shard_map(local, mesh=mesh, in_specs=in_specs, out_specs=out_specs, check_vma=False)
```

profile of v0, /device:TPU:0, one launch (start us, length us, event | category | flops | bytes accessed | tf_op | source)
XLA Modules:
  0.0 387.4 jit_solution(11387767187985435500)
XLA Ops:
  5.8 2.3 collective-permute-start.2
  8.1 2.1 collective-permute-start.3
  10.2 2.1 collective-permute-done.2
  15.9 2.7 collective-permute-done.4
  20.0 77.0 %while.72 = (s32[]{:T(128)}, f32[2,5,5,6,128]{4,3,0,2,1:T(8,128)S(1)}, f32[6,5,5,6,128]{4,3,0,2,1:T(8,128)S(1)}, s32[]{:T(128)}, s32[]{:T(128)}, /*index=5*/s32[...) while((s32[]{:T(128)}, f32[2,5,5,6,128]{4,3,0,2,1:T(8,128)S(1)}, ...), condition=%wide.region_55.56_spmd, body=%wide.region_0.55_spmd.sunk | while | flops 21871652 | bytes 1245886 | solution.py:83
  97.2 3.3 collective-permute-done.6
  103.4 4.4 %collective-permute-done.8 = f32[2,3,6,128]{3,0,2,1:T(2,128)S(1)} collective-permute-done((f32[2,3,6,128]{3,0,2,1:T(2,128)S(1)}, f32[2,3,6,128]{3,0,2,1:T(2,128)S(1)}, u32[]{:S(2)}, u32[]{:S(2)}) %collective-permute-start.8) | collective-permute-done | bytes 18464 | tf_op jit(solution)/shard_map/ppermute | solution.py:12
  108.8 2.8 collective-permute-done.9
  112.9 2.5 collective-permute-done.10
  116.7 2.5 collective-permute-done.11
  119.9 38.4 %pmax.7 = f32[]{:T(128)} all-reduce(f32[]{:T(128)} %select_reduce_fusion), channel_id=1, replica_groups=mesh['gx'=4,'gy'=4,'gz'=2] {'gx','gy','gz'}, use_global_device_ids=true, to_apply=%region_57.58 | all-reduce | flops 1 | bytes 8 | tf_op jit(solution)/shard_map/pmax | solution.py:119
  162.2 2.2 collective-permute-start.14
  168.0 2.5 collective-permute-start.16
  174.4 77.1 %while.73 = (s32[]{:T(128)}, f32[2,5,5,6,128]{4,3,0,2,1:T(8,128)S(1)}, f32[6,5,5,6,128]{4,3,0,2,1:T(8,128)S(1)}, s32[]{:T(128)}, s32[]{:T(128)}, /*index=5*/s32[...) while((s32[]{:T(128)}, ...), condition=%wide.region_113.114_spmd, body=%wide.region_58.113_spmd.sunk | while | flops 21871652 | bytes 1245886 | solution.py:83
  251.6 3.4 collective-permute-done.18
  258.2 4.2 %collective-permute-done.20 = f32[2,3,6,128]{3,2,1,0:T(8,128)S(1)} collective-permute-done((f32[2,3,6,128]{3,2,1,0:T(8,128)S(1)}, f32[2,3,6,128]{3,2,1,0:T(8,128)S(1)}, u32[]{:S(2)}, u32[]{:S(2)}) %collective-permute-start.20) | collective-permute-done | bytes 18464 | tf_op jit(solution)/shard_map/ppermute | solution.py:12
  264.2 2.1 collective-permute-done.21
  266.6 3.5 collective-permute-done.22
  270.4 3.5 collective-permute-done.23
  277.2 3.8 collective-permute-start.27
  286.8 77.2 %while.74 = (s32[]{:T(128)}, f32[2,5,5,6,128]{4,3,0,2,1:T(8,128)S(1)}, f32[6,5,5,6,128]{4,3,0,2,1:T(8,128)S(1)}, s32[]{:T(128)}, s32[]{:T(128)}, /*index=5*/s32[...) while((s32[]{:T(128)}, ...), condition=%wide.region_169.170_spmd, body=%wide.region_114.169_spmd.sunk | while | flops 21871652 | bytes 1245886 | solution.py:83
  364.1 3.4 collective-permute-done.30
  370.2 4.8 %collective-permute-done.32 = f32[2,3,6,128]{3,2,1,0:T(8,128)S(1)} collective-permute-done((f32[2,3,6,128]{3,2,1,0:T(8,128)S(1)}, f32[2,3,6,128]{3,2,1,0:T(8,128)S(1)}, u32[]{:S(2)}, u32[]{:S(2)}) %collective-permute-start.32) | collective-permute-done | bytes 18464 | tf_op jit(solution)/shard_map/ppermute | solution.py:12
  375.0 2.1 collective-permute-start.33
  (1328 shorter events, 278.2 us)
Async XLA Ops:
  1.6 4.0 %collective-permute-start = (f32[5,1,3,4,128]{4,3,0,2,1:T(4,128)S(1)}, f32[5,1,3,4,128]{4,3,0,2,1:T(4,128)S(1)}, u32[]{:S(2)}, u32[]{:S(2)}) collective-permute-start(f32[5,1,3,4,128]{4,3,0,2,1:T(4,128)S(1)} %get-tuple-element.1266), channel_id=1, source_target_pairs={{0,8},{8,16},{16,24},{24,0},{1,9},{9,17},{17,25},{25,1},{2,10},{10... | collective-permute-start | bytes 92168 | tf_op jit(solution)/shard_map/ppermute | solution.py:22
  5.8 6.5 %collective-permute-start.2 = (f32[5,5,1,4,128]{4,3,0,2,1:T(4,128)S(1)}, f32[5,5,1,4,128]{4,3,0,2,1:T(4,128)S(1)}, u32[]{:S(2)}, u32[]{:S(2)}) collective-permute-start(f32[5,5,1,4,128]{4,3,0,2,1:T(4,128)S(1)} %get-tuple-element.1264), channel_id=1, source_target_pairs={{0,2},{2,4},{4,6},{6,0},{1,3},{3,5},{5,7},{7,1},{8,10},{10,12},{12... | collective-permute-start | bytes 153608 | tf_op jit(solution)/shard_map/ppermute | solution.py:22
  8.1 5.6 %collective-permute-start.3 = (f32[5,5,1,4,128]{4,3,0,2,1:T(4,128)S(1)}, f32[5,5,1,4,128]{4,3,0,2,1:T(4,128)S(1)}, u32[]{:S(2)}, u32[]{:S(2)}) collective-permute-start(f32[5,5,1,4,128]{4,3,0,2,1:T(4,128)S(1)} %get-tuple-element.1265), channel_id=1, source_target_pairs={{2,0},{4,2},{6,4},{0,6},{3,1},{5,3},{7,5},{1,7},{10,8},{12,10},{14... | collective-permute-start | bytes 153608 | tf_op jit(solution)/shard_map/ppermute | solution.py:23
  13.9 4.8 %collective-permute-start.4 = (f32[5,5,5,1,128]{4,3,0,2,1:T(1,128)S(1)}, f32[5,5,5,1,128]{4,3,0,2,1:T(1,128)S(1)}, u32[]{:S(2)}, u32[]{:S(2)}) collective-permute-start(f32[5,5,5,1,128]{4,3,0,2,1:T(1,128)S(1)} %get-tuple-element.1262), channel_id=1, source_target_pairs={{0,1},{1,0},{2,3},{3,2},{4,5},{5,4},{6,7},{7,6},{8,9},{9,8},{10,11... | collective-permute-start | bytes 192008 | tf_op jit(solution)/shard_map/ppermute | solution.py:22
  15.2 4.3 %collective-permute-start.5 = (f32[5,5,5,1,128]{4,3,0,2,1:T(1,128)S(1)}, f32[5,5,5,1,128]{4,3,0,2,1:T(1,128)S(1)}, u32[]{:S(2)}, u32[]{:S(2)}) collective-permute-start(f32[5,5,5,1,128]{4,3,0,2,1:T(1,128)S(1)} %get-tuple-element.1263), channel_id=1, source_target_pairs={{1,0},{0,1},{3,2},{2,3},{5,4},{4,5},{7,6},{6,7},{9,8},{8,9},{11,10... | collective-permute-start | bytes 192008 | tf_op jit(solution)/shard_map/ppermute | solution.py:23
  102.2 5.6 %collective-permute-start.8 = (f32[2,3,6,128]{3,0,2,1:T(2,128)S(1)}, f32[2,3,6,128]{3,0,2,1:T(2,128)S(1)}, u32[]{:S(2)}, u32[]{:S(2)}) collective-permute-start(f32[2,3,6,128]{3,0,2,1:T(2,128)S(1)} %slice_bitcast_fusion.187), channel_id=1, source_target_pairs={{6,0},{0,2},{2,4},{4,6},{7,1},{1,3},{3,5},{5,7},{14,8},{8,10},{10,... | collective-permute-start | bytes 55304 | tf_op jit(solution)/shard_map/ppermute | solution.py:12
  107.8 3.8 collective-permute-start.9
  111.7 3.7 collective-permute-start.10
  115.4 3.7 collective-permute-start.11
  162.2 5.5 %collective-permute-start.14 = (f32[5,1,4,128]{3,2,0,1:T(4,128)S(1)}, f32[5,1,4,128]{3,2,0,1:T(4,128)S(1)}, u32[]{:S(2)}, u32[]{:S(2)}) collective-permute-start(f32[5,1,4,128]{3,2,0,1:T(4,128)S(1)} %get-tuple-element.1276), channel_id=1, source_target_pairs={{0,2},{2,4},{4,6},{6,0},{1,3},{3,5},{5,7},{7,1},{8,10},{10,12},{12... | collective-permute-start | bytes 30728 | tf_op jit(solution)/shard_map/ppermute | solution.py:22
  168.0 4.2 %collective-permute-start.16 = (f32[5,5,1,128]{3,2,0,1:T(1,128)S(1)}, f32[5,5,1,128]{3,2,0,1:T(1,128)S(1)}, u32[]{:S(2)}, u32[]{:S(2)}) collective-permute-start(f32[5,5,1,128]{3,2,0,1:T(1,128)S(1)} %get-tuple-element.1272), channel_id=1, source_target_pairs={{0,1},{1,0},{2,3},{3,2},{4,5},{5,4},{6,7},{7,6},{8,9},{9,8},{10,11... | collective-permute-start | bytes 38408 | tf_op jit(solution)/shard_map/ppermute | solution.py:22
  170.5 3.7 collective-permute-start.17
  256.8 5.7 %collective-permute-start.20 = (f32[2,3,6,128]{3,2,1,0:T(8,128)S(1)}, f32[2,3,6,128]{3,2,1,0:T(8,128)S(1)}, u32[]{:S(2)}, u32[]{:S(2)}) collective-permute-start(f32[2,3,6,128]{3,2,1,0:T(8,128)S(1)} %slice_bitcast_fusion.184), channel_id=1, source_target_pairs={{6,0},{0,2},{2,4},{4,6},{7,1},{1,3},{3,5},{5,7},{14,8},{8,10},{10,... | collective-permute-start | bytes 55304 | tf_op jit(solution)/shard_map/ppermute | solution.py:12
  262.4 3.9 %collective-permute-start.21 = (f32[2,3,6,128]{3,2,1,0:T(8,128)S(1)}, f32[2,3,6,128]{3,2,1,0:T(8,128)S(1)}, u32[]{:S(2)}, u32[]{:S(2)}) collective-permute-start(f32[2,3,6,128]{3,2,1,0:T(8,128)S(1)} %slice_bitcast_fusion.183), channel_id=1, source_target_pairs={{2,0},{4,2},{6,4},{0,6},{3,1},{5,3},{7,5},{1,7},{10,8},{12,10},{14... | collective-permute-start | bytes 55304 | tf_op jit(solution)/shard_map/ppermute | solution.py:12
  266.4 3.7 collective-permute-start.22
  270.2 3.7 collective-permute-start.23
  277.2 5.5 %collective-permute-start.26 = (f32[5,1,4,128]{3,2,0,1:T(4,128)S(1)}, f32[5,1,4,128]{3,2,0,1:T(4,128)S(1)}, u32[]{:S(2)}, u32[]{:S(2)}) collective-permute-start(f32[5,1,4,128]{3,2,0,1:T(4,128)S(1)} %get-tuple-element.1274), channel_id=1, source_target_pairs={{0,2},{2,4},{4,6},{6,0},{1,3},{3,5},{5,7},{7,1},{8,10},{10,12},{12... | collective-permute-start | bytes 30728 | tf_op jit(solution)/shard_map/ppermute | solution.py:22
  277.2 5.5 %collective-permute-start.27 = (f32[5,1,4,128]{3,2,0,1:T(4,128)S(1)}, f32[5,1,4,128]{3,2,0,1:T(4,128)S(1)}, u32[]{:S(2)}, u32[]{:S(2)}) collective-permute-start(f32[5,1,4,128]{3,2,0,1:T(4,128)S(1)} %get-tuple-element.1275), channel_id=1, source_target_pairs={{2,0},{4,2},{6,4},{0,6},{3,1},{5,3},{7,5},{1,7},{10,8},{12,10},{14... | collective-permute-start | bytes 30728 | tf_op jit(solution)/shard_map/ppermute | solution.py:23
  282.7 3.8 collective-permute-start.28
  282.9 3.7 collective-permute-start.29
  369.3 5.7 %collective-permute-start.32 = (f32[2,3,6,128]{3,2,1,0:T(8,128)S(1)}, f32[2,3,6,128]{3,2,1,0:T(8,128)S(1)}, u32[]{:S(2)}, u32[]{:S(2)}) collective-permute-start(f32[2,3,6,128]{3,2,1,0:T(8,128)S(1)} %slice_bitcast_fusion.181), channel_id=1, source_target_pairs={{6,0},{0,2},{2,4},{4,6},{7,1},{1,3},{3,5},{5,7},{14,8},{8,10},{10,... | collective-permute-start | bytes 55304 | tf_op jit(solution)/shard_map/ppermute | solution.py:12
  375.0 4.1 %collective-permute-start.33 = (f32[2,3,6,128]{3,2,1,0:T(8,128)S(1)}, f32[2,3,6,128]{3,2,1,0:T(8,128)S(1)}, u32[]{:S(2)}, u32[]{:S(2)}) collective-permute-start(f32[2,3,6,128]{3,2,1,0:T(8,128)S(1)} %slice_bitcast_fusion.180), channel_id=1, source_target_pairs={{2,0},{4,2},{6,4},{0,6},{3,1},{5,3},{7,5},{1,7},{10,8},{12,10},{14... | collective-permute-start | bytes 55304 | tf_op jit(solution)/shard_map/ppermute | solution.py:12
  379.1 3.7 collective-permute-start.34
  383.0 3.7 collective-permute-start.35
  (15 other events, 50.2 us)
where the time goes:
time: 388 us; the launch traced here: 387 us
  other arithmetic  190 us (49%)
  waiting for transfers between devices  72 us (19%)
  starting transfers between devices  39.9 us (10%)
  blocking collectives  38.4 us (10%)
  local copies, waits for them, and re-layouts  36.3 us (9%)
  loops' own time  9.42 us (2%)
    reduce_sum x189, other arithmetic, visit(): jnp.sum(toward_target * spread, axis=2)  178 us
    ppermute x18, waiting for transfers between devices, shifted(): return lax.ppermute(block, axis, route)  51.4 us
    pmax x1, blocking collectives, step_size(): largest = lax.pmax(jnp.max(row_sums), ('gx', 'gy', 'gz'))  38.4 us
    dynamic_update_slice x243, local copies, waits for them, and re-layouts, visit(): lax.dynamic_update_slice(totals, window + returned.reshape((2, 1, 1, exte...  30.3 us
    ppermute x9, starting transfers between devices, with_halo(): after = lax.ppermute(leading, axis, down)  15.7 us
    ppermute x9, waiting for transfers between devices, with_halo(): before = lax.ppermute(last, axis, up)  15.5 us
    ppermute x18, starting transfers between devices, shifted(): return lax.ppermute(block, axis, route)  14.9 us
    another operation x3, loops' own time, paired(): return lax.fori_loop(0, extent_x * extent_y, visit, totals)  9.42 us
  transfers between devices with their start and end apart: 36, of which 33 were waited for; matrix products, arithmetic and copies ran while one was open for 0% of the time, Pallas kernels for 0%

commit v1 on v0

v1 whole, which is shorter than its diff:
```python
import jax
import jax.numpy as jnp
from jax import lax
from jax.experimental import pallas as pl
from jax.experimental.pallas import tpu as pltpu
from jax.sharding import PartitionSpec as P

step_factor = 2.0
AXES = ("gx", "gy", "gz")
ROUNDER = 192.0
SHIFTS = (-1, 0, 1)
PAIRS = [(sx, sy) for sx in SHIFTS for sy in SHIFTS]


def swap_faces(value, axis, dim):
    size, length = lax.axis_size(axis), value.shape[dim]
    last = lax.slice_in_dim(value, length - 1, length, axis=dim)
    leading = lax.slice_in_dim(value, 0, 1, axis=dim)
    up = [(i, (i + 1) % size) for i in range(size)]
    if size == 2:
        both = lax.ppermute(jnp.concatenate([last, leading], axis=dim), axis, up)
        return lax.slice_in_dim(both, 0, 1, axis=dim), lax.slice_in_dim(both, 1, 2, axis=dim)
    down = [(j, i) for i, j in up]
    return lax.ppermute(last, axis, up), lax.ppermute(leading, axis, down)


def with_halo(value, first_dim):
    for place, axis in enumerate(AXES):
        dim = first_dim + place
        before, after = swap_faces(value, axis, dim)
        value = jnp.concatenate([before, value, after], axis=dim)
    return value


def rounded(x):
    return x.astype(jnp.bfloat16).astype(jnp.float32)


def split3(x):
    a = rounded(x)
    b = rounded(x - a)
    return a, b, x - a - b


def by_row(rows, row):
    out = rows[-1]
    for r in range(len(rows) - 2, -1, -1):
        out = jnp.where(row == r, rows[r], out)
    return out


class Sizes:
    def __init__(self, nx, ny, nz, slots):
        self.nx, self.ny, self.nz, self.slots = nx, ny, nz, slots
        self.px, self.py, self.pz = nx + 2, ny + 2, nz + 2
        self.cells = nx * ny * nz
        self.padded = self.px * self.py * self.pz
        self.half = nz // 2
        self.pairs = nx * ny * self.half
        self.columns = self.px * self.py

    def only_first(self):
        return 4 * self.slots * (4 * rounded_up(self.padded) + rounded_up(self.cells))

    def place(self, p):
        zp = p % self.half
        column = p // self.half
        return column // self.ny, column % self.ny, zp, column * self.nz + 2 * zp


def route(axis, distance):
    size = lax.axis_size(axis)
    return [(i, (i + distance) % size) for i in range(size)]


def rounded_up(rows):
    return -(-rows // 8) * 8


class Faces:
    def __init__(self, s):
        self.s = s
        self.x_rows = s.ny * s.nz
        self.y_rows = s.px * s.nz
        self.z_rows = s.px * s.py
        self.joined = lax.axis_size("gz") == 2

    def message(self, rows):
        return jax.ShapeDtypeStruct((rounded_up(rows + 1), self.s.slots), jnp.float32)

    def x_messages(self):
        return (self.message(self.x_rows),) * 2

    def y_messages(self):
        return (self.message(self.y_rows),) * 2

    def z_messages(self):
        return (self.message(2 * self.z_rows),) if self.joined else (self.message(self.z_rows),) * 2

    def row(self, x, y, z):
        return (x * self.s.py + y) * self.s.pz + z

    def put_own(self, halo, own):
        s = self.s
        for x in range(s.nx):
            for y in range(s.ny):
                at, start = self.row(x + 1, y + 1, 1), (x * s.ny + y) * s.nz
                halo[at : at + s.nz, :] = own[start : start + s.nz, :]

    def put_x(self, halo, before, after):
        s = self.s
        for side, x in ((before, 0), (after, s.nx + 1)):
            for y in range(s.ny):
                at = self.row(x, y + 1, 1)
                halo[at : at + s.nz, :] = side[y * s.nz : (y + 1) * s.nz, :]

    def put_y(self, halo, before, after):
        s = self.s
        for side, y in ((before, 0), (after, s.ny + 1)):
            for x in range(s.px):
                at = self.row(x, y, 1)
                halo[at : at + s.nz, :] = side[x * s.nz : (x + 1) * s.nz, :]

    def put_z(self, halo, sides):
        s = self.s
        for k, z in ((0, 0), (1, s.nz + 1)):
            side, base = (sides[0], k * self.z_rows) if self.joined else (sides[k], 0)
            for column in range(self.z_rows):
                halo[column * s.pz + z : column * s.pz + z + 1, :] = side[base + column : base + column + 1, :]

    def pack_x(self, own, top, up, down):
        s = self.s
        n = self.x_rows
        up[0:n, :] = own[(s.nx - 1) * n : s.nx * n, :]
        down[0:n, :] = own[0:n, :]
        for m in (up, down):
            m[n : n + 1, :] = top

    def pack_y(self, halo, top, up, down):
        s = self.s
        for x in range(s.px):
            for m, y in ((up, s.ny), (down, 1)):
                at = self.row(x, y, 1)
                m[x * s.nz : (x + 1) * s.nz, :] = halo[at : at + s.nz, :]
        for m in (up, down):
            m[self.y_rows : self.y_rows + 1, :] = top

    def pack_z(self, halo, top, messages):
        s = self.s
        for k, z in ((0, s.nz), (1, 1)):
            m, base = (messages[0], k * self.z_rows) if self.joined else (messages[k], 0)
            for column in range(self.z_rows):
                at = column * s.pz + z
                m[base + column : base + column + 1, :] = halo[at : at + 1, :]
        for m in messages:
            n = 2 * self.z_rows if self.joined else self.z_rows
            m[n : n + 1, :] = top

    def largest(self, rows, refs):
        return jnp.maximum(refs[0][rows : rows + 1, :], refs[-1][rows : rows + 1, :])

    def y_packer(self):
        s = self.s

        def body(own, top, before, after, up, down, top_out, halo):
            self.put_own(halo, own)
            self.put_x(halo, before, after)
            most = jnp.maximum(top[...], self.largest(self.x_rows, (before, after)))
            top_out[...] = most
            self.pack_y(halo, most, up, down)

        return pl.pallas_call(
            body,
            out_shape=(*self.y_messages(), jax.ShapeDtypeStruct((1, s.slots), jnp.float32)),
            scratch_shapes=[pltpu.VMEM((s.padded, s.slots), jnp.float32)],
            compiler_params=SMALL,
            name="pack_y",
        )

    def z_packer(self):
        s = self.s
        count = len(self.z_messages())

        def body(own, top, x0, x1, y0, y1, *rest):
            messages, top_out, halo = rest[:count], rest[count], rest[-1]
            self.put_own(halo, own)
            self.put_x(halo, x0, x1)
            self.put_y(halo, y0, y1)
            most = jnp.maximum(top[...], self.largest(self.y_rows, (y0, y1)))
            top_out[...] = most
            self.pack_z(halo, most, messages)

        return pl.pallas_call(
            body,
            out_shape=(*self.z_messages(), jax.ShapeDtypeStruct((1, s.slots), jnp.float32)),
            scratch_shapes=[pltpu.VMEM((s.padded, s.slots), jnp.float32)],
            compiler_params=SMALL,
            name="pack_z",
        )

    def exchange(self, own, top, up, down):
        x0 = lax.ppermute(up, "gx", route("gx", 1))
        x1 = lax.ppermute(down, "gx", route("gx", -1))
        up, down, top = self.y_packer()(own, top, x0, x1)
        y0 = lax.ppermute(up, "gy", route("gy", 1))
        y1 = lax.ppermute(down, "gy", route("gy", -1))
        *messages, top = self.z_packer()(own, top, x0, x1, y0, y1)
        if self.joined:
            z = (lax.ppermute(messages[0], "gz", route("gz", 1)),)
        else:
            z = (lax.ppermute(messages[0], "gz", route("gz", 1)), lax.ppermute(messages[1], "gz", route("gz", -1)))
        return (own, top, x0, x1, y0, y1, *z)

    def lay_out(self, halo, own, x0, x1, y0, y1, z):
        self.put_own(halo, own)
        self.put_x(halo, x0, x1)
        self.put_y(halo, y0, y1)
        self.put_z(halo, z)

    def latest_top(self, top, z):
        n = 2 * self.z_rows if self.joined else self.z_rows
        return jnp.maximum(top[...], self.largest(n, z))


SMALL = pltpu.CompilerParams(vmem_limit_bytes=2 << 20)
ROOM = 8 << 20


def weights_of(s, volume, conduct, temp, gains):
    row = lax.broadcasted_iota(jnp.int32, (8, s.slots), 0)
    use_c = (row % 4) < 2
    use_u = row < 4
    odd = (row % 2) == 1

    def one(cell, carry):
        def rows(ref):
            return jnp.broadcast_to(ref[pl.ds(cell, 1), :], (8, s.slots))

        full = rows(volume) * jnp.where(use_c, rows(conduct), 1.0)
        full = full * jnp.where(use_u, rows(temp), 1.0)
        top = rounded(full)
        gains[cell] = jnp.where(odd, full - top, top)
        return carry

    lax.fori_loop(0, s.padded, one, 0, unroll=6)


def gain_pair(gains, cell):
    both = jnp.concatenate([gains[cell], gains[cell + 1]], axis=0)
    return both.astype(jnp.bfloat16)


def keep_sums(s, total, own, sums):
    sums[own] = total[0:8, 0 : s.slots]
    sums[own + 1] = total[8:16, s.slots : 2 * s.slots]


def flow_from(s, sums_row, conduct_own, temp_own):
    def of(r):
        return sums_row(r)

    weight = of(4) + of(5) + conduct_own * (of(6) + of(7))
    flow = of(0) + of(1) + conduct_own * (of(2) + of(3)) - temp_own * weight
    return flow, weight


def first_kernel(s):
    slots = s.slots
    faces = Faces(s)

    def body(position, volume, temp, own_volume, own_temp, kernel_out, flow_out, conduct_out, top_out,
             up, down, left, gains, sums):
        conduct_out[...] = temp[...] * temp[...] * jnp.sqrt(temp[...])
        weights_of(s, volume, conduct_out, temp, gains)
        row = lax.broadcasted_iota(jnp.int32, (8, slots), 0)

        def axis_rows(cell, d):
            raw = position[d, pl.ds(cell, 1), :] - 0.5
            return jnp.broadcast_to((raw + ROUNDER) - ROUNDER, (8, slots))

        def features(column, carry):
            blocks = []
            for z in range(s.pz):
                cell = column * s.pz + z
                q = [axis_rows(cell, d) for d in range(3)]
                square = split3(q[0] * q[0] + q[1] * q[1] + q[2] * q[2])
                for d in range(3):
                    h = rounded(q[d])
                    m = q[d] - h
                    block = jnp.where(row % 2 == 0, h, m)
                    block = jnp.where(row < 4, block, jnp.where(row < 7, 1.0, square[d]))
                    blocks.append(block)
                blocks.append(jnp.zeros((8, slots), jnp.float32))
            for zp in range(s.half):
                quad = jnp.concatenate(blocks[8 * zp : 8 * zp + 16], axis=0)
                left[column * s.half + zp] = quad.T.astype(jnp.bfloat16)
            return carry

        lax.fori_loop(0, s.columns, features, 0)

        def target_rows(cell, d):
            q = axis_rows(cell, d)
            out = []
            for shift in SHIFTS:
                t = q - float(shift)
                h = rounded(t)
                m = t - h
                sq = split3(t * t)
                block = jnp.where(row < 2, -2.0 * h, -2.0 * m)
                rest = jnp.where(row == 4, sq[0], jnp.where(row == 5, sq[1], sq[2]))
                out.append(jnp.where(row < 4, block, jnp.where(row < 7, rest, 1.0)))
            return out

        nothing = jnp.zeros((16, slots), jnp.bfloat16)
        zero8 = jnp.zeros((8, slots), jnp.float32)

        def pair(p, carry):
            x, y, zp, own = s.place(p)
            centre = ((x + 1) * s.py + y + 1) * s.pz + 2 * zp + 1
            rows = [[target_rows(centre + k, d) for d in range(3)] for k in range(2)]
            low = [
                [[jnp.concatenate([rows[k][0][i], rows[k][1][j]], 0).astype(jnp.bfloat16) for j in range(3)]
                 for i in range(3)]
                for k in range(2)
            ]
            high = [
                [jnp.concatenate([rows[k][2][i], zero8], 0).astype(jnp.bfloat16) for i in range(3)]
                for k in range(2)
            ]
            total = jnp.zeros((16, 2 * slots), jnp.float32)
            for i in range(3):
                for j in range(3):
                    column = (x + i) * s.py + y + j
                    source = left[column * s.half + zp]
                    for e in range(3):
                        lanes = []
                        for k in range(2):
                            parts = [nothing] * 8
                            parts[2 * (e + k)] = low[k][i][j]
                            parts[2 * (e + k) + 1] = high[k][e]
                            lanes.append(jnp.concatenate(parts, axis=0))
                        right = jnp.concatenate(lanes, axis=1)
                        dist = jnp.dot(source, right, preferred_element_type=jnp.float32)
                        dist = jnp.maximum(dist, 1e-20)
                        gap = jnp.maximum(1.0 - dist * lax.rsqrt(dist), 0.0)
                        kernel = (gap * gap * gap).astype(jnp.bfloat16)
                        place = (i * 3 + j) * 3 + e
                        kernel_out[p, place * slots : (place + 1) * slots, :] = kernel
                        gain = gain_pair(gains, column * s.pz + 2 * zp + e)
                        total = total + jnp.dot(gain, kernel, preferred_element_type=jnp.float32)
            keep_sums(s, total, own, sums)
            return carry

        lax.fori_loop(0, s.pairs, pair, 0)

        def finish(cell, top):
            one = sums[cell]
            centre = own_cell(s, cell)
            flow, weight = flow_from(
                s, lambda r: one[r : r + 1, :], conduct_out[pl.ds(centre, 1), :], own_temp[pl.ds(cell, 1), :]
            )
            flow_out[pl.ds(cell, 1), :] = flow
            return jnp.maximum(top, jnp.where(own_volume[pl.ds(cell, 1), :] > 0.0, weight, 0.0))

        top = lax.fori_loop(0, s.cells, finish, jnp.zeros((1, slots), jnp.float32))
        top_out[...] = top
        faces.pack_x(flow_out, top, up, down)

    return pl.pallas_call(
        body,
        out_shape=(
            jax.ShapeDtypeStruct((s.pairs, 27 * slots, 2 * slots), jnp.bfloat16),
            jax.ShapeDtypeStruct((s.cells, slots), jnp.float32),
            jax.ShapeDtypeStruct((s.padded, slots), jnp.float32),
            jax.ShapeDtypeStruct((1, slots), jnp.float32),
            *faces.x_messages(),
        ),
        scratch_shapes=[
            pltpu.VMEM((s.columns * s.half, slots, 128), jnp.bfloat16),
            pltpu.VMEM((s.padded, 8, slots), jnp.float32),
            pltpu.VMEM((s.cells, 8, slots), jnp.float32),
        ],
        compiler_params=pltpu.CompilerParams(vmem_limit_bytes=ROOM),
        name="kernel_and_first_flow",
    )


def own_cell(s, cell):
    z = cell % s.nz
    column = cell // s.nz
    return ((column // s.ny + 1) * s.py + column % s.ny + 1) * s.pz + z + 1


def next_kernel(s, last):
    slots = s.slots
    faces = Faces(s)
    arrivals = len(faces.z_messages())

    def body(kernel, volume, conduct, own_temp, flow1, own, top, x0, x1, y0, y1, *rest):
        z, rest = rest[:arrivals], rest[arrivals:]
        if last:
            final_out, flow_out, temp, gains, sums = rest
        else:
            flow_out, top_out, up, down, temp, gains, sums = rest
        faces.lay_out(temp, own, x0, x1, y0, y1, z)
        most = faces.latest_top(top, z)
        weights_of(s, volume, conduct, temp, gains)

        def pair(p, carry):
            x, y, zp, cell = s.place(p)
            parts = []
            for i in range(3):
                for j in range(3):
                    for e in range(3):
                        source = ((x + i) * s.py + y + j) * s.pz + 2 * zp + e
                        parts.append(gain_pair(gains, source))
            gain = jnp.concatenate(parts, axis=1)
            total = jnp.dot(gain, kernel[p], preferred_element_type=jnp.float32)
            keep_sums(s, total, cell, sums)
            return carry

        lax.fori_loop(0, s.pairs, pair, 0)

        def finish(cell, carry):
            one = sums[cell]
            centre = own_cell(s, cell)
            flow, _ = flow_from(
                s, lambda r: one[r : r + 1, :], conduct[pl.ds(centre, 1), :], own[pl.ds(cell, 1), :]
            )
            flow_out[pl.ds(cell, 1), :] = flow
            return carry

        lax.fori_loop(0, s.cells, finish, 0)
        if last:
            if covered():
                step = step_factor / jnp.max(most, axis=1, keepdims=True)
                final_out[...] = polynomial(own_temp[...], step, flow1[...], own[...], flow_out[...])
        else:
            top_out[...] = most
            faces.pack_x(flow_out, most, up, down)

    flow_shape = jax.ShapeDtypeStruct((s.cells, slots), jnp.float32)
    if last:
        outs = (flow_shape, flow_shape)
    else:
        outs = (flow_shape, jax.ShapeDtypeStruct((1, slots), jnp.float32), *faces.x_messages())
    return pl.pallas_call(
        body,
        in_specs=[pl.BlockSpec(memory_space=pltpu.VMEM)] * (11 + arrivals),
        out_shape=outs,
        scratch_shapes=[
            pltpu.VMEM((s.padded, slots), jnp.float32),
            pltpu.VMEM((s.padded, 8, slots), jnp.float32),
            pltpu.VMEM((s.cells, 8, slots), jnp.float32),
        ],
        compiler_params=pltpu.CompilerParams(vmem_limit_bytes=ROOM + s.only_first()),
        name="last_flow" if last else "next_flow",
    )


def covered():
    return all(lax.axis_size(axis) <= 5 for axis in AXES)


def polynomial(start, step, flow1, flow2, flow3):
    return start + step * (flow1 + step * (0.5 * flow2 + step * (1.0 / 15.0) * flow3))


def local(relative_placements, mass_per_density, opening_heat_level, bin_fill_counts):
    nx, ny, nz, slots = opening_heat_level.shape
    s = Sizes(nx, ny, nz, slots)
    faces = Faces(s)
    occupied = jnp.arange(slots, dtype=jnp.int32) < bin_fill_counts[..., None]
    volume = jnp.where(occupied, mass_per_density, 0.0)
    fields = jnp.concatenate([relative_placements, volume[None], opening_heat_level[None]], axis=0)
    near = with_halo(fields, 1).reshape(5, s.padded, slots)
    own_volume = volume.reshape(s.cells, slots)
    own_temp = opening_heat_level.reshape(s.cells, slots)
    kernel, flow1, conduct, top, up, down = first_kernel(s)(near[:3], near[3], near[4], own_volume, own_temp)
    arrived = faces.exchange(flow1, top, up, down)
    flow2, top, up, down = next_kernel(s, False)(kernel, near[3], conduct, own_temp, flow1, *arrived)
    arrived = faces.exchange(flow2, top, up, down)
    final, flow3 = next_kernel(s, True)(kernel, near[3], conduct, own_temp, flow1, *arrived)
    if not covered():
        top, flow3 = lax.optimization_barrier((top, flow3))
        step = step_factor / lax.pmax(jnp.max(top), AXES)
        final = polynomial(own_temp, step, flow1, flow2, flow3)
    return final.reshape(nx, ny, nz, slots)


def solution(mesh):
    in_specs = (
        P(None, "gx", "gy", "gz", None),
        P("gx", "gy", "gz", None),
        P("gx", "gy", "gz", None),
        P("gx", "gy", "gz"),
    )
    out_specs = P("gx", "gy", "gz", None)
    return jax.shard_map(local, mesh=mesh, in_specs=in_specs, out_specs=out_specs, check_vma=False)
```

time: 388 us -> 105 us (0.27)
  other arithmetic: 190 us -> 5.21 us
  Pallas kernels: 0 us -> 56.2 us
  waiting for transfers between devices: 72 us -> 18.8 us
  blocking collectives: 38.4 us -> 0 us
  local copies, waits for them, and re-layouts: 36.3 us -> 1.54 us
  starting transfers between devices: 39.9 us -> 22.6 us
  loops' own time: 9.42 us -> 0 us
    reduce_sum x189 -> x0, other arithmetic: 178 us -> none  [visit(): jnp.sum(toward_target * spread, axis=2)]
    pallas_call x0 -> x7, Pallas kernels: none -> 56.2 us  [the longest x1 40.3 us: local(): first_kernel(s)(near[:3], near[3], near[4], own_volume, own_temp)]
    ppermute x36 -> x15, waiting for transfers between devices: 72 us -> 18.8 us  [the longest x2 4.98 us: exchange(): z = (lax.ppermute(messages[0], 'gz', route('gz', 1)),)]
    pmax x1 -> x0, blocking collectives: 38.4 us -> none  [step_size(): largest = lax.pmax(jnp.max(row_sums), ('gx', 'gy', 'gz'))]
    dynamic_update_slice x270 -> x0, local copies, waits for them, and re-layouts: 33.7 us -> none  [the longest x243 30.3 us: visit(): lax.dynamic_update_slice(totals, window + returned.reshape((2, 1, 1, exte...]
    ppermute x36 -> x15, starting transfers between devices: 39.9 us -> 22.6 us  [the longest x4 6.91 us: swap_faces(): return (lax.ppermute(last, axis, up), lax.ppermute(leading, axis, down))]
    another operation x3 -> x0, loops' own time: 9.42 us -> none  [paired(): return lax.fori_loop(0, extent_x * extent_y, visit, totals)]
    add x302 -> x0, other arithmetic: 5.24 us -> none  [the longest x243 3.58 us: visit(): window + returned.reshape((2, 1, 1, extent_z, bin_dimensions))]
  transfers between devices with their start and end apart: 36 -> 15, of which waited for: 33 -> 11; matrix products, arithmetic and copies ran while one was open for 0% -> 1% of each run, Pallas kernels for 0% -> 0%
where the time goes in v1:
time: 105 us
  Pallas kernels  56.2 us (54%)
  starting transfers between devices  22.6 us (22%)
  waiting for transfers between devices  18.8 us (18%)
  other arithmetic  5.21 us (5%)
  local copies, waits for them, and re-layouts  1.54 us (1%)
    pallas_call x1, Pallas kernels, local(): first_kernel(s)(near[:3], near[3], near[4], own_volume, own_temp)  40.3 us
    pallas_call x1, Pallas kernels, local(): next_kernel(s, True)(kernel, near[3], conduct, own_temp, flow1, *arrived)  8.24 us
    pallas_call x1, Pallas kernels, local(): next_kernel(s, False)(kernel, near[3], conduct, own_temp, flow1, *arrived)  7.64 us
    ppermute x4, starting transfers between devices, swap_faces(): return (lax.ppermute(last, axis, up), lax.ppermute(leading, axis, down))  6.91 us
    ppermute x2, starting transfers between devices, exchange(): y1 = lax.ppermute(down, 'gy', route('gy', -1))  6.56 us
    ppermute x2, waiting for transfers between devices, exchange(): z = (lax.ppermute(messages[0], 'gz', route('gz', 1)),)  4.98 us
    ppermute x4, waiting for transfers between devices, swap_faces(): return (lax.ppermute(last, axis, up), lax.ppermute(leading, axis, down))  4.48 us
    ppermute x2, starting transfers between devices, exchange(): x1 = lax.ppermute(down, 'gx', route('gx', -1))  3.47 us
  transfers between devices with their start and end apart: 15, of which 11 were waited for; matrix products, arithmetic and copies ran while one was open for 1% of the time, Pallas kernels for 0%

profile of v1, /device:TPU:0, one launch (start us, length us, event | category | flops | bytes accessed | tf_op | source)
XLA Modules:
  0.0 104.5 jit_solution(9582426322574580175)
XLA Ops:
  2.1 2.0 %collective-permute-start.1 = (f32[5,1,3,4,128]{4,3,2,1,0:T(4,128)S(1)}, f32[5,1,3,4,128]{4,3,2,1,0:T(4,128)S(1)}, u32[]{:S(2)}, u32[]{:S(2)}) collective-permute-start(f32[5,1,3,4,128]{4,3,2,1,0:T(4,128)S(1)} %get-tuple-element.54), channel_id=1, source_target_pairs={{8,0},{16,8},{24,16},{0,24},{9,1},{17,9},{25,17},{1,25},{10,2},{18... | collective-permute-start | bytes 92168 | tf_op jit(solution)/shard_map/ppermute | solution.py:24
  4.1 1.5 %collective-permute-done = f32[5,1,3,4,128]{4,3,2,1,0:T(4,128)S(1)} collective-permute-done((f32[5,1,3,4,128]{4,3,2,1,0:T(4,128)S(1)}, f32[5,1,3,4,128]{4,3,2,1,0:T(4,128)S(1)}, u32[]{:S(2)}, u32[]{:S(2)}) %collective-permute-start) | collective-permute-done | bytes 30752 | tf_op jit(solution)/shard_map/ppermute | solution.py:24
  6.6 2.3 %collective-permute-start.2 = (f32[5,5,1,4,128]{4,3,2,1,0:T(4,128)S(1)}, f32[5,5,1,4,128]{4,3,2,1,0:T(4,128)S(1)}, u32[]{:S(2)}, u32[]{:S(2)}) collective-permute-start(f32[5,5,1,4,128]{4,3,2,1,0:T(4,128)S(1)} %get-tuple-element.49), channel_id=1, source_target_pairs={{0,2},{2,4},{4,6},{6,0},{1,3},{3,5},{5,7},{7,1},{8,10},{10,12},{12... | collective-permute-start | bytes 153608 | tf_op jit(solution)/shard_map/ppermute | solution.py:24
  8.9 2.1 %collective-permute-start.3 = (f32[5,5,1,4,128]{4,3,2,1,0:T(4,128)S(1)}, f32[5,5,1,4,128]{4,3,2,1,0:T(4,128)S(1)}, u32[]{:S(2)}, u32[]{:S(2)}) collective-permute-start(f32[5,5,1,4,128]{4,3,2,1,0:T(4,128)S(1)} %get-tuple-element.50), channel_id=1, source_target_pairs={{2,0},{4,2},{6,4},{0,6},{3,1},{5,3},{7,5},{1,7},{10,8},{12,10},{14... | collective-permute-start | bytes 153608 | tf_op jit(solution)/shard_map/ppermute | solution.py:24
  11.7 1.4 %collective-permute-done.2 = f32[5,5,1,4,128]{4,3,2,1,0:T(4,128)S(1)} collective-permute-done((f32[5,5,1,4,128]{4,3,2,1,0:T(4,128)S(1)}, f32[5,5,1,4,128]{4,3,2,1,0:T(4,128)S(1)}, u32[]{:S(2)}, u32[]{:S(2)}) %collective-permute-start.2) | collective-permute-done | bytes 51232 | tf_op jit(solution)/shard_map/ppermute | solution.py:24
  13.1 1.4 %collective-permute-done.3 = f32[5,5,1,4,128]{4,3,2,1,0:T(4,128)S(1)} collective-permute-done((f32[5,5,1,4,128]{4,3,2,1,0:T(4,128)S(1)}, f32[5,5,1,4,128]{4,3,2,1,0:T(4,128)S(1)}, u32[]{:S(2)}, u32[]{:S(2)}) %collective-permute-start.3) | collective-permute-done | bytes 51232 | tf_op jit(solution)/shard_map/ppermute | solution.py:24
  15.6 1.4 %collective-permute-start.4 = (f32[5,5,5,2,128]{4,3,2,1,0:T(2,128)S(1)}, f32[5,5,5,2,128]{4,3,2,1,0:T(2,128)S(1)}, u32[]{:S(2)}, u32[]{:S(2)}) collective-permute-start(f32[5,5,5,2,128]{4,3,2,1,0:T(2,128)S(1)} %fusion), channel_id=1, source_target_pairs={{0,1},{1,0},{2,3},{3,2},{4,5},{5,4},{6,7},{7,6},{8,9},{9,8},{10,11... | collective-permute-start | bytes 384008 | tf_op jit(solution)/shard_map/ppermute | solution.py:21
  17.7 3.3 %collective-permute-done.4 = f32[5,5,5,2,128]{4,3,2,1,0:T(2,128)S(1)} collective-permute-done((f32[5,5,5,2,128]{4,3,2,1,0:T(2,128)S(1)}, f32[5,5,5,2,128]{4,3,2,1,0:T(2,128)S(1)}, u32[]{:S(2)}, u32[]{:S(2)}) %collective-permute-start.4) | collective-permute-done | bytes 128032 | tf_op jit(solution)/shard_map/ppermute | solution.py:21
  22.3 40.3 %kernel_and_first_flow.1 = (bf16[18,3456,256]{2,1,0:T(8,128)(2,1)S(1)}, f32[36,128]{1,0:T(8,128)S(1)}, f32[150,128]{1,0:T(8,128)S(1)}, f32[1,128]{1,0:T(1,128)S(...) custom-call(f32[3,150,128]{2,1,0:T(8,128)S(1)} %slice.49.position, f32[150,128]{1,0:T(8,128)S(1)} %squeeze.8.volume, ...), custom_call_target="tpu_custom_call" | custom-call | tf_op jit(solution)/shard_map/kernel_and_first_flow/pallas_call | solution.py:479
  62.7 1.7 %collective-permute-start.6 = (f32[16,128]{1,0:T(8,128)S(1)}, f32[16,128]{1,0:T(8,128)S(1)}, u32[]{:S(2)}, u32[]{:S(2)}) collective-permute-start(f32[16,128]{1,0:T(8,128)S(1)} %get-tuple-element.31), channel_id=1, source_target_pairs={{0,24},{8,0},{16,8},{24,16},{1,25},{9,1},{17,9},{25,17},{2,26},{10... | collective-permute-start | bytes 24584 | tf_op jit(solution)/shard_map/ppermute | solution.py:203
  64.4 1.3 %collective-permute-done.5.before.x0 = f32[16,128]{1,0:T(8,128)S(1)} collective-permute-done((f32[16,128]{1,0:T(8,128)S(1)}, f32[16,128]{1,0:T(8,128)S(1)}, u32[]{:S(2)}, u32[]{:S(2)}) %collective-permute-start.5) | collective-permute-done | bytes 8224 | tf_op jit(solution)/shard_map/ppermute | solution.py:202
  65.8 1.1 %collective-permute-start.7 = (f32[24,128]{1,0:T(8,128)S(1)}, f32[24,128]{1,0:T(8,128)S(1)}, u32[]{:S(2)}, u32[]{:S(2)}) collective-permute-start(f32[24,128]{1,0:T(8,128)S(1)} %get-tuple-element.33), channel_id=1, source_target_pairs={{0,2},{2,4},{4,6},{6,0},{1,3},{3,5},{5,7},{7,1},{8,10},{10,12},{12... | collective-permute-start | bytes 36872 | tf_op jit(solution)/shard_map/ppermute | solution.py:205
  66.8 2.8 %collective-permute-start.8 = (f32[24,128]{1,0:T(8,128)S(1)}, f32[24,128]{1,0:T(8,128)S(1)}, u32[]{:S(2)}, u32[]{:S(2)}) collective-permute-start(f32[24,128]{1,0:T(8,128)S(1)} %get-tuple-element.34), channel_id=1, source_target_pairs={{0,6},{2,0},{4,2},{6,4},{1,7},{3,1},{5,3},{7,5},{8,14},{10,8},{12,... | collective-permute-start | bytes 36872 | tf_op jit(solution)/shard_map/ppermute | solution.py:206
  69.6 1.7 %collective-permute-done.7.y0 = f32[24,128]{1,0:T(8,128)S(1)} collective-permute-done((f32[24,128]{1,0:T(8,128)S(1)}, f32[24,128]{1,0:T(8,128)S(1)}, u32[]{:S(2)}, u32[]{:S(2)}) %collective-permute-start.7) | collective-permute-done | bytes 12320 | tf_op jit(solution)/shard_map/ppermute | solution.py:205
  71.4 1.4 %collective-permute-start.9 = (f32[56,128]{1,0:T(8,128)S(1)}, f32[56,128]{1,0:T(8,128)S(1)}, u32[]{:S(2)}, u32[]{:S(2)}) collective-permute-start(f32[56,128]{1,0:T(8,128)S(1)} %get-tuple-element.36), channel_id=1, source_target_pairs={{0,1},{1,0},{2,3},{3,2},{4,5},{5,4},{6,7},{7,6},{8,9},{9,8},{10,11... | collective-permute-start | bytes 86024 | tf_op jit(solution)/shard_map/ppermute | solution.py:209
  72.8 2.5 %collective-permute-done.9.rest_0_ = f32[56,128]{1,0:T(8,128)S(1)} collective-permute-done((f32[56,128]{1,0:T(8,128)S(1)}, f32[56,128]{1,0:T(8,128)S(1)}, u32[]{:S(2)}, u32[]{:S(2)}) %collective-permute-start.9) | collective-permute-done | bytes 28704 | tf_op jit(solution)/shard_map/ppermute | solution.py:209
  75.3 7.6 %next_flow.1 = (f32[36,128]{1,0:T(8,128)S(1)}, f32[1,128]{1,0:T(1,128)S(1)}, f32[16,128]{1,0:T(8,128)S(1)}, f32[16,128]{1,0:T(8,128)S(1)}) custom-call(bf16[18,3456,256]{2,1,0:T(8,128)(2,1)S(1)} %get-tuple-element.26.kernel, f32[150,128]{1,0:T(8,128)S(1)} %squeeze.8.volume, f32[150,128]{1,0:T(8,128)S(1)} %get-tuple-element.27.conduct, ...), custom_call_target="tpu_custom_call" | custom-call | tf_op jit(solution)/shard_map/next_flow/pallas_call | solution.py:481
  83.0 1.7 %collective-permute-start.11 = (f32[16,128]{1,0:T(8,128)S(1)}, f32[16,128]{1,0:T(8,128)S(1)}, u32[]{:S(2)}, u32[]{:S(2)}) collective-permute-start(f32[16,128]{1,0:T(8,128)S(1)} %get-tuple-element.40), channel_id=1, source_target_pairs={{0,24},{8,0},{16,8},{24,16},{1,25},{9,1},{17,9},{25,17},{2,26},{10... | collective-permute-start | bytes 24584 | tf_op jit(solution)/shard_map/ppermute | solution.py:203
  84.7 1.3 %collective-permute-done.10.before.x0 = f32[16,128]{1,0:T(8,128)S(1)} collective-permute-done((f32[16,128]{1,0:T(8,128)S(1)}, f32[16,128]{1,0:T(8,128)S(1)}, u32[]{:S(2)}, u32[]{:S(2)}) %collective-permute-start.10) | collective-permute-done | bytes 8224 | tf_op jit(solution)/shard_map/ppermute | solution.py:202
  86.3 3.7 %collective-permute-start.13 = (f32[24,128]{1,0:T(8,128)S(1)}, f32[24,128]{1,0:T(8,128)S(1)}, u32[]{:S(2)}, u32[]{:S(2)}) collective-permute-start(f32[24,128]{1,0:T(8,128)S(1)} %get-tuple-element.43), channel_id=1, source_target_pairs={{0,6},{2,0},{4,2},{6,4},{1,7},{3,1},{5,3},{7,5},{8,14},{10,8},{12,... | collective-permute-start | bytes 36872 | tf_op jit(solution)/shard_map/ppermute | solution.py:206
  90.0 1.6 %collective-permute-done.12.y0 = f32[24,128]{1,0:T(8,128)S(1)} collective-permute-done((f32[24,128]{1,0:T(8,128)S(1)}, f32[24,128]{1,0:T(8,128)S(1)}, u32[]{:S(2)}, u32[]{:S(2)}) %collective-permute-start.12) | collective-permute-done | bytes 12320 | tf_op jit(solution)/shard_map/ppermute | solution.py:205
  91.7 1.5 %collective-permute-start.14 = (f32[56,128]{1,0:T(8,128)S(1)}, f32[56,128]{1,0:T(8,128)S(1)}, u32[]{:S(2)}, u32[]{:S(2)}) collective-permute-start(f32[56,128]{1,0:T(8,128)S(1)} %get-tuple-element.45), channel_id=1, source_target_pairs={{0,1},{1,0},{2,3},{3,2},{4,5},{5,4},{6,7},{7,6},{8,9},{9,8},{10,11... | collective-permute-start | bytes 86024 | tf_op jit(solution)/shard_map/ppermute | solution.py:209
  93.2 2.5 %collective-permute-done.14.rest_0_ = f32[56,128]{1,0:T(8,128)S(1)} collective-permute-done((f32[56,128]{1,0:T(8,128)S(1)}, f32[56,128]{1,0:T(8,128)S(1)}, u32[]{:S(2)}, u32[]{:S(2)}) %collective-permute-start.14) | collective-permute-done | bytes 28704 | tf_op jit(solution)/shard_map/ppermute | solution.py:209
  95.6 8.2 %last_flow.1 = (f32[36,128]{1,0:T(8,128)S(1)}, f32[36,128]{1,0:T(8,128)}) custom-call(bf16[18,3456,256]{2,1,0:T(8,128)(2,1)S(1)} %get-tuple-element.26.kernel, f32[150,128]{1,0:T(8,128)S(1)} %squeeze.8.volume, f32[150,128]{1,0:T(8,128)S(1)} %get-tuple-element.27.conduct, f32[36,128]{1,0:T(8,128)S(1)} %reshape.17.own_temp, ...), custom_call_target="tpu_custom_call" | custom-call | tf_op jit(solution)/shard_map/last_flow/pallas_call | solution.py:483
  (28 shorter events, 7.9 us)
Async XLA Ops:
  1.6 4.0 %collective-permute-start = (f32[5,1,3,4,128]{4,3,2,1,0:T(4,128)S(1)}, f32[5,1,3,4,128]{4,3,2,1,0:T(4,128)S(1)}, u32[]{:S(2)}, u32[]{:S(2)}) collective-permute-start(f32[5,1,3,4,128]{4,3,2,1,0:T(4,128)S(1)} %get-tuple-element.53), channel_id=1, source_target_pairs={{0,8},{8,16},{16,24},{24,0},{1,9},{9,17},{17,25},{25,1},{2,10},{10... | collective-permute-start | bytes 92168 | tf_op jit(solution)/shard_map/ppermute | solution.py:24
  2.1 3.6 %collective-permute-start.1 = (f32[5,1,3,4,128]{4,3,2,1,0:T(4,128)S(1)}, f32[5,1,3,4,128]{4,3,2,1,0:T(4,128)S(1)}, u32[]{:S(2)}, u32[]{:S(2)}) collective-permute-start(f32[5,1,3,4,128]{4,3,2,1,0:T(4,128)S(1)} %get-tuple-element.54), channel_id=1, source_target_pairs={{8,0},{16,8},{24,16},{0,24},{9,1},{17,9},{25,17},{1,25},{10,2},{18... | collective-permute-start | bytes 92168 | tf_op jit(solution)/shard_map/ppermute | solution.py:24
  6.6 6.5 %collective-permute-start.2 = (f32[5,5,1,4,128]{4,3,2,1,0:T(4,128)S(1)}, f32[5,5,1,4,128]{4,3,2,1,0:T(4,128)S(1)}, u32[]{:S(2)}, u32[]{:S(2)}) collective-permute-start(f32[5,5,1,4,128]{4,3,2,1,0:T(4,128)S(1)} %get-tuple-element.49), channel_id=1, source_target_pairs={{0,2},{2,4},{4,6},{6,0},{1,3},{3,5},{5,7},{7,1},{8,10},{10,12},{12... | collective-permute-start | bytes 153608 | tf_op jit(solution)/shard_map/ppermute | solution.py:24
  8.9 5.6 %collective-permute-start.3 = (f32[5,5,1,4,128]{4,3,2,1,0:T(4,128)S(1)}, f32[5,5,1,4,128]{4,3,2,1,0:T(4,128)S(1)}, u32[]{:S(2)}, u32[]{:S(2)}) collective-permute-start(f32[5,5,1,4,128]{4,3,2,1,0:T(4,128)S(1)} %get-tuple-element.50), channel_id=1, source_target_pairs={{2,0},{4,2},{6,4},{0,6},{3,1},{5,3},{7,5},{1,7},{10,8},{12,10},{14... | collective-permute-start | bytes 153608 | tf_op jit(solution)/shard_map/ppermute | solution.py:24
  15.6 5.5 %collective-permute-start.4 = (f32[5,5,5,2,128]{4,3,2,1,0:T(2,128)S(1)}, f32[5,5,5,2,128]{4,3,2,1,0:T(2,128)S(1)}, u32[]{:S(2)}, u32[]{:S(2)}) collective-permute-start(f32[5,5,5,2,128]{4,3,2,1,0:T(2,128)S(1)} %fusion), channel_id=1, source_target_pairs={{0,1},{1,0},{2,3},{3,2},{4,5},{5,4},{6,7},{7,6},{8,9},{9,8},{10,11... | collective-permute-start | bytes 384008 | tf_op jit(solution)/shard_map/ppermute | solution.py:21
  62.6 3.1 %collective-permute-start.5 = (f32[16,128]{1,0:T(8,128)S(1)}, f32[16,128]{1,0:T(8,128)S(1)}, u32[]{:S(2)}, u32[]{:S(2)}) collective-permute-start(f32[16,128]{1,0:T(8,128)S(1)} %get-tuple-element.30), channel_id=1, source_target_pairs={{0,8},{8,16},{16,24},{24,0},{1,9},{9,17},{17,25},{25,1},{2,10},{10... | collective-permute-start | bytes 24584 | tf_op jit(solution)/shard_map/ppermute | solution.py:202
  62.7 3.1 %collective-permute-start.6 = (f32[16,128]{1,0:T(8,128)S(1)}, f32[16,128]{1,0:T(8,128)S(1)}, u32[]{:S(2)}, u32[]{:S(2)}) collective-permute-start(f32[16,128]{1,0:T(8,128)S(1)} %get-tuple-element.31), channel_id=1, source_target_pairs={{0,24},{8,0},{16,8},{24,16},{1,25},{9,1},{17,9},{25,17},{2,26},{10... | collective-permute-start | bytes 24584 | tf_op jit(solution)/shard_map/ppermute | solution.py:203
  65.8 5.5 %collective-permute-start.7 = (f32[24,128]{1,0:T(8,128)S(1)}, f32[24,128]{1,0:T(8,128)S(1)}, u32[]{:S(2)}, u32[]{:S(2)}) collective-permute-start(f32[24,128]{1,0:T(8,128)S(1)} %get-tuple-element.33), channel_id=1, source_target_pairs={{0,2},{2,4},{4,6},{6,0},{1,3},{3,5},{5,7},{7,1},{8,10},{10,12},{12... | collective-permute-start | bytes 36872 | tf_op jit(solution)/shard_map/ppermute | solution.py:205
  66.8 4.5 %collective-permute-start.8 = (f32[24,128]{1,0:T(8,128)S(1)}, f32[24,128]{1,0:T(8,128)S(1)}, u32[]{:S(2)}, u32[]{:S(2)}) collective-permute-start(f32[24,128]{1,0:T(8,128)S(1)} %get-tuple-element.34), channel_id=1, source_target_pairs={{0,6},{2,0},{4,2},{6,4},{1,7},{3,1},{5,3},{7,5},{8,14},{10,8},{12,... | collective-permute-start | bytes 36872 | tf_op jit(solution)/shard_map/ppermute | solution.py:206
  71.4 3.9 %collective-permute-start.9 = (f32[56,128]{1,0:T(8,128)S(1)}, f32[56,128]{1,0:T(8,128)S(1)}, u32[]{:S(2)}, u32[]{:S(2)}) collective-permute-start(f32[56,128]{1,0:T(8,128)S(1)} %get-tuple-element.36), channel_id=1, source_target_pairs={{0,1},{1,0},{2,3},{3,2},{4,5},{5,4},{6,7},{7,6},{8,9},{9,8},{10,11... | collective-permute-start | bytes 86024 | tf_op jit(solution)/shard_map/ppermute | solution.py:209
  82.9 3.1 %collective-permute-start.10 = (f32[16,128]{1,0:T(8,128)S(1)}, f32[16,128]{1,0:T(8,128)S(1)}, u32[]{:S(2)}, u32[]{:S(2)}) collective-permute-start(f32[16,128]{1,0:T(8,128)S(1)} %get-tuple-element.39), channel_id=1, source_target_pairs={{0,8},{8,16},{16,24},{24,0},{1,9},{9,17},{17,25},{25,1},{2,10},{10... | collective-permute-start | bytes 24584 | tf_op jit(solution)/shard_map/ppermute | solution.py:202
  83.0 3.1 %collective-permute-start.11 = (f32[16,128]{1,0:T(8,128)S(1)}, f32[16,128]{1,0:T(8,128)S(1)}, u32[]{:S(2)}, u32[]{:S(2)}) collective-permute-start(f32[16,128]{1,0:T(8,128)S(1)} %get-tuple-element.40), channel_id=1, source_target_pairs={{0,24},{8,0},{16,8},{24,16},{1,25},{9,1},{17,9},{25,17},{2,26},{10... | collective-permute-start | bytes 24584 | tf_op jit(solution)/shard_map/ppermute | solution.py:203
  86.1 5.6 %collective-permute-start.12 = (f32[24,128]{1,0:T(8,128)S(1)}, f32[24,128]{1,0:T(8,128)S(1)}, u32[]{:S(2)}, u32[]{:S(2)}) collective-permute-start(f32[24,128]{1,0:T(8,128)S(1)} %get-tuple-element.42), channel_id=1, source_target_pairs={{0,2},{2,4},{4,6},{6,0},{1,3},{3,5},{5,7},{7,1},{8,10},{10,12},{12... | collective-permute-start | bytes 36872 | tf_op jit(solution)/shard_map/ppermute | solution.py:205
  86.3 5.4 %collective-permute-start.13 = (f32[24,128]{1,0:T(8,128)S(1)}, f32[24,128]{1,0:T(8,128)S(1)}, u32[]{:S(2)}, u32[]{:S(2)}) collective-permute-start(f32[24,128]{1,0:T(8,128)S(1)} %get-tuple-element.43), channel_id=1, source_target_pairs={{0,6},{2,0},{4,2},{6,4},{1,7},{3,1},{5,3},{7,5},{8,14},{10,8},{12,... | collective-permute-start | bytes 36872 | tf_op jit(solution)/shard_map/ppermute | solution.py:206
  91.7 3.9 %collective-permute-start.14 = (f32[56,128]{1,0:T(8,128)S(1)}, f32[56,128]{1,0:T(8,128)S(1)}, u32[]{:S(2)}, u32[]{:S(2)}) collective-permute-start(f32[56,128]{1,0:T(8,128)S(1)} %get-tuple-element.45), channel_id=1, source_target_pairs={{0,1},{1,0},{2,3},{3,2},{4,5},{5,4},{6,7},{7,6},{8,9},{9,8},{10,11... | collective-permute-start | bytes 86024 | tf_op jit(solution)/shard_map/ppermute | solution.py:209

commit v2 on v0

v2 whole, which is shorter than its diff:
```python
import jax
import jax.numpy as jnp
from jax import lax
from jax.experimental import pallas as pl
from jax.experimental.pallas import tpu as pltpu
from jax.sharding import PartitionSpec as P

step_factor = 2.0
AXES = ("gx", "gy", "gz")
ROUNDER = 192.0
SHIFTS = (-1, 0, 1)
FIELDS = 5
ROOM = 8 << 20
SMALL = pltpu.CompilerParams(vmem_limit_bytes=2 << 20)


def route(axis, distance):
    size = lax.axis_size(axis)
    return [(i, (i + distance) % size) for i in range(size)]


def rounded_up(rows):
    return -(-rows // 8) * 8


def f32(*shape):
    return jax.ShapeDtypeStruct(shape, jnp.float32)


class Sizes:
    def __init__(self, nx, ny, nz, slots):
        self.nx, self.ny, self.nz, self.slots = nx, ny, nz, slots
        self.px, self.py, self.pz = nx + 2, ny + 2, nz + 2
        self.cells = nx * ny * nz
        self.padded = self.px * self.py * self.pz
        self.half = nz // 2
        self.pairs = nx * ny * self.half
        self.columns = self.px * self.py

    def place(self, p):
        zp = p % self.half
        column = p // self.half
        return column // self.ny, column % self.ny, zp, column * self.nz + 2 * zp


class Faces:
    def __init__(self, s, fields):
        self.s, self.fields = s, fields
        self.x_rows = s.ny * s.nz
        self.y_rows = s.px * s.nz
        self.joined = lax.axis_size("gz") == 2
        self.z_rows = s.px * s.py
        self.z_faces = 2 if self.joined else 1
        self.halo_shape = pltpu.VMEM((fields * s.padded, s.slots), jnp.float32)

    def message(self, rows):
        return f32(rounded_up(self.fields * rows + 1), self.s.slots)

    def x_messages(self):
        return (self.message(self.x_rows),) * 2

    def y_messages(self):
        return (self.message(self.y_rows),) * 2

    def z_messages(self):
        return (self.message(self.z_faces * self.z_rows),) * (2 // self.z_faces)

    def row(self, f, x, y, z):
        return f * self.s.padded + (x * self.s.py + y) * self.s.pz + z

    def put_own(self, halo, own):
        s = self.s
        for f in range(self.fields):
            for x in range(s.nx):
                for y in range(s.ny):
                    at, start = self.row(f, x + 1, y + 1, 1), f * s.cells + (x * s.ny + y) * s.nz
                    halo[at : at + s.nz, :] = own[start : start + s.nz, :]

    def put_x(self, halo, before, after):
        s = self.s
        for f in range(self.fields):
            for side, x in ((before, 0), (after, s.nx + 1)):
                for y in range(s.ny):
                    at, start = self.row(f, x, y + 1, 1), f * self.x_rows + y * s.nz
                    halo[at : at + s.nz, :] = side[start : start + s.nz, :]

    def put_y(self, halo, before, after):
        s = self.s
        for f in range(self.fields):
            for side, y in ((before, 0), (after, s.ny + 1)):
                for x in range(s.px):
                    at, start = self.row(f, x, y, 1), f * self.y_rows + x * s.nz
                    halo[at : at + s.nz, :] = side[start : start + s.nz, :]

    def z_places(self, below, above):
        for f in range(self.fields):
            for k, z in ((0, below), (1, above)):
                m, base = (0, k * self.z_rows) if self.joined else (k, 0)
                for column in range(self.z_rows):
                    yield m, f * self.z_faces * self.z_rows + base + column, f, column, z

    def put_z(self, halo, sides):
        for m, start, f, column, z in self.z_places(0, self.s.nz + 1):
            at = f * self.s.padded + column * self.s.pz + z
            halo[at : at + 1, :] = sides[m][start : start + 1, :]

    def end(self, message, rows, top):
        n = self.fields * rows
        message[n : n + 1, :] = top

    def pack_x(self, own, top, up, down):
        s = self.s
        n = self.x_rows
        for f in range(self.fields):
            up[f * n : f * n + n, :] = own[f * s.cells + (s.nx - 1) * n : f * s.cells + s.nx * n, :]
            down[f * n : f * n + n, :] = own[f * s.cells : f * s.cells + n, :]
        for m in (up, down):
            self.end(m, n, top)

    def pack_y(self, halo, top, up, down):
        s = self.s
        for f in range(self.fields):
            for x in range(s.px):
                for m, y in ((up, s.ny), (down, 1)):
                    at, start = self.row(f, x, y, 1), f * self.y_rows + x * s.nz
                    m[start : start + s.nz, :] = halo[at : at + s.nz, :]
        for m in (up, down):
            self.end(m, self.y_rows, top)

    def pack_z(self, halo, top, messages):
        for m, start, f, column, z in self.z_places(self.s.nz, 1):
            at = f * self.s.padded + column * self.s.pz + z
            messages[m][start : start + 1, :] = halo[at : at + 1, :]
        for m in messages:
            self.end(m, self.z_faces * self.z_rows, top)

    def largest(self, top, rows, refs):
        n = self.fields * rows
        return jnp.maximum(top[...], jnp.maximum(refs[0][n : n + 1, :], refs[-1][n : n + 1, :]))

    def y_packer(self):
        def body(own, top, before, after, up, down, top_out, halo):
            self.put_own(halo, own)
            self.put_x(halo, before, after)
            most = self.largest(top, self.x_rows, (before, after))
            top_out[...] = most
            self.pack_y(halo, most, up, down)

        return pl.pallas_call(
            body,
            out_shape=(*self.y_messages(), f32(1, self.s.slots)),
            scratch_shapes=[self.halo_shape],
            compiler_params=SMALL,
            name="pack_y",
        )

    def z_packer(self):
        count = len(self.z_messages())

        def body(own, top, x0, x1, y0, y1, *rest):
            messages, top_out, halo = rest[:count], rest[count], rest[-1]
            self.put_own(halo, own)
            self.put_x(halo, x0, x1)
            self.put_y(halo, y0, y1)
            most = self.largest(top, self.y_rows, (y0, y1))
            top_out[...] = most
            self.pack_z(halo, most, messages)

        return pl.pallas_call(
            body,
            out_shape=(*self.z_messages(), f32(1, self.s.slots)),
            scratch_shapes=[self.halo_shape],
            compiler_params=SMALL,
            name="pack_z",
        )

    def exchange(self, own, top, up, down):
        x0 = lax.ppermute(up, "gx", route("gx", 1))
        x1 = lax.ppermute(down, "gx", route("gx", -1))
        up, down, top = self.y_packer()(own, top, x0, x1)
        y0 = lax.ppermute(up, "gy", route("gy", 1))
        y1 = lax.ppermute(down, "gy", route("gy", -1))
        *messages, top = self.z_packer()(own, top, x0, x1, y0, y1)
        z = [lax.ppermute(m, "gz", route("gz", d)) for m, d in zip(messages, (1, -1))]
        return (own, top, x0, x1, y0, y1, *z)

    def lay_out(self, halo, own, x0, x1, y0, y1, z):
        self.put_own(halo, own)
        self.put_x(halo, x0, x1)
        self.put_y(halo, y0, y1)
        self.put_z(halo, z)

    def latest_top(self, top, z):
        return self.largest(top, self.z_faces * self.z_rows, z)


def rounded(x):
    return x.astype(jnp.bfloat16).astype(jnp.float32)


def split3(x):
    a = rounded(x)
    b = rounded(x - a)
    return a, b, x - a - b


def start_kernel(s):
    faces = Faces(s, FIELDS)

    def body(counts_in, placements_in, mass_in, temp_in, own, top_out, up, down,
             counts, placements, mass, temp, arrived):
        copies = [
            pltpu.make_async_copy(a, b, arrived.at[k])
            for k, (a, b) in enumerate(
                ((counts_in, counts), (placements_in, placements), (mass_in, mass), (temp_in, temp))
            )
        ]
        for copy in copies:
            copy.start()
        for copy in copies:
            copy.wait()
        slot = lax.broadcasted_iota(jnp.int32, (1, s.slots), 1)
        for x in range(s.nx):
            for y in range(s.ny):
                start = (x * s.ny + y) * s.nz
                for d in range(3):
                    own[d * s.cells + start : d * s.cells + start + s.nz, :] = placements[d, x, y]
                rows = [
                    jnp.where(slot < counts[x, y, z], mass[x, y, z : z + 1, :], 0.0) for z in range(s.nz)
                ]
                own[3 * s.cells + start : 3 * s.cells + start + s.nz, :] = jnp.concatenate(rows, axis=0)
                own[4 * s.cells + start : 4 * s.cells + start + s.nz, :] = temp[x, y]
        none = jnp.zeros((1, s.slots), jnp.float32)
        top_out[...] = none
        faces.pack_x(own, none, up, down)

    block = (s.nx, s.ny, s.nz, s.slots)
    return pl.pallas_call(
        body,
        in_specs=[pl.BlockSpec(memory_space=pltpu.HBM)] * 4,
        out_shape=(f32(FIELDS * s.cells, s.slots), f32(1, s.slots), *faces.x_messages()),
        scratch_shapes=[
            pltpu.SMEM(block[:3], jnp.int32),
            pltpu.VMEM((3, *block), jnp.float32),
            pltpu.VMEM(block, jnp.float32),
            pltpu.VMEM(block, jnp.float32),
            pltpu.SemaphoreType.DMA((4,)),
        ],
        compiler_params=SMALL,
        name="start",
    )


def source_rows(s, volume, scaled, temp, gains):
    row = lax.broadcasted_iota(jnp.int32, (8, s.slots), 0)
    use_c = (row % 4) < 2
    use_u = row < 4
    odd = (row % 2) == 1

    def one(cell, carry):
        def rows(ref):
            return jnp.broadcast_to(ref[pl.ds(cell, 1), :], (8, s.slots))

        full = jnp.where(use_c, rows(scaled), rows(volume)) * jnp.where(use_u, rows(temp), 1.0)
        top = rounded(full)
        gains[cell] = jnp.where(odd, full - top, top)
        return carry

    lax.fori_loop(0, s.padded, one, 0, unroll=6)


def gain_pair(gains, cell):
    return jnp.concatenate([gains[cell], gains[cell + 1]], axis=0).astype(jnp.bfloat16)


def keep_sums(s, total, own, sums):
    sums[pl.ds(pl.multiple_of(own * 8, 8), 8), :] = total[0:8, 0 : s.slots]
    sums[pl.ds(pl.multiple_of(own * 8 + 8, 8), 8), :] = total[8:16, s.slots : 2 * s.slots]


def flow_of(s, sums, conduct_own, temp_own):
    def of(r):
        return sums[pl.ds(r, s.cells, stride=8), :]

    weight = of(4) + of(5) + conduct_own * (of(6) + of(7))
    flow = of(0) + of(1) + conduct_own * (of(2) + of(3)) - temp_own * weight
    return flow, weight


def gathered(s, gains, kernel, p, x, y, zp):
    parts = []
    for i in range(3):
        for j in range(3):
            for e in range(3):
                parts.append(gain_pair(gains, ((x + i) * s.py + y + j) * s.pz + 2 * zp + e))
    return jnp.dot(jnp.concatenate(parts, axis=1), kernel[p], preferred_element_type=jnp.float32)


def conductivity(temp):
    return temp * temp * jnp.sqrt(temp)


def first_kernel(s):
    slots = s.slots
    fields = Faces(s, FIELDS)
    faces = Faces(s, 1)
    arrivals = len(fields.z_messages())
    inputs = 4 * slots * sum(
        rounded_up(m.shape[0])
        for m in (f32(FIELDS * s.cells), *fields.x_messages(), *fields.y_messages(), *fields.z_messages())
    )

    def body(own, x0, x1, y0, y1, *rest):
        z, rest = rest[:arrivals], rest[arrivals:]
        (kernel_out, flow_out, volume_out, scaled_out, conduct_own, temp_own, top_out, up, down,
         halo, left, gains, sums, halves, targets) = rest
        fields.lay_out(halo, own, x0, x1, y0, y1, z)
        temp = halo.at[pl.ds(4 * s.padded, s.padded)]
        volume_out[...] = halo[3 * s.padded : 4 * s.padded, :]
        scaled_out[...] = volume_out[...] * conductivity(temp[...])
        temp_own[...] = own[4 * s.cells : 5 * s.cells, :]
        conduct_own[...] = conductivity(temp_own[...])
        source_rows(s, volume_out, scaled_out, temp, gains)
        row = lax.broadcasted_iota(jnp.int32, (8, slots), 0)

        even = row % 2 == 0
        square = 0.0
        for d in range(3):
            q = (halo[d * s.padded : (d + 1) * s.padded, :] - 0.5 + ROUNDER) - ROUNDER
            halves[2 * d] = rounded(q)
            halves[2 * d + 1] = q - rounded(q)
            square = square + q * q
            q = (own[d * s.cells : (d + 1) * s.cells, :] - 0.5 + ROUNDER) - ROUNDER
            for k, shift in enumerate(SHIFTS):
                t = q - float(shift)
                h = rounded(t)
                for r, part in enumerate((-2.0 * h, -2.0 * (t - h), *split3(t * t))):
                    targets[(d * 3 + k) * 5 + r] = part
        for d, part in enumerate(split3(square)):
            halves[6 + d] = part

        def spread(ref, k, cell):
            return jnp.broadcast_to(ref[k, pl.ds(cell, 1), :], (8, slots))

        def features(column, carry):
            blocks = []
            for z in range(s.pz):
                cell = column * s.pz + z
                for d in range(3):
                    block = jnp.where(even, spread(halves, 2 * d, cell), spread(halves, 2 * d + 1, cell))
                    rest = jnp.where(row < 7, 1.0, spread(halves, 6 + d, cell))
                    blocks.append(jnp.where(row < 4, block, rest))
                blocks.append(jnp.zeros((8, slots), jnp.float32))
            for zp in range(s.half):
                quad = jnp.concatenate(blocks[8 * zp : 8 * zp + 16], axis=0)
                left[column * s.half + zp] = quad.T.astype(jnp.bfloat16)
            return carry

        lax.fori_loop(0, s.columns, features, 0, unroll=5)

        def target_rows(cell, d):
            out = []
            for k in range(3):
                part = [spread(targets, (d * 3 + k) * 5 + r, cell) for r in range(5)]
                block = jnp.where(row == 5, part[3], jnp.where(row == 6, part[4], 1.0))
                block = jnp.where(row < 4, part[1], jnp.where(row == 4, part[2], block))
                out.append(jnp.where(row < 2, part[0], block))
            return out

        nothing = jnp.zeros((16, slots), jnp.bfloat16)
        zero8 = jnp.zeros((8, slots), jnp.float32)

        def pair(p, carry):
            x, y, zp, cell = s.place(p)
            rows = [[target_rows(cell + k, d) for d in range(3)] for k in range(2)]
            low = [
                [[jnp.concatenate([rows[k][0][i], rows[k][1][j]], 0).astype(jnp.bfloat16) for j in range(3)]
                 for i in range(3)]
                for k in range(2)
            ]
            high = [
                [jnp.concatenate([rows[k][2][i], zero8], 0).astype(jnp.bfloat16) for i in range(3)]
                for k in range(2)
            ]
            for i in range(3):
                for j in range(3):
                    source = left[((x + i) * s.py + y + j) * s.half + zp]
                    for e in range(3):
                        lanes = []
                        for k in range(2):
                            parts = [nothing] * 8
                            parts[2 * (e + k)] = low[k][i][j]
                            parts[2 * (e + k) + 1] = high[k][e]
                            lanes.append(jnp.concatenate(parts, axis=0))
                        right = jnp.concatenate(lanes, axis=1)
                        dist = jnp.dot(source, right, preferred_element_type=jnp.float32)
                        gap = 1.0 - dist * lax.rsqrt(jnp.maximum(dist, 2.5e-7))
                        kernel = jnp.maximum((gap * gap * gap).astype(jnp.bfloat16), jnp.bfloat16(0.0))
                        at = ((i * 3 + j) * 3 + e) * slots
                        kernel_out[p, at : at + slots, :] = kernel
            keep_sums(s, gathered(s, gains, kernel_out, p, x, y, zp), cell, sums)
            return carry

        lax.fori_loop(0, s.pairs, pair, 0, unroll=2)

        flow, weight = flow_of(s, sums, conduct_own[...], temp_own[...])
        flow_out[...] = flow
        occupied = own[3 * s.cells : 4 * s.cells, :] > 0.0
        top = jnp.max(jnp.where(occupied, weight, 0.0), axis=0, keepdims=True)
        top_out[...] = top
        faces.pack_x(flow_out, top, up, down)

    cells, padded = f32(s.cells, slots), f32(s.padded, slots)
    call = pl.pallas_call(
        body,
        out_shape=(
            jax.ShapeDtypeStruct((s.pairs, 27 * slots, 2 * slots), jnp.bfloat16),
            cells,
            padded,
            padded,
            cells,
            cells,
            f32(1, slots),
            *faces.x_messages(),
        ),
        scratch_shapes=[
            fields.halo_shape,
            pltpu.VMEM((s.columns * s.half, slots, 128), jnp.bfloat16),
            pltpu.VMEM((s.padded, 8, slots), jnp.float32),
            pltpu.VMEM((s.cells * 8, slots), jnp.float32),
            pltpu.VMEM((9, s.padded, slots), jnp.float32),
            pltpu.VMEM((45, s.cells, slots), jnp.float32),
        ],
        compiler_params=pltpu.CompilerParams(vmem_limit_bytes=ROOM),
        name="kernel_and_first_flow",
    )
    return call, inputs


def next_kernel(s, room, last):
    slots = s.slots
    faces = Faces(s, 1)
    arrivals = len(faces.z_messages())

    def body(kernel, volume, scaled, conduct_own, *rest):
        if last:
            temp_own, flow1, *rest = rest
        own, top, x0, x1, y0, y1, *rest = rest
        z, rest = rest[:arrivals], rest[arrivals:]
        if last:
            out, temp, gains, sums, *rest = rest
        else:
            flow_out, top_out, up, down, temp, gains, sums = rest
        faces.lay_out(temp, own, x0, x1, y0, y1, z)
        most = faces.latest_top(top, z)
        source_rows(s, volume, scaled, temp, gains)

        def pair(p, carry):
            x, y, zp, cell = s.place(p)
            keep_sums(s, gathered(s, gains, kernel, p, x, y, zp), cell, sums)
            return carry

        lax.fori_loop(0, s.pairs, pair, 0)
        flow, _ = flow_of(s, sums, conduct_own[...], own[...])
        if last and covered():
            rows, block, arrived = rest
            step = step_factor / jnp.max(most, axis=1, keepdims=True)
            rows[...] = polynomial(temp_own[...], step, flow1[...], own[...], flow)
            for x in range(s.nx):
                for y in range(s.ny):
                    start = (x * s.ny + y) * s.nz
                    block[x, y] = rows[start : start + s.nz, :]
            copy = pltpu.make_async_copy(block, out, arrived)
            copy.start()
            copy.wait()
        elif last:
            out[...] = flow
        else:
            flow_out[...] = flow
            top_out[...] = most
            faces.pack_x(flow_out, most, up, down)

    cells, shape = f32(s.cells, slots), (s.nx, s.ny, s.nz, slots)
    outs = (cells, f32(1, slots), *faces.x_messages())
    spaces = [pltpu.VMEM] * len(outs)
    scratch = [
        faces.halo_shape,
        pltpu.VMEM((s.padded, 8, slots), jnp.float32),
        pltpu.VMEM((s.cells * 8, slots), jnp.float32),
    ]
    if last and covered():
        outs, spaces = (f32(*shape),), [pl.ANY]
        scratch += [pltpu.VMEM((s.cells, slots), jnp.float32), pltpu.VMEM(shape, jnp.float32), pltpu.SemaphoreType.DMA]
    elif last:
        outs, spaces = (cells,), [pltpu.VMEM]
    return pl.pallas_call(
        body,
        out_shape=outs,
        out_specs=tuple(pl.BlockSpec(memory_space=space) for space in spaces),
        scratch_shapes=scratch,
        compiler_params=pltpu.CompilerParams(vmem_limit_bytes=room),
        name="last_flow" if last else "next_flow",
    )


def covered():
    return all(lax.axis_size(axis) <= 5 for axis in AXES)


def polynomial(start, step, flow1, flow2, flow3):
    return start + step * (flow1 + step * (0.5 * flow2 + step * (1.0 / 15.0) * flow3))


def local(relative_placements, mass_per_density, opening_heat_level, bin_fill_counts):
    nx, ny, nz, slots = opening_heat_level.shape
    s = Sizes(nx, ny, nz, slots)
    fields, faces = Faces(s, FIELDS), Faces(s, 1)
    arguments = (bin_fill_counts, relative_placements, mass_per_density, opening_heat_level)
    started = start_kernel(s)(*[pltpu.with_memory_space_constraint(a, pltpu.HBM) for a in arguments])
    own, _, *messages = fields.exchange(*started)
    first, inputs = first_kernel(s)
    kernel, flow1, volume, scaled, conduct_own, temp_own, top, up, down = first(own, *messages)
    arrived = faces.exchange(flow1, top, up, down)
    flow2, top, up, down = next_kernel(s, ROOM + inputs, False)(kernel, volume, scaled, conduct_own, *arrived)
    arrived = faces.exchange(flow2, top, up, down)
    (final,) = next_kernel(s, ROOM + inputs, True)(
        kernel, volume, scaled, conduct_own, temp_own, flow1, *arrived
    )
    if not covered():
        top, flow3 = lax.optimization_barrier((arrived[1], final))
        step = step_factor / lax.pmax(jnp.max(top), AXES)
        final = polynomial(temp_own, step, flow1, flow2, flow3).reshape(nx, ny, nz, slots)
    return final


def solution(mesh):
    in_specs = (
        P(None, "gx", "gy", "gz", None),
        P("gx", "gy", "gz", None),
        P("gx", "gy", "gz", None),
        P("gx", "gy", "gz"),
    )
    out_specs = P("gx", "gy", "gz", None)
    return jax.shard_map(local, mesh=mesh, in_specs=in_specs, out_specs=out_specs, check_vma=False)
```

time: 388 us -> 80.7 us (0.21)
  other arithmetic: 190 us -> 0 us
  waiting for transfers between devices: 72 us -> 20.5 us
  blocking collectives: 38.4 us -> 0 us
  Pallas kernels: 0 us -> 37.5 us
  local copies, waits for them, and re-layouts: 36.3 us -> 0 us
  starting transfers between devices: 39.9 us -> 22.5 us
  loops' own time: 9.42 us -> 0 us
    reduce_sum x189 -> x0, other arithmetic: 178 us -> none  [visit(): jnp.sum(toward_target * spread, axis=2)]
    ppermute x36 -> x15, waiting for transfers between devices: 72 us -> 20.5 us  [the longest x3 9.18 us: exchange(): lax.ppermute(m, 'gz', route('gz', d))]
    pmax x1 -> x0, blocking collectives: 38.4 us -> none  [step_size(): largest = lax.pmax(jnp.max(row_sums), ('gx', 'gy', 'gz'))]
    pallas_call x0 -> x10, Pallas kernels: none -> 37.5 us  [the longest x1 21.8 us: local(): first(own, *messages)]
    dynamic_update_slice x270 -> x0, local copies, waits for them, and re-layouts: 33.7 us -> none  [the longest x243 30.3 us: visit(): lax.dynamic_update_slice(totals, window + returned.reshape((2, 1, 1, exte...]
    ppermute x36 -> x15, starting transfers between devices: 39.9 us -> 22.5 us  [the longest x3 8.57 us: exchange(): y1 = lax.ppermute(down, 'gy', route('gy', -1))]
    another operation x3 -> x0, loops' own time: 9.42 us -> none  [paired(): return lax.fori_loop(0, extent_x * extent_y, visit, totals)]
    add x302 -> x0, other arithmetic: 5.24 us -> none  [the longest x243 3.58 us: visit(): window + returned.reshape((2, 1, 1, extent_z, bin_dimensions))]
  transfers between devices with their start and end apart: 36 -> 15, of which waited for: 33 -> 11; matrix products, arithmetic and copies ran while one was open for 0% -> 0% of each run, Pallas kernels for 0% -> 0%
where the time goes in v2:
time: 80.7 us; the launch traced here: 80.6 us
  Pallas kernels  37.5 us (46%)
  starting transfers between devices  22.5 us (28%)
  waiting for transfers between devices  20.5 us (25%)
    pallas_call x1, Pallas kernels, local(): first(own, *messages)  21.8 us
    ppermute x3, waiting for transfers between devices, exchange(): lax.ppermute(m, 'gz', route('gz', d))  9.18 us
    ppermute x3, starting transfers between devices, exchange(): y1 = lax.ppermute(down, 'gy', route('gy', -1))  8.57 us
    pallas_call x1, Pallas kernels, local(): next_kernel(s, ROOM + inputs, True)  7.31 us
    pallas_call x1, Pallas kernels, local(): next_kernel(s, ROOM + inputs, False)  6.7 us
    ppermute x3, starting transfers between devices, exchange(): x1 = lax.ppermute(down, 'gx', route('gx', -1))  5.44 us
    ppermute x3, waiting for transfers between devices, exchange(): y0 = lax.ppermute(up, 'gy', route('gy', 1))  5.43 us
    ppermute x3, starting transfers between devices, exchange(): lax.ppermute(m, 'gz', route('gz', d))  4.21 us
  transfers between devices with their start and end apart: 15, of which 11 were waited for; matrix products, arithmetic and copies ran while one was open for 0% of the time, Pallas kernels for 0%

profile of v2, /device:TPU:0, one launch (start us, length us, event | category | flops | bytes accessed | tf_op | source)
XLA Modules:
  0.0 80.6 jit_solution(6621122841132726643)
XLA Ops:
  1.4 2.0 %collective-permute-start.1 = (f32[64,128]{1,0:T(8,128)S(1)}, f32[64,128]{1,0:T(8,128)S(1)}, u32[]{:S(2)}, u32[]{:S(2)}) collective-permute-start(f32[64,128]{1,0:T(8,128)S(1)} %get-tuple-element.38), channel_id=1, source_target_pairs={{0,24},{8,0},{16,8},{24,16},{1,25},{9,1},{17,9},{25,17},{2,26},{10... | collective-permute-start | bytes 98312 | tf_op jit(solution)/shard_map/ppermute | solution.py:179
  3.4 1.5 %collective-permute-done.before.x0 = f32[64,128]{1,0:T(8,128)S(1)} collective-permute-done((f32[64,128]{1,0:T(8,128)S(1)}, f32[64,128]{1,0:T(8,128)S(1)}, u32[]{:S(2)}, u32[]{:S(2)}) %collective-permute-start) | collective-permute-done | bytes 32800 | tf_op jit(solution)/shard_map/ppermute | solution.py:178
  5.2 2.3 %collective-permute-start.2 = (f32[104,128]{1,0:T(8,128)S(1)}, f32[104,128]{1,0:T(8,128)S(1)}, u32[]{:S(2)}, u32[]{:S(2)}) collective-permute-start(f32[104,128]{1,0:T(8,128)S(1)} %get-tuple-element.40), channel_id=1, source_target_pairs={{0,2},{2,4},{4,6},{6,0},{1,3},{3,5},{5,7},{7,1},{8,10},{10,12},{12... | collective-permute-start | bytes 159752 | tf_op jit(solution)/shard_map/ppermute | solution.py:181
  7.4 2.1 %collective-permute-start.3 = (f32[104,128]{1,0:T(8,128)S(1)}, f32[104,128]{1,0:T(8,128)S(1)}, u32[]{:S(2)}, u32[]{:S(2)}) collective-permute-start(f32[104,128]{1,0:T(8,128)S(1)} %get-tuple-element.41), channel_id=1, source_target_pairs={{0,6},{2,0},{4,2},{6,4},{1,7},{3,1},{5,3},{7,5},{8,14},{10,8},{12,... | collective-permute-start | bytes 159752 | tf_op jit(solution)/shard_map/ppermute | solution.py:182
  9.5 2.2 %collective-permute-done.2.y0 = f32[104,128]{1,0:T(8,128)S(1)} collective-permute-done((f32[104,128]{1,0:T(8,128)S(1)}, f32[104,128]{1,0:T(8,128)S(1)}, u32[]{:S(2)}, u32[]{:S(2)}) %collective-permute-start.2) | collective-permute-done | bytes 53280 | tf_op jit(solution)/shard_map/ppermute | solution.py:181
  11.7 1.5 %collective-permute-done.3.y1 = f32[104,128]{1,0:T(8,128)S(1)} collective-permute-done((f32[104,128]{1,0:T(8,128)S(1)}, f32[104,128]{1,0:T(8,128)S(1)}, u32[]{:S(2)}, u32[]{:S(2)}) %collective-permute-start.3) | collective-permute-done | bytes 53280 | tf_op jit(solution)/shard_map/ppermute | solution.py:182
  13.8 1.3 %collective-permute-start.4 = (f32[256,128]{1,0:T(8,128)S(1)}, f32[256,128]{1,0:T(8,128)S(1)}, u32[]{:S(2)}, u32[]{:S(2)}) collective-permute-start(f32[256,128]{1,0:T(8,128)S(1)} %get-tuple-element.43), channel_id=1, source_target_pairs={{0,1},{1,0},{2,3},{3,2},{4,5},{5,4},{6,7},{7,6},{8,9},{9,8},{10,11... | collective-permute-start | bytes 393224 | tf_op jit(solution)/shard_map/ppermute | solution.py:184
  15.1 4.2 %collective-permute-done.4.rest_0_ = f32[256,128]{1,0:T(8,128)S(1)} collective-permute-done((f32[256,128]{1,0:T(8,128)S(1)}, f32[256,128]{1,0:T(8,128)S(1)}, u32[]{:S(2)}, u32[]{:S(2)}) %collective-permute-start.4) | collective-permute-done | bytes 131104 | tf_op jit(solution)/shard_map/ppermute | solution.py:184
  19.3 21.8 %kernel_and_first_flow.1 = (bf16[18,3456,256]{2,1,0:T(8,128)(2,1)S(1)}, f32[36,128]{1,0:T(8,128)S(1)}, f32[150,128]{1,0:T(8,128)S(1)}, f32[150,128]{1,0:T(8,128)...) custom-call(f32[180,128]{1,0:T(8,128)S(1)} %get-tuple-element.36.own, ...), custom_call_target="tpu_custom_call" | custom-call | tf_op jit(solution)/shard_map/kernel_and_first_flow/pallas_call | solution.py:522
  41.2 1.7 %collective-permute-start.6 = (f32[16,128]{1,0:T(8,128)S(1)}, f32[16,128]{1,0:T(8,128)S(1)}, u32[]{:S(2)}, u32[]{:S(2)}) collective-permute-start(f32[16,128]{1,0:T(8,128)S(1)} %get-tuple-element.52), channel_id=1, source_target_pairs={{0,24},{8,0},{16,8},{24,16},{1,25},{9,1},{17,9},{25,17},{2,26},{10... | collective-permute-start | bytes 24584 | tf_op jit(solution)/shard_map/ppermute | solution.py:179
  43.0 1.3 %collective-permute-done.5.before.x0.rest_2_ = f32[16,128]{1,0:T(8,128)S(1)} collective-permute-done((f32[16,128]{1,0:T(8,128)S(1)}, f32[16,128]{1,0:T(8,128)S(1)}, u32[]{:S(2)}, u32[]{:S(2)}) %collective-permute-start.5) | collective-permute-done | bytes 8224 | tf_op jit(solution)/shard_map/ppermute | solution.py:178
  44.3 1.0 %collective-permute-start.7 = (f32[24,128]{1,0:T(8,128)S(1)}, f32[24,128]{1,0:T(8,128)S(1)}, u32[]{:S(2)}, u32[]{:S(2)}) collective-permute-start(f32[24,128]{1,0:T(8,128)S(1)} %get-tuple-element.54), channel_id=1, source_target_pairs={{0,2},{2,4},{4,6},{6,0},{1,3},{3,5},{5,7},{7,1},{8,10},{10,12},{12... | collective-permute-start | bytes 36872 | tf_op jit(solution)/shard_map/ppermute | solution.py:181
  45.4 2.8 %collective-permute-start.8 = (f32[24,128]{1,0:T(8,128)S(1)}, f32[24,128]{1,0:T(8,128)S(1)}, u32[]{:S(2)}, u32[]{:S(2)}) collective-permute-start(f32[24,128]{1,0:T(8,128)S(1)} %get-tuple-element.55), channel_id=1, source_target_pairs={{0,6},{2,0},{4,2},{6,4},{1,7},{3,1},{5,3},{7,5},{8,14},{10,8},{12,... | collective-permute-start | bytes 36872 | tf_op jit(solution)/shard_map/ppermute | solution.py:182
  48.2 1.7 %collective-permute-done.7.y0.rest_4_ = f32[24,128]{1,0:T(8,128)S(1)} collective-permute-done((f32[24,128]{1,0:T(8,128)S(1)}, f32[24,128]{1,0:T(8,128)S(1)}, u32[]{:S(2)}, u32[]{:S(2)}) %collective-permute-start.7) | collective-permute-done | bytes 12320 | tf_op jit(solution)/shard_map/ppermute | solution.py:181
  49.9 1.4 %collective-permute-start.9 = (f32[56,128]{1,0:T(8,128)S(1)}, f32[56,128]{1,0:T(8,128)S(1)}, u32[]{:S(2)}, u32[]{:S(2)}) collective-permute-start(f32[56,128]{1,0:T(8,128)S(1)} %get-tuple-element.57), channel_id=1, source_target_pairs={{0,1},{1,0},{2,3},{3,2},{4,5},{5,4},{6,7},{7,6},{8,9},{9,8},{10,11... | collective-permute-start | bytes 86024 | tf_op jit(solution)/shard_map/ppermute | solution.py:184
  51.3 2.5 %collective-permute-done.9.rest_6_ = f32[56,128]{1,0:T(8,128)S(1)} collective-permute-done((f32[56,128]{1,0:T(8,128)S(1)}, f32[56,128]{1,0:T(8,128)S(1)}, u32[]{:S(2)}, u32[]{:S(2)}) %collective-permute-start.9) | collective-permute-done | bytes 28704 | tf_op jit(solution)/shard_map/ppermute | solution.py:184
  53.9 6.7 %next_flow.1 = (f32[36,128]{1,0:T(8,128)S(1)}, f32[1,128]{1,0:T(1,128)S(1)}, f32[16,128]{1,0:T(8,128)S(1)}, f32[16,128]{1,0:T(8,128)S(1)}) custom-call(bf16[18,3456,256]{2,1,0:T(8,128)(2,1)S(1)} %get-tuple-element.44.kernel, f32[150,128]{1,0:T(8,128)S(1)} %get-tuple-element.45.volume, f32[150,128]{1,0:T(8,128)S(1)} %get-tuple-element.46.scaled, ...), custom_call_target="tpu_custom_call" | custom-call | tf_op jit(solution)/shard_map/next_flow/pallas_call | solution.py:524
  60.6 1.7 %collective-permute-start.11 = (f32[16,128]{1,0:T(8,128)S(1)}, f32[16,128]{1,0:T(8,128)S(1)}, u32[]{:S(2)}, u32[]{:S(2)}) collective-permute-start(f32[16,128]{1,0:T(8,128)S(1)} %get-tuple-element.61), channel_id=1, source_target_pairs={{0,24},{8,0},{16,8},{24,16},{1,25},{9,1},{17,9},{25,17},{2,26},{10... | collective-permute-start | bytes 24584 | tf_op jit(solution)/shard_map/ppermute | solution.py:179
  62.4 1.3 %collective-permute-done.10.before.x0.rest_4_ = f32[16,128]{1,0:T(8,128)S(1)} collective-permute-done((f32[16,128]{1,0:T(8,128)S(1)}, f32[16,128]{1,0:T(8,128)S(1)}, u32[]{:S(2)}, u32[]{:S(2)}) %collective-permute-start.10) | collective-permute-done | bytes 8224 | tf_op jit(solution)/shard_map/ppermute | solution.py:178
  64.0 3.6 %collective-permute-start.13 = (f32[24,128]{1,0:T(8,128)S(1)}, f32[24,128]{1,0:T(8,128)S(1)}, u32[]{:S(2)}, u32[]{:S(2)}) collective-permute-start(f32[24,128]{1,0:T(8,128)S(1)} %get-tuple-element.64), channel_id=1, source_target_pairs={{0,6},{2,0},{4,2},{6,4},{1,7},{3,1},{5,3},{7,5},{8,14},{10,8},{12,... | collective-permute-start | bytes 36872 | tf_op jit(solution)/shard_map/ppermute | solution.py:182
  67.7 1.6 %collective-permute-done.12.y0.rest_6_ = f32[24,128]{1,0:T(8,128)S(1)} collective-permute-done((f32[24,128]{1,0:T(8,128)S(1)}, f32[24,128]{1,0:T(8,128)S(1)}, u32[]{:S(2)}, u32[]{:S(2)}) %collective-permute-start.12) | collective-permute-done | bytes 12320 | tf_op jit(solution)/shard_map/ppermute | solution.py:181
  69.3 1.5 %collective-permute-start.14 = (f32[56,128]{1,0:T(8,128)S(1)}, f32[56,128]{1,0:T(8,128)S(1)}, u32[]{:S(2)}, u32[]{:S(2)}) collective-permute-start(f32[56,128]{1,0:T(8,128)S(1)} %get-tuple-element.66), channel_id=1, source_target_pairs={{0,1},{1,0},{2,3},{3,2},{4,5},{5,4},{6,7},{7,6},{8,9},{9,8},{10,11... | collective-permute-start | bytes 86024 | tf_op jit(solution)/shard_map/ppermute | solution.py:184
  70.8 2.4 %collective-permute-done.14.rest_8_ = f32[56,128]{1,0:T(8,128)S(1)} collective-permute-done((f32[56,128]{1,0:T(8,128)S(1)}, f32[56,128]{1,0:T(8,128)S(1)}, u32[]{:S(2)}, u32[]{:S(2)}) %collective-permute-start.14) | collective-permute-done | bytes 28704 | tf_op jit(solution)/shard_map/ppermute | solution.py:184
  73.3 7.3 %last_flow.1 = f32[3,3,4,128]{3,2,1,0:T(4,128)} custom-call(bf16[18,3456,256]{2,1,0:T(8,128)(2,1)S(1)} %get-tuple-element.44.kernel, f32[150,128]{1,0:T(8,128)S(1)} %get-tuple-element.45.volume, f32[150,128]{1,0:T(8,128)S(1)} %get-tuple-element.46.scaled, f32[36,128]{1,0:T(8,128)S(1)} %get-tuple-element.47.conduct_own, ...), custom_call_target="tpu_custom_call" | custom-call | tf_op jit(solution)/shard_map/last_flow/pallas_call | solution.py:526
  (16 shorter events, 2.9 us)
Async XLA Ops:
  0.9 4.1 %collective-permute-start = (f32[64,128]{1,0:T(8,128)S(1)}, f32[64,128]{1,0:T(8,128)S(1)}, u32[]{:S(2)}, u32[]{:S(2)}) collective-permute-start(f32[64,128]{1,0:T(8,128)S(1)} %get-tuple-element.37), channel_id=1, source_target_pairs={{0,8},{8,16},{16,24},{24,0},{1,9},{9,17},{17,25},{25,1},{2,10},{10... | collective-permute-start | bytes 98312 | tf_op jit(solution)/shard_map/ppermute | solution.py:178
  1.4 3.7 %collective-permute-start.1 = (f32[64,128]{1,0:T(8,128)S(1)}, f32[64,128]{1,0:T(8,128)S(1)}, u32[]{:S(2)}, u32[]{:S(2)}) collective-permute-start(f32[64,128]{1,0:T(8,128)S(1)} %get-tuple-element.38), channel_id=1, source_target_pairs={{0,24},{8,0},{16,8},{24,16},{1,25},{9,1},{17,9},{25,17},{2,26},{10... | collective-permute-start | bytes 98312 | tf_op jit(solution)/shard_map/ppermute | solution.py:179
  5.2 6.5 %collective-permute-start.2 = (f32[104,128]{1,0:T(8,128)S(1)}, f32[104,128]{1,0:T(8,128)S(1)}, u32[]{:S(2)}, u32[]{:S(2)}) collective-permute-start(f32[104,128]{1,0:T(8,128)S(1)} %get-tuple-element.40), channel_id=1, source_target_pairs={{0,2},{2,4},{4,6},{6,0},{1,3},{3,5},{5,7},{7,1},{8,10},{10,12},{12... | collective-permute-start | bytes 159752 | tf_op jit(solution)/shard_map/ppermute | solution.py:181
  7.4 5.7 %collective-permute-start.3 = (f32[104,128]{1,0:T(8,128)S(1)}, f32[104,128]{1,0:T(8,128)S(1)}, u32[]{:S(2)}, u32[]{:S(2)}) collective-permute-start(f32[104,128]{1,0:T(8,128)S(1)} %get-tuple-element.41), channel_id=1, source_target_pairs={{0,6},{2,0},{4,2},{6,4},{1,7},{3,1},{5,3},{7,5},{8,14},{10,8},{12,... | collective-permute-start | bytes 159752 | tf_op jit(solution)/shard_map/ppermute | solution.py:182
  13.8 5.5 %collective-permute-start.4 = (f32[256,128]{1,0:T(8,128)S(1)}, f32[256,128]{1,0:T(8,128)S(1)}, u32[]{:S(2)}, u32[]{:S(2)}) collective-permute-start(f32[256,128]{1,0:T(8,128)S(1)} %get-tuple-element.43), channel_id=1, source_target_pairs={{0,1},{1,0},{2,3},{3,2},{4,5},{5,4},{6,7},{7,6},{8,9},{9,8},{10,11... | collective-permute-start | bytes 393224 | tf_op jit(solution)/shard_map/ppermute | solution.py:184
  41.2 3.1 %collective-permute-start.5 = (f32[16,128]{1,0:T(8,128)S(1)}, f32[16,128]{1,0:T(8,128)S(1)}, u32[]{:S(2)}, u32[]{:S(2)}) collective-permute-start(f32[16,128]{1,0:T(8,128)S(1)} %get-tuple-element.51), channel_id=1, source_target_pairs={{0,8},{8,16},{16,24},{24,0},{1,9},{9,17},{17,25},{25,1},{2,10},{10... | collective-permute-start | bytes 24584 | tf_op jit(solution)/shard_map/ppermute | solution.py:178
  41.2 3.1 %collective-permute-start.6 = (f32[16,128]{1,0:T(8,128)S(1)}, f32[16,128]{1,0:T(8,128)S(1)}, u32[]{:S(2)}, u32[]{:S(2)}) collective-permute-start(f32[16,128]{1,0:T(8,128)S(1)} %get-tuple-element.52), channel_id=1, source_target_pairs={{0,24},{8,0},{16,8},{24,16},{1,25},{9,1},{17,9},{25,17},{2,26},{10... | collective-permute-start | bytes 24584 | tf_op jit(solution)/shard_map/ppermute | solution.py:179
  44.3 5.5 %collective-permute-start.7 = (f32[24,128]{1,0:T(8,128)S(1)}, f32[24,128]{1,0:T(8,128)S(1)}, u32[]{:S(2)}, u32[]{:S(2)}) collective-permute-start(f32[24,128]{1,0:T(8,128)S(1)} %get-tuple-element.54), channel_id=1, source_target_pairs={{0,2},{2,4},{4,6},{6,0},{1,3},{3,5},{5,7},{7,1},{8,10},{10,12},{12... | collective-permute-start | bytes 36872 | tf_op jit(solution)/shard_map/ppermute | solution.py:181
  45.4 4.5 %collective-permute-start.8 = (f32[24,128]{1,0:T(8,128)S(1)}, f32[24,128]{1,0:T(8,128)S(1)}, u32[]{:S(2)}, u32[]{:S(2)}) collective-permute-start(f32[24,128]{1,0:T(8,128)S(1)} %get-tuple-element.55), channel_id=1, source_target_pairs={{0,6},{2,0},{4,2},{6,4},{1,7},{3,1},{5,3},{7,5},{8,14},{10,8},{12,... | collective-permute-start | bytes 36872 | tf_op jit(solution)/shard_map/ppermute | solution.py:182
  49.9 3.9 %collective-permute-start.9 = (f32[56,128]{1,0:T(8,128)S(1)}, f32[56,128]{1,0:T(8,128)S(1)}, u32[]{:S(2)}, u32[]{:S(2)}) collective-permute-start(f32[56,128]{1,0:T(8,128)S(1)} %get-tuple-element.57), channel_id=1, source_target_pairs={{0,1},{1,0},{2,3},{3,2},{4,5},{5,4},{6,7},{7,6},{8,9},{9,8},{10,11... | collective-permute-start | bytes 86024 | tf_op jit(solution)/shard_map/ppermute | solution.py:184
  60.6 3.1 %collective-permute-start.10 = (f32[16,128]{1,0:T(8,128)S(1)}, f32[16,128]{1,0:T(8,128)S(1)}, u32[]{:S(2)}, u32[]{:S(2)}) collective-permute-start(f32[16,128]{1,0:T(8,128)S(1)} %get-tuple-element.60), channel_id=1, source_target_pairs={{0,8},{8,16},{16,24},{24,0},{1,9},{9,17},{17,25},{25,1},{2,10},{10... | collective-permute-start | bytes 24584 | tf_op jit(solution)/shard_map/ppermute | solution.py:178
  60.6 3.1 %collective-permute-start.11 = (f32[16,128]{1,0:T(8,128)S(1)}, f32[16,128]{1,0:T(8,128)S(1)}, u32[]{:S(2)}, u32[]{:S(2)}) collective-permute-start(f32[16,128]{1,0:T(8,128)S(1)} %get-tuple-element.61), channel_id=1, source_target_pairs={{0,24},{8,0},{16,8},{24,16},{1,25},{9,1},{17,9},{25,17},{2,26},{10... | collective-permute-start | bytes 24584 | tf_op jit(solution)/shard_map/ppermute | solution.py:179
  63.7 5.5 %collective-permute-start.12 = (f32[24,128]{1,0:T(8,128)S(1)}, f32[24,128]{1,0:T(8,128)S(1)}, u32[]{:S(2)}, u32[]{:S(2)}) collective-permute-start(f32[24,128]{1,0:T(8,128)S(1)} %get-tuple-element.63), channel_id=1, source_target_pairs={{0,2},{2,4},{4,6},{6,0},{1,3},{3,5},{5,7},{7,1},{8,10},{10,12},{12... | collective-permute-start | bytes 36872 | tf_op jit(solution)/shard_map/ppermute | solution.py:181
  64.0 5.3 %collective-permute-start.13 = (f32[24,128]{1,0:T(8,128)S(1)}, f32[24,128]{1,0:T(8,128)S(1)}, u32[]{:S(2)}, u32[]{:S(2)}) collective-permute-start(f32[24,128]{1,0:T(8,128)S(1)} %get-tuple-element.64), channel_id=1, source_target_pairs={{0,6},{2,0},{4,2},{6,4},{1,7},{3,1},{5,3},{7,5},{8,14},{10,8},{12,... | collective-permute-start | bytes 36872 | tf_op jit(solution)/shard_map/ppermute | solution.py:182
  69.3 3.9 %collective-permute-start.14 = (f32[56,128]{1,0:T(8,128)S(1)}, f32[56,128]{1,0:T(8,128)S(1)}, u32[]{:S(2)}, u32[]{:S(2)}) collective-permute-start(f32[56,128]{1,0:T(8,128)S(1)} %get-tuple-element.66), channel_id=1, source_target_pairs={{0,1},{1,0},{2,3},{3,2},{4,5},{5,4},{6,7},{7,6},{8,9},{9,8},{10,11... | collective-permute-start | bytes 86024 | tf_op jit(solution)/shard_map/ppermute | solution.py:184

commit v3 on v2

--- a/solution.py
+++ b/solution.py
@@ -1,3 +1,5 @@
+import functools
+
 import jax
 import jax.numpy as jnp
 from jax import lax
@@ -37,11 +39,6 @@
         self.pairs = nx * ny * self.half
         self.columns = self.px * self.py
 
-    def place(self, p):
-        zp = p % self.half
-        column = p // self.half
-        return column // self.ny, column % self.ny, zp, column * self.nz + 2 * zp
-
 
 class Faces:
     def __init__(self, s, fields):
@@ -138,8 +135,9 @@
         n = self.fields * rows
         return jnp.maximum(top[...], jnp.maximum(refs[0][n : n + 1, :], refs[-1][n : n + 1, :]))
 
-    def y_packer(self):
-        def body(own, top, before, after, up, down, top_out, halo):
+    def y_packer(self, waits):
+        def body(own, top, before, after, *rest):
+            up, down, top_out, halo = rest[waits:]
             self.put_own(halo, own)
             self.put_x(halo, before, after)
             most = self.largest(top, self.x_rows, (before, after))
@@ -154,10 +152,11 @@
             name="pack_y",
         )
 
-    def z_packer(self):
+    def z_packer(self, waits):
         count = len(self.z_messages())
 
         def body(own, top, x0, x1, y0, y1, *rest):
+            rest = rest[waits:]
             messages, top_out, halo = rest[:count], rest[count], rest[-1]
             self.put_own(halo, own)
             self.put_x(halo, x0, x1)
@@ -174,14 +173,20 @@
             name="pack_z",
         )
 
-    def exchange(self, own, top, up, down):
+    def exchange(self, own, top, up, down, during=None):
+        def beside(phase, top):
+            return () if during is None else (during(phase, top),)
+
         x0 = lax.ppermute(up, "gx", route("gx", 1))
         x1 = lax.ppermute(down, "gx", route("gx", -1))
-        up, down, top = self.y_packer()(own, top, x0, x1)
+        waits = beside(0, top)
+        up, down, top = self.y_packer(len(waits))(own, top, x0, x1, *waits)
         y0 = lax.ppermute(up, "gy", route("gy", 1))
         y1 = lax.ppermute(down, "gy", route("gy", -1))
-        *messages, top = self.z_packer()(own, top, x0, x1, y0, y1)
+        waits = beside(1, top)
+        *messages, top = self.z_packer(len(waits))(own, top, x0, x1, y0, y1, *waits)
         z = [lax.ppermute(m, "gz", route("gz", d)) for m, d in zip(messages, (1, -1))]
+        beside(2, top)
         return (own, top, x0, x1, y0, y1, *z)
 
     def lay_out(self, halo, own, x0, x1, y0, y1, z):
@@ -273,9 +278,10 @@
     return jnp.concatenate([gains[cell], gains[cell + 1]], axis=0).astype(jnp.bfloat16)
 
 
-def keep_sums(s, total, own, sums):
-    sums[pl.ds(pl.multiple_of(own * 8, 8), 8), :] = total[0:8, 0 : s.slots]
-    sums[pl.ds(pl.multiple_of(own * 8 + 8, 8), 8), :] = total[8:16, s.slots : 2 * s.slots]
+def add_sums(s, total, cell, sums):
+    for k in range(2):
+        rows = pl.ds(pl.multiple_of((cell + k) * 8, 8), 8)
+        sums[rows, :] = sums[rows, :] + total[8 * k : 8 * k + 8, k * s.slots : (k + 1) * s.slots]
 
 
 def flow_of(s, sums, conduct_own, temp_own):
@@ -287,33 +293,196 @@
     return flow, weight
 
 
-def gathered(s, gains, kernel, p, x, y, zp):
-    parts = []
+def line(s, c):
+    own = combos_x(s)
+    x, side = (c + 1) // 3, c - own
+    return (
+        jnp.where(c < own, x, side * (s.nx - 1)),
+        jnp.where(c < own, c - 2 * x + 1, side * (s.px - 1)),
+    )
+
+
+def apply_line(s, c, yz, gains, kernel, sums):
+    x, source_x = line(s, c)
+    y, zp = yz // s.half, yz % s.half
+    parts = [
+        gain_pair(gains, (source_x * s.py + y + j) * s.pz + 2 * zp + e) for j in range(3) for e in range(3)
+    ]
+    total = jnp.dot(jnp.concatenate(parts, axis=1), kernel[c, yz], preferred_element_type=jnp.float32)
+    add_sums(s, total, 2 * (x * s.ny * s.half + yz), sums)
+
+
+def kernel_shape(s):
+    return jax.ShapeDtypeStruct((combos_x(s) + 2, s.ny * s.half, 9 * s.slots, 2 * s.slots), jnp.bfloat16)
+
+
+def conductivity(temp):
+    return temp * temp * jnp.sqrt(temp)
+
+
+def rows_of(s, k, ref, cell):
+    return jnp.broadcast_to(ref[k, pl.ds(cell, 1), :], (8, s.slots))
+
+
+def on_grid(ref, d, count):
+    return (ref[d * count : (d + 1) * count, :] - 0.5 + ROUNDER) - ROUNDER
+
+
+def source_tables(s, ref, count, halves):
+    square = 0.0
+    for d in range(3):
+        q = on_grid(ref, d, count)
+        halves[2 * d] = rounded(q)
+        halves[2 * d + 1] = q - rounded(q)
+        square = square + q * q
+    for d, part in enumerate(split3(square)):
+        halves[6 + d] = part
+
+
+def source_quads(s, halves, first_cell, present, left, at):
+    row = lax.broadcasted_iota(jnp.int32, (8, s.slots), 0)
+    zero8 = jnp.zeros((8, s.slots), jnp.float32)
+    blocks = []
+    for z in range(s.pz):
+        if z not in present:
+            blocks += [zero8] * 4
+            continue
+        cell = first_cell + present.index(z)
+        for d in range(3):
+            block = jnp.where(row % 2 == 0, rows_of(s, 2 * d, halves, cell), rows_of(s, 2 * d + 1, halves, cell))
+            rest = jnp.where(row < 7, 1.0, rows_of(s, 6 + d, halves, cell))
+            blocks.append(jnp.where(row < 4, block, rest))
+        blocks.append(zero8)
+    for zp in range(s.half):
+        quad = jnp.concatenate(blocks[8 * zp : 8 * zp + 16], axis=0)
+        left[at * s.half + zp] = quad.T.astype(jnp.bfloat16)
+
+
+def target_tables(s, own, targets):
+    for d in range(3):
+        q = on_grid(own, d, s.cells)
+        for k, shift in enumerate(SHIFTS):
+            t = q - float(shift)
+            h = rounded(t)
+            for r, part in enumerate((-2.0 * h, -2.0 * (t - h), *split3(t * t))):
+                targets[(d * 3 + k) * 5 + r] = part
+
+
+def target_blocks(s, targets, cell, low, high):
+    row = lax.broadcasted_iota(jnp.int32, (8, s.slots), 0)
+    rows = []
+    for d in range(3):
+        for k in range(3):
+            part = [rows_of(s, (d * 3 + k) * 5 + r, targets, cell) for r in range(5)]
+            block = jnp.where(row == 5, part[3], jnp.where(row == 6, part[4], 1.0))
+            block = jnp.where(row < 4, part[1], jnp.where(row == 4, part[2], block))
+            rows.append(jnp.where(row < 2, part[0], block))
     for i in range(3):
         for j in range(3):
-            for e in range(3):
-                parts.append(gain_pair(gains, ((x + i) * s.py + y + j) * s.pz + 2 * zp + e))
-    return jnp.dot(jnp.concatenate(parts, axis=1), kernel[p], preferred_element_type=jnp.float32)
-
-
-def conductivity(temp):
-    return temp * temp * jnp.sqrt(temp)
-
-
-def first_kernel(s):
+            low[cell * 9 + i * 3 + j] = jnp.concatenate([rows[i], rows[3 + j]], 0).astype(jnp.bfloat16)
+    for e in range(3):
+        high[cell * 3 + e] = jnp.concatenate([rows[6 + e], jnp.zeros_like(rows[0])], 0).astype(jnp.bfloat16)
+
+
+def pair_block(s, c, yz, cell, i, j, e, source, low, high, kernel):
+    nothing = jnp.zeros((16, s.slots), jnp.bfloat16)
+    lanes = []
+    for k in range(2):
+        parts = [nothing] * 8
+        parts[2 * (e + k)] = low[(cell + k) * 9 + i * 3 + j]
+        parts[2 * (e + k) + 1] = high[(cell + k) * 3 + e]
+        lanes.append(jnp.concatenate(parts, axis=0))
+    right = jnp.concatenate(lanes, axis=1)
+    dist = jnp.dot(source, right, preferred_element_type=jnp.float32)
+    gap = 1.0 - dist * lax.rsqrt(jnp.maximum(dist, 2.5e-7))
+    value = jnp.maximum((gap * gap * gap).astype(jnp.bfloat16), jnp.bfloat16(0.0))
+    kernel[c, yz, (j * 3 + e) * s.slots : (j * 3 + e + 1) * s.slots, :] = value
+
+
+def inner_z(s, zp, e):
+    return 0 <= 2 * zp + e - 1 and 2 * zp + e < s.nz
+
+
+def combos_x(s):
+    return 3 * s.nx - 2
+
+
+def inner_kernel(s, room, begin, end):
+    slots = s.slots
+    opening = begin == 0
+
+    def blocks(left, low, high, kernel):
+        def along_x(c, carry):
+            x, source_x = line(s, c)
+            for yz in range(s.ny * s.half):
+                y, zp = yz // s.half, yz % s.half
+                cell = 2 * (x * s.ny * s.half + yz)
+                for j in range(3):
+                    if not 0 <= y + j - 1 < s.ny:
+                        continue
+                    source = left[((source_x - 1) * s.ny + y + j - 1) * s.half + zp]
+                    for e in range(3):
+                        if inner_z(s, zp, e):
+                            pair_block(s, c, yz, cell, source_x - x, j, e, source, low, high, kernel)
+            return carry
+
+        lax.fori_loop(begin, end, along_x, 0)
+
+    def first(own, after, kernel, low, high, left, done, halves, targets):
+        done[...] = after[...]
+        source_tables(s, own, s.cells, halves)
+        target_tables(s, own, targets)
+
+        def prepare(column, carry):
+            source_quads(s, halves, column * s.nz, list(range(1, s.nz + 1)), left, column)
+            for z in range(s.nz):
+                target_blocks(s, targets, column * s.nz + z, low, high)
+            return carry
+
+        lax.fori_loop(0, s.nx * s.ny, prepare, 0)
+        blocks(left, low, high, kernel)
+
+    def second(kernel_in, low, high, left, after, kernel, done):
+        done[...] = after[...]
+        blocks(left, low, high, kernel)
+
+    kernel = kernel_shape(s)
+    if opening:
+        return pl.pallas_call(
+            first,
+            out_shape=(
+                kernel,
+                jax.ShapeDtypeStruct((s.cells * 9, 16, slots), jnp.bfloat16),
+                jax.ShapeDtypeStruct((s.cells * 3, 16, slots), jnp.bfloat16),
+                jax.ShapeDtypeStruct((s.pairs, slots, 128), jnp.bfloat16),
+                f32(1, slots),
+            ),
+            scratch_shapes=[
+                pltpu.VMEM((9, s.cells, slots), jnp.float32),
+                pltpu.VMEM((45, s.cells, slots), jnp.float32),
+            ],
+            compiler_params=pltpu.CompilerParams(vmem_limit_bytes=room),
+            name="inner_first",
+        )
+    return pl.pallas_call(
+        second,
+        out_shape=(kernel, f32(1, slots)),
+        input_output_aliases={0: 0},
+        compiler_params=pltpu.CompilerParams(vmem_limit_bytes=room),
+        name="inner_second",
+    )
+
+
+def outer_kernel(s, room):
     slots = s.slots
     fields = Faces(s, FIELDS)
     faces = Faces(s, 1)
     arrivals = len(fields.z_messages())
-    inputs = 4 * slots * sum(
-        rounded_up(m.shape[0])
-        for m in (f32(FIELDS * s.cells), *fields.x_messages(), *fields.y_messages(), *fields.z_messages())
-    )
-
-    def body(own, x0, x1, y0, y1, *rest):
+
+    def body(kernel_in, low, high, own, x0, x1, y0, y1, *rest):
         z, rest = rest[:arrivals], rest[arrivals:]
-        (kernel_out, flow_out, volume_out, scaled_out, conduct_own, temp_own, top_out, up, down,
-         halo, left, gains, sums, halves, targets) = rest
+        (kernel, flow_out, volume_out, scaled_out, conduct_own, temp_own, top_out, up, down,
+         halo, left, gains, sums, halves) = rest
         fields.lay_out(halo, own, x0, x1, y0, y1, z)
         temp = halo.at[pl.ds(4 * s.padded, s.padded)]
         volume_out[...] = halo[3 * s.padded : 4 * s.padded, :]
@@ -321,87 +490,34 @@
         temp_own[...] = own[4 * s.cells : 5 * s.cells, :]
         conduct_own[...] = conductivity(temp_own[...])
         source_rows(s, volume_out, scaled_out, temp, gains)
-        row = lax.broadcasted_iota(jnp.int32, (8, slots), 0)
-
-        even = row % 2 == 0
-        square = 0.0
-        for d in range(3):
-            q = (halo[d * s.padded : (d + 1) * s.padded, :] - 0.5 + ROUNDER) - ROUNDER
-            halves[2 * d] = rounded(q)
-            halves[2 * d + 1] = q - rounded(q)
-            square = square + q * q
-            q = (own[d * s.cells : (d + 1) * s.cells, :] - 0.5 + ROUNDER) - ROUNDER
-            for k, shift in enumerate(SHIFTS):
-                t = q - float(shift)
-                h = rounded(t)
-                for r, part in enumerate((-2.0 * h, -2.0 * (t - h), *split3(t * t))):
-                    targets[(d * 3 + k) * 5 + r] = part
-        for d, part in enumerate(split3(square)):
-            halves[6 + d] = part
-
-        def spread(ref, k, cell):
-            return jnp.broadcast_to(ref[k, pl.ds(cell, 1), :], (8, slots))
+        source_tables(s, halo, s.padded, halves)
 
         def features(column, carry):
-            blocks = []
-            for z in range(s.pz):
-                cell = column * s.pz + z
-                for d in range(3):
-                    block = jnp.where(even, spread(halves, 2 * d, cell), spread(halves, 2 * d + 1, cell))
-                    rest = jnp.where(row < 7, 1.0, spread(halves, 6 + d, cell))
-                    blocks.append(jnp.where(row < 4, block, rest))
-                blocks.append(jnp.zeros((8, slots), jnp.float32))
-            for zp in range(s.half):
-                quad = jnp.concatenate(blocks[8 * zp : 8 * zp + 16], axis=0)
-                left[column * s.half + zp] = quad.T.astype(jnp.bfloat16)
+            source_quads(s, halves, column * s.pz, list(range(s.pz)), left, column)
             return carry
 
         lax.fori_loop(0, s.columns, features, 0, unroll=5)
 
-        def target_rows(cell, d):
-            out = []
-            for k in range(3):
-                part = [spread(targets, (d * 3 + k) * 5 + r, cell) for r in range(5)]
-                block = jnp.where(row == 5, part[3], jnp.where(row == 6, part[4], 1.0))
-                block = jnp.where(row < 4, part[1], jnp.where(row == 4, part[2], block))
-                out.append(jnp.where(row < 2, part[0], block))
-            return out
-
-        nothing = jnp.zeros((16, slots), jnp.bfloat16)
-        zero8 = jnp.zeros((8, slots), jnp.float32)
-
-        def pair(p, carry):
-            x, y, zp, cell = s.place(p)
-            rows = [[target_rows(cell + k, d) for d in range(3)] for k in range(2)]
-            low = [
-                [[jnp.concatenate([rows[k][0][i], rows[k][1][j]], 0).astype(jnp.bfloat16) for j in range(3)]
-                 for i in range(3)]
-                for k in range(2)
-            ]
-            high = [
-                [jnp.concatenate([rows[k][2][i], zero8], 0).astype(jnp.bfloat16) for i in range(3)]
-                for k in range(2)
-            ]
-            for i in range(3):
+        sums[...] = jnp.zeros_like(sums)
+
+        def along_x(skip, c, carry):
+            x, source_x = line(s, c)
+            for yz in range(s.ny * s.half):
+                y, zp = yz // s.half, yz % s.half
+                cell = 2 * (x * s.ny * s.half + yz)
                 for j in range(3):
-                    source = left[((x + i) * s.py + y + j) * s.half + zp]
+                    inside = skip and 0 <= y + j - 1 < s.ny
+                    source = left[(source_x * s.py + y + j) * s.half + zp]
                     for e in range(3):
-                        lanes = []
-                        for k in range(2):
-                            parts = [nothing] * 8
-                            parts[2 * (e + k)] = low[k][i][j]
-                            parts[2 * (e + k) + 1] = high[k][e]
-                            lanes.append(jnp.concatenate(parts, axis=0))
-                        right = jnp.concatenate(lanes, axis=1)
-                        dist = jnp.dot(source, right, preferred_element_type=jnp.float32)
-                        gap = 1.0 - dist * lax.rsqrt(jnp.maximum(dist, 2.5e-7))
-                        kernel = jnp.maximum((gap * gap * gap).astype(jnp.bfloat16), jnp.bfloat16(0.0))
-                        at = ((i * 3 + j) * 3 + e) * slots
-                        kernel_out[p, at : at + slots, :] = kernel
-            keep_sums(s, gathered(s, gains, kernel_out, p, x, y, zp), cell, sums)
+                        if not (inside and inner_z(s, zp, e)):
+                            pair_block(s, c, yz, cell, source_x - x, j, e, source, low, high, kernel)
+                if yz > 0:
+                    apply_line(s, c, yz - 1, gains, kernel, sums)
+            apply_line(s, c, s.ny * s.half - 1, gains, kernel, sums)
             return carry
 
-        lax.fori_loop(0, s.pairs, pair, 0, unroll=2)
+        lax.fori_loop(0, combos_x(s), functools.partial(along_x, True), 0)
+        lax.fori_loop(combos_x(s), combos_x(s) + 2, functools.partial(along_x, False), 0)
 
         flow, weight = flow_of(s, sums, conduct_own[...], temp_own[...])
         flow_out[...] = flow
@@ -411,10 +527,10 @@
         faces.pack_x(flow_out, top, up, down)
 
     cells, padded = f32(s.cells, slots), f32(s.padded, slots)
-    call = pl.pallas_call(
+    return pl.pallas_call(
         body,
         out_shape=(
-            jax.ShapeDtypeStruct((s.pairs, 27 * slots, 2 * slots), jnp.bfloat16),
+            kernel_shape(s),
             cells,
             padded,
             padded,
@@ -423,18 +539,17 @@
             f32(1, slots),
             *faces.x_messages(),
         ),
+        input_output_aliases={0: 0},
         scratch_shapes=[
             fields.halo_shape,
             pltpu.VMEM((s.columns * s.half, slots, 128), jnp.bfloat16),
             pltpu.VMEM((s.padded, 8, slots), jnp.float32),
             pltpu.VMEM((s.cells * 8, slots), jnp.float32),
             pltpu.VMEM((9, s.padded, slots), jnp.float32),
-            pltpu.VMEM((45, s.cells, slots), jnp.float32),
         ],
-        compiler_params=pltpu.CompilerParams(vmem_limit_bytes=ROOM),
-        name="kernel_and_first_flow",
+        compiler_params=pltpu.CompilerParams(vmem_limit_bytes=room),
+        name="outer_and_first_flow",
     )
-    return call, inputs
 
 
 def next_kernel(s, room, last):
@@ -455,12 +570,14 @@
         most = faces.latest_top(top, z)
         source_rows(s, volume, scaled, temp, gains)
 
-        def pair(p, carry):
-            x, y, zp, cell = s.place(p)
-            keep_sums(s, gathered(s, gains, kernel, p, x, y, zp), cell, sums)
+        sums[...] = jnp.zeros_like(sums)
+
+        def along_x(c, carry):
+            for yz in range(s.ny * s.half):
+                apply_line(s, c, yz, gains, kernel, sums)
             return carry
 
-        lax.fori_loop(0, s.pairs, pair, 0)
+        lax.fori_loop(0, combos_x(s) + 2, along_x, 0, unroll=3)
         flow, _ = flow_of(s, sums, conduct_own[...], own[...])
         if last and covered():
             rows, block, arrived = rest
@@ -517,15 +634,28 @@
     fields, faces = Faces(s, FIELDS), Faces(s, 1)
     arguments = (bin_fill_counts, relative_placements, mass_per_density, opening_heat_level)
     started = start_kernel(s)(*[pltpu.with_memory_space_constraint(a, pltpu.HBM) for a in arguments])
-    own, _, *messages = fields.exchange(*started)
-    first, inputs = first_kernel(s)
-    kernel, flow1, volume, scaled, conduct_own, temp_own, top, up, down = first(own, *messages)
+    made = []
+    own_bytes = 4 * slots * rounded_up(FIELDS * s.cells)
+    parts = (0, 2 * combos_x(s) // 7, 5 * combos_x(s) // 7, combos_x(s))
+
+    def during(phase, after):
+        begin, end = parts[phase], parts[phase + 1]
+        if phase == 0:
+            *outs, done = inner_kernel(s, ROOM - own_bytes - 4096, begin, end)(started[0], after)
+            made.extend(outs)
+        else:
+            made[0], done = inner_kernel(s, ROOM, begin, end)(*made, after)
+        return done
+
+    own, _, *messages = fields.exchange(*started, during)
+    kernel, low, high, _ = made
+    kernel, flow1, volume, scaled, conduct_own, temp_own, top, up, down = outer_kernel(s, ROOM - own_bytes)(
+        kernel, low, high, own, *messages
+    )
     arrived = faces.exchange(flow1, top, up, down)
-    flow2, top, up, down = next_kernel(s, ROOM + inputs, False)(kernel, volume, scaled, conduct_own, *arrived)
+    flow2, top, up, down = next_kernel(s, ROOM, False)(kernel, volume, scaled, conduct_own, *arrived)
     arrived = faces.exchange(flow2, top, up, down)
-    (final,) = next_kernel(s, ROOM + inputs, True)(
-        kernel, volume, scaled, conduct_own, temp_own, flow1, *arrived
-    )
+    (final,) = next_kernel(s, ROOM, True)(kernel, volume, scaled, conduct_own, temp_own, flow1, *arrived)
     if not covered():
         top, flow3 = lax.optimization_barrier((arrived[1], final))
         step = step_factor / lax.pmax(jnp.max(top), AXES)

time: 80.7 us -> 71.6 us (0.89)
  waiting for transfers between devices: 20.5 us -> 11.7 us
  Pallas kernels: 37.5 us -> 36.1 us
  starting transfers between devices: 22.5 us -> 23.6 us
    ppermute x3, waiting for transfers between devices: 9.18 us -> 5.68 us  [exchange(): lax.ppermute(m, 'gz', route('gz', d))]
    ppermute x3, waiting for transfers between devices: 5.43 us -> 3.29 us  [exchange(): y0 = lax.ppermute(up, 'gy', route('gy', 1))]
    ppermute x3, waiting for transfers between devices: 4.19 us -> 2.66 us  [exchange(): x0 = lax.ppermute(up, 'gx', route('gx', 1))]
    ppermute x3, waiting for transfers between devices: 1.5 us -> 0.01 us  [exchange(): y1 = lax.ppermute(down, 'gy', route('gy', -1))]
    pallas_call x9 -> x12, Pallas kernels: 36.6 us -> 35.2 us  [the longest x1 15.4 us: local(): outer_kernel(s, ROOM - own_bytes)(kernel, low, high, own, *messages)]
    ppermute x3, starting transfers between devices: 8.57 us -> 9.56 us  [exchange(): y1 = lax.ppermute(down, 'gy', route('gy', -1))]
    ppermute x3, starting transfers between devices: 4.21 us -> 5.18 us  [exchange(): lax.ppermute(m, 'gz', route('gz', d))]
    ppermute x3, starting transfers between devices: 3.61 us -> 2.72 us  [exchange(): y0 = lax.ppermute(up, 'gy', route('gy', 1))]
  transfers between devices with their start and end apart: 15 -> 15, of which waited for: 11 -> 7; matrix products, arithmetic and copies ran while one was open for 0% -> 0% of each run, Pallas kernels for 0% -> 13%
where the time goes in v3:
time: 71.6 us; the launch traced here: 71.5 us
  Pallas kernels  36.1 us (50%)
  starting transfers between devices  23.6 us (33%)
  waiting for transfers between devices  11.7 us (16%)
    pallas_call x1, Pallas kernels, local(): outer_kernel(s, ROOM - own_bytes)(kernel, low, high, own, *messages)  15.4 us
    ppermute x3, starting transfers between devices, exchange(): y1 = lax.ppermute(down, 'gy', route('gy', -1))  9.56 us
    ppermute x3, waiting for transfers between devices, exchange(): lax.ppermute(m, 'gz', route('gz', d))  5.68 us
    pallas_call x2, Pallas kernels, during(): made[0], done = inner_kernel(s, ROOM, begin, end)(*made, after)  5.56 us
    pallas_call x1, Pallas kernels, local(): next_kernel(s, ROOM, True)  5.48 us
    ppermute x3, starting transfers between devices, exchange(): x1 = lax.ppermute(down, 'gx', route('gx', -1))  5.44 us
    ppermute x3, starting transfers between devices, exchange(): lax.ppermute(m, 'gz', route('gz', d))  5.18 us
    pallas_call x1, Pallas kernels, local(): next_kernel(s, ROOM, False)(kernel, volume, scaled, conduct_own, *arrived)  4.86 us
  transfers between devices with their start and end apart: 15, of which 7 were waited for; matrix products, arithmetic and copies ran while one was open for 0% of the time, Pallas kernels for 13%

profile of v3, /device:TPU:0, one launch (start us, length us, event | category | flops | bytes accessed | tf_op | source)
XLA Modules:
  0.0 71.5 jit_solution(7091998192472793590)
XLA Ops:
  0.0 0.9 %start.1 = (f32[180,128]{1,0:T(8,128)S(1)}, f32[1,128]{1,0:T(1,128)S(1)}, f32[64,128]{1,0:T(8,128)S(1)}, f32[64,128]{1,0:T(8,128)S(1)}) custom-call(s32[3,3,4]{2,1,0:T(4,128)} %counts_in.1, f32[3,3,3,4,128]{4,3,2,1,0:T(4,128)} %placements_in.1, f32[3,3,4,128]{3,2,1,0:T(4,128)} %mass_in.1, f32[3,3,4,128]{3,2,1,0:T(4,128)} %temp_in.1), custom_call_target="tpu_custom_call" | custom-call | tf_op jit(solution)/shard_map/start/pallas_call | solution.py:636
  1.4 2.0 %collective-permute-start.1 = (f32[64,128]{1,0:T(8,128)S(1)}, f32[64,128]{1,0:T(8,128)S(1)}, u32[]{:S(2)}, u32[]{:S(2)}) collective-permute-start(f32[64,128]{1,0:T(8,128)S(1)} %get-tuple-element.52), channel_id=1, source_target_pairs={{0,24},{8,0},{16,8},{24,16},{1,25},{9,1},{17,9},{25,17},{2,26},{10... | collective-permute-start | bytes 98312 | tf_op jit(solution)/shard_map/ppermute | solution.py:181
  3.4 3.6 %inner_first.1 = (bf16[9,6,1152,256]{3,2,1,0:T(8,128)(2,1)S(1)}, bf16[324,16,128]{2,1,0:T(8,128)(2,1)S(1)}, bf16[108,16,128]{2,1,0:T(8,128)(2,1)S(1)}, bf16[18,128,128]{2,1,0:T(8,128)(2,1)S(1)}, f32[1,128]{1,0:T(1,128)S(1)}) custom-call(f32[180,128]{1,0:T(8,128)S(1)} %get-tuple-element.45.own, f32[1,128]{1,0:T(1,128)S(1)} %get-tuple-element.46.after.top), custom_call_target="tpu_custom_call" | custom-call | tf_op jit(solution)/shard_map/inner_first/pallas_call | solution.py:644
  7.1 2.4 %collective-permute-start.2 = (f32[104,128]{1,0:T(8,128)S(1)}, f32[104,128]{1,0:T(8,128)S(1)}, u32[]{:S(2)}, u32[]{:S(2)}) collective-permute-start(f32[104,128]{1,0:T(8,128)S(1)} %get-tuple-element.56), channel_id=1, source_target_pairs={{0,2},{2,4},{4,6},{6,0},{1,3},{3,5},{5,7},{7,1},{8,10},{10,12},{12... | collective-permute-start | bytes 159752 | tf_op jit(solution)/shard_map/ppermute | solution.py:184
  9.5 2.1 %collective-permute-start.3 = (f32[104,128]{1,0:T(8,128)S(1)}, f32[104,128]{1,0:T(8,128)S(1)}, u32[]{:S(2)}, u32[]{:S(2)}) collective-permute-start(f32[104,128]{1,0:T(8,128)S(1)} %get-tuple-element.57), channel_id=1, source_target_pairs={{0,6},{2,0},{4,2},{6,4},{1,7},{3,1},{5,3},{7,5},{8,14},{10,8},{12,... | collective-permute-start | bytes 159752 | tf_op jit(solution)/shard_map/ppermute | solution.py:185
  11.6 3.3 %inner_second.2 = (bf16[9,6,1152,256]{3,2,1,0:T(8,128)(2,1)S(1)}, f32[1,128]{1,0:T(1,128)S(1)}) custom-call(bf16[9,6,1152,256]{3,2,1,0:T(8,128)(2,1)S(1)} %get-tuple-element.47.kernel_in, bf16[324,16,128]{2,1,0:T(8,128)(2,1)S(1)} %get-tuple-element.48.low, bf16[108,16,128]{2,1,0:T(8,128)(2,1)S(1)} %get-tuple-element.49.high, ...), custom_call_target="tpu_custom_call", output_to_operand_aliasing={{0}: (0, {})} | custom-call | tf_op jit(solution)/shard_map/inner_second/pallas_call | solution.py:647
  15.1 1.7 %collective-permute-start.4 = (f32[256,128]{1,0:T(8,128)S(1)}, f32[256,128]{1,0:T(8,128)S(1)}, u32[]{:S(2)}, u32[]{:S(2)}) collective-permute-start(f32[256,128]{1,0:T(8,128)S(1)} %get-tuple-element.61), channel_id=1, source_target_pairs={{0,1},{1,0},{2,3},{3,2},{4,5},{5,4},{6,7},{7,6},{8,9},{9,8},{10,11... | collective-permute-start | bytes 393224 | tf_op jit(solution)/shard_map/ppermute | solution.py:188
  16.8 2.2 %inner_second.3 = (bf16[9,6,1152,256]{3,2,1,0:T(8,128)(2,1)S(1)}, f32[1,128]{1,0:T(1,128)}) custom-call(bf16[9,6,1152,256]{3,2,1,0:T(8,128)(2,1)S(1)} %get-tuple-element.55.kernel_in, bf16[324,16,128]{2,1,0:T(8,128)(2,1)S(1)} %get-tuple-element.48.low, bf16[108,16,128]{2,1,0:T(8,128)(2,1)S(1)} %get-tuple-element.49.high, ...), custom_call_target="tpu_custom_call", output_to_operand_aliasing={{0}: (0, {})} | custom-call | tf_op jit(solution)/shard_map/inner_second/pallas_call | solution.py:647
  19.1 1.1 %collective-permute-done.4.rest_0_ = f32[256,128]{1,0:T(8,128)S(1)} collective-permute-done((f32[256,128]{1,0:T(8,128)S(1)}, f32[256,128]{1,0:T(8,128)S(1)}, u32[]{:S(2)}, u32[]{:S(2)}) %collective-permute-start.4) | collective-permute-done | bytes 131104 | tf_op jit(solution)/shard_map/ppermute | solution.py:188
  20.1 15.4 %outer_and_first_flow.1 = (bf16[9,6,1152,256]{3,2,1,0:T(8,128)(2,1)S(1)}, f32[36,128]{1,0:T(8,128)S(1)}, f32[150,128]{1,0:T(8,128)S(1)}, f32[150,128]{1,0:T(8,12...) custom-call(bf16[9,6,1152,256]{3,2,1,0:T(8,128)(2,1)S(1)} %get-tuple, ...), custom_call_target="tpu_custom_call", output_to_operand_aliasing={{0}: (0, {})} | custom-call | tf_op jit(solution)/shard_map/outer_and_first_flow/pallas_call | solution.py:652
  35.6 1.7 %collective-permute-start.6 = (f32[16,128]{1,0:T(8,128)S(1)}, f32[16,128]{1,0:T(8,128)S(1)}, u32[]{:S(2)}, u32[]{:S(2)}) collective-permute-start(f32[16,128]{1,0:T(8,128)S(1)} %get-tuple-element.70), channel_id=1, source_target_pairs={{0,24},{8,0},{16,8},{24,16},{1,25},{9,1},{17,9},{25,17},{2,26},{10... | collective-permute-start | bytes 24584 | tf_op jit(solution)/shard_map/ppermute | solution.py:181
  37.3 1.3 %collective-permute-done.5.before.x0.rest_2_ = f32[16,128]{1,0:T(8,128)S(1)} collective-permute-done((f32[16,128]{1,0:T(8,128)S(1)}, f32[16,128]{1,0:T(8,128)S(1)}, u32[]{:S(2)}, u32[]{:S(2)}) %collective-permute-start.5) | collective-permute-done | bytes 8224 | tf_op jit(solution)/shard_map/ppermute | solution.py:180
  39.0 3.6 %collective-permute-start.8 = (f32[24,128]{1,0:T(8,128)S(1)}, f32[24,128]{1,0:T(8,128)S(1)}, u32[]{:S(2)}, u32[]{:S(2)}) collective-permute-start(f32[24,128]{1,0:T(8,128)S(1)} %get-tuple-element.73), channel_id=1, source_target_pairs={{0,6},{2,0},{4,2},{6,4},{1,7},{3,1},{5,3},{7,5},{8,14},{10,8},{12,... | collective-permute-start | bytes 36872 | tf_op jit(solution)/shard_map/ppermute | solution.py:185
  42.6 1.7 %collective-permute-done.7.y0.rest_4_ = f32[24,128]{1,0:T(8,128)S(1)} collective-permute-done((f32[24,128]{1,0:T(8,128)S(1)}, f32[24,128]{1,0:T(8,128)S(1)}, u32[]{:S(2)}, u32[]{:S(2)}) %collective-permute-start.7) | collective-permute-done | bytes 12320 | tf_op jit(solution)/shard_map/ppermute | solution.py:184
  44.3 1.7 %collective-permute-start.9 = (f32[56,128]{1,0:T(8,128)S(1)}, f32[56,128]{1,0:T(8,128)S(1)}, u32[]{:S(2)}, u32[]{:S(2)}) collective-permute-start(f32[56,128]{1,0:T(8,128)S(1)} %get-tuple-element.75), channel_id=1, source_target_pairs={{0,1},{1,0},{2,3},{3,2},{4,5},{5,4},{6,7},{7,6},{8,9},{9,8},{10,11... | collective-permute-start | bytes 86024 | tf_op jit(solution)/shard_map/ppermute | solution.py:188
  46.0 2.2 %collective-permute-done.9.rest_6_ = f32[56,128]{1,0:T(8,128)S(1)} collective-permute-done((f32[56,128]{1,0:T(8,128)S(1)}, f32[56,128]{1,0:T(8,128)S(1)}, u32[]{:S(2)}, u32[]{:S(2)}) %collective-permute-start.9) | collective-permute-done | bytes 28704 | tf_op jit(solution)/shard_map/ppermute | solution.py:188
  48.3 4.9 %next_flow.1 = (f32[36,128]{1,0:T(8,128)S(1)}, f32[1,128]{1,0:T(1,128)S(1)}, f32[16,128]{1,0:T(8,128)S(1)}, f32[16,128]{1,0:T(8,128)S(1)}) custom-call(bf16[9,6,1152,256]{3,2,1,0:T(8,128)(2,1)S(1)} %get-tuple-element.62.kernel, f32[150,128]{1,0:T(8,128)S(1)} %get-tuple-element.63.volume, f32[150,128]{1,0:T(8,128)S(1)} %get-tuple-element.64.scaled, ...), custom_call_target="tpu_custom_call" | custom-call | tf_op jit(solution)/shard_map/next_flow/pallas_call | solution.py:656
  53.2 1.7 %collective-permute-start.11 = (f32[16,128]{1,0:T(8,128)S(1)}, f32[16,128]{1,0:T(8,128)S(1)}, u32[]{:S(2)}, u32[]{:S(2)}) collective-permute-start(f32[16,128]{1,0:T(8,128)S(1)} %get-tuple-element.79), channel_id=1, source_target_pairs={{0,24},{8,0},{16,8},{24,16},{1,25},{9,1},{17,9},{25,17},{2,26},{10... | collective-permute-start | bytes 24584 | tf_op jit(solution)/shard_map/ppermute | solution.py:181
  54.9 1.3 %collective-permute-done.10.before.x0.rest_4_ = f32[16,128]{1,0:T(8,128)S(1)} collective-permute-done((f32[16,128]{1,0:T(8,128)S(1)}, f32[16,128]{1,0:T(8,128)S(1)}, u32[]{:S(2)}, u32[]{:S(2)}) %collective-permute-start.10) | collective-permute-done | bytes 8224 | tf_op jit(solution)/shard_map/ppermute | solution.py:180
  56.4 3.9 %collective-permute-start.13 = (f32[24,128]{1,0:T(8,128)S(1)}, f32[24,128]{1,0:T(8,128)S(1)}, u32[]{:S(2)}, u32[]{:S(2)}) collective-permute-start(f32[24,128]{1,0:T(8,128)S(1)} %get-tuple-element.82), channel_id=1, source_target_pairs={{0,6},{2,0},{4,2},{6,4},{1,7},{3,1},{5,3},{7,5},{8,14},{10,8},{12,... | collective-permute-start | bytes 36872 | tf_op jit(solution)/shard_map/ppermute | solution.py:185
  60.2 1.6 %collective-permute-done.12.y0.rest_6_ = f32[24,128]{1,0:T(8,128)S(1)} collective-permute-done((f32[24,128]{1,0:T(8,128)S(1)}, f32[24,128]{1,0:T(8,128)S(1)}, u32[]{:S(2)}, u32[]{:S(2)}) %collective-permute-start.12) | collective-permute-done | bytes 12320 | tf_op jit(solution)/shard_map/ppermute | solution.py:184
  61.9 1.7 %collective-permute-start.14 = (f32[56,128]{1,0:T(8,128)S(1)}, f32[56,128]{1,0:T(8,128)S(1)}, u32[]{:S(2)}, u32[]{:S(2)}) collective-permute-start(f32[56,128]{1,0:T(8,128)S(1)} %get-tuple-element.84), channel_id=1, source_target_pairs={{0,1},{1,0},{2,3},{3,2},{4,5},{5,4},{6,7},{7,6},{8,9},{9,8},{10,11... | collective-permute-start | bytes 86024 | tf_op jit(solution)/shard_map/ppermute | solution.py:188
  63.6 2.4 %collective-permute-done.14.rest_8_ = f32[56,128]{1,0:T(8,128)S(1)} collective-permute-done((f32[56,128]{1,0:T(8,128)S(1)}, f32[56,128]{1,0:T(8,128)S(1)}, u32[]{:S(2)}, u32[]{:S(2)}) %collective-permute-start.14) | collective-permute-done | bytes 28704 | tf_op jit(solution)/shard_map/ppermute | solution.py:188
  66.0 5.5 %last_flow.1 = f32[3,3,4,128]{3,2,1,0:T(4,128)} custom-call(bf16[9,6,1152,256]{3,2,1,0:T(8,128)(2,1)S(1)} %get-tuple-element.62.kernel, f32[150,128]{1,0:T(8,128)S(1)} %get-tuple-element.63.volume, f32[150,128]{1,0:T(8,128)S(1)} %get-tuple-element.64.scaled, f32[36,128]{1,0:T(8,128)S(1)} %get-tuple-element.65.conduct_own, ...), custom_call_target="tpu_custom_call" | custom-call | tf_op jit(solution)/shard_map/last_flow/pallas_call | solution.py:658
  (19 shorter events, 1.3 us)
Async XLA Ops:
  0.9 6.1 %collective-permute-start = (f32[64,128]{1,0:T(8,128)S(1)}, f32[64,128]{1,0:T(8,128)S(1)}, u32[]{:S(2)}, u32[]{:S(2)}) collective-permute-start(f32[64,128]{1,0:T(8,128)S(1)} %get-tuple-element.51), channel_id=1, source_target_pairs={{0,8},{8,16},{16,24},{24,0},{1,9},{9,17},{17,25},{25,1},{2,10},{10... | collective-permute-start | bytes 98312 | tf_op jit(solution)/shard_map/ppermute | solution.py:180
  1.4 5.6 %collective-permute-start.1 = (f32[64,128]{1,0:T(8,128)S(1)}, f32[64,128]{1,0:T(8,128)S(1)}, u32[]{:S(2)}, u32[]{:S(2)}) collective-permute-start(f32[64,128]{1,0:T(8,128)S(1)} %get-tuple-element.52), channel_id=1, source_target_pairs={{0,24},{8,0},{16,8},{24,16},{1,25},{9,1},{17,9},{25,17},{2,26},{10... | collective-permute-start | bytes 98312 | tf_op jit(solution)/shard_map/ppermute | solution.py:181
  7.1 7.8 %collective-permute-start.2 = (f32[104,128]{1,0:T(8,128)S(1)}, f32[104,128]{1,0:T(8,128)S(1)}, u32[]{:S(2)}, u32[]{:S(2)}) collective-permute-start(f32[104,128]{1,0:T(8,128)S(1)} %get-tuple-element.56), channel_id=1, source_target_pairs={{0,2},{2,4},{4,6},{6,0},{1,3},{3,5},{5,7},{7,1},{8,10},{10,12},{12... | collective-permute-start | bytes 159752 | tf_op jit(solution)/shard_map/ppermute | solution.py:184
  9.5 5.4 %collective-permute-start.3 = (f32[104,128]{1,0:T(8,128)S(1)}, f32[104,128]{1,0:T(8,128)S(1)}, u32[]{:S(2)}, u32[]{:S(2)}) collective-permute-start(f32[104,128]{1,0:T(8,128)S(1)} %get-tuple-element.57), channel_id=1, source_target_pairs={{0,6},{2,0},{4,2},{6,4},{1,7},{3,1},{5,3},{7,5},{8,14},{10,8},{12,... | collective-permute-start | bytes 159752 | tf_op jit(solution)/shard_map/ppermute | solution.py:185
  15.1 5.1 %collective-permute-start.4 = (f32[256,128]{1,0:T(8,128)S(1)}, f32[256,128]{1,0:T(8,128)S(1)}, u32[]{:S(2)}, u32[]{:S(2)}) collective-permute-start(f32[256,128]{1,0:T(8,128)S(1)} %get-tuple-element.61), channel_id=1, source_target_pairs={{0,1},{1,0},{2,3},{3,2},{4,5},{5,4},{6,7},{7,6},{8,9},{9,8},{10,11... | collective-permute-start | bytes 393224 | tf_op jit(solution)/shard_map/ppermute | solution.py:188
  35.6 3.1 %collective-permute-start.5 = (f32[16,128]{1,0:T(8,128)S(1)}, f32[16,128]{1,0:T(8,128)S(1)}, u32[]{:S(2)}, u32[]{:S(2)}) collective-permute-start(f32[16,128]{1,0:T(8,128)S(1)} %get-tuple-element.69), channel_id=1, source_target_pairs={{0,8},{8,16},{16,24},{24,0},{1,9},{9,17},{17,25},{25,1},{2,10},{10... | collective-permute-start | bytes 24584 | tf_op jit(solution)/shard_map/ppermute | solution.py:180
  35.6 3.1 %collective-permute-start.6 = (f32[16,128]{1,0:T(8,128)S(1)}, f32[16,128]{1,0:T(8,128)S(1)}, u32[]{:S(2)}, u32[]{:S(2)}) collective-permute-start(f32[16,128]{1,0:T(8,128)S(1)} %get-tuple-element.70), channel_id=1, source_target_pairs={{0,24},{8,0},{16,8},{24,16},{1,25},{9,1},{17,9},{25,17},{2,26},{10... | collective-permute-start | bytes 24584 | tf_op jit(solution)/shard_map/ppermute | solution.py:181
  38.7 5.6 %collective-permute-start.7 = (f32[24,128]{1,0:T(8,128)S(1)}, f32[24,128]{1,0:T(8,128)S(1)}, u32[]{:S(2)}, u32[]{:S(2)}) collective-permute-start(f32[24,128]{1,0:T(8,128)S(1)} %get-tuple-element.72), channel_id=1, source_target_pairs={{0,2},{2,4},{4,6},{6,0},{1,3},{3,5},{5,7},{7,1},{8,10},{10,12},{12... | collective-permute-start | bytes 36872 | tf_op jit(solution)/shard_map/ppermute | solution.py:184
  39.0 5.3 %collective-permute-start.8 = (f32[24,128]{1,0:T(8,128)S(1)}, f32[24,128]{1,0:T(8,128)S(1)}, u32[]{:S(2)}, u32[]{:S(2)}) collective-permute-start(f32[24,128]{1,0:T(8,128)S(1)} %get-tuple-element.73), channel_id=1, source_target_pairs={{0,6},{2,0},{4,2},{6,4},{1,7},{3,1},{5,3},{7,5},{8,14},{10,8},{12,... | collective-permute-start | bytes 36872 | tf_op jit(solution)/shard_map/ppermute | solution.py:185
  44.3 3.9 %collective-permute-start.9 = (f32[56,128]{1,0:T(8,128)S(1)}, f32[56,128]{1,0:T(8,128)S(1)}, u32[]{:S(2)}, u32[]{:S(2)}) collective-permute-start(f32[56,128]{1,0:T(8,128)S(1)} %get-tuple-element.75), channel_id=1, source_target_pairs={{0,1},{1,0},{2,3},{3,2},{4,5},{5,4},{6,7},{7,6},{8,9},{9,8},{10,11... | collective-permute-start | bytes 86024 | tf_op jit(solution)/shard_map/ppermute | solution.py:188
  53.1 3.1 %collective-permute-start.10 = (f32[16,128]{1,0:T(8,128)S(1)}, f32[16,128]{1,0:T(8,128)S(1)}, u32[]{:S(2)}, u32[]{:S(2)}) collective-permute-start(f32[16,128]{1,0:T(8,128)S(1)} %get-tuple-element.78), channel_id=1, source_target_pairs={{0,8},{8,16},{16,24},{24,0},{1,9},{9,17},{17,25},{25,1},{2,10},{10... | collective-permute-start | bytes 24584 | tf_op jit(solution)/shard_map/ppermute | solution.py:180
  53.2 3.1 %collective-permute-start.11 = (f32[16,128]{1,0:T(8,128)S(1)}, f32[16,128]{1,0:T(8,128)S(1)}, u32[]{:S(2)}, u32[]{:S(2)}) collective-permute-start(f32[16,128]{1,0:T(8,128)S(1)} %get-tuple-element.79), channel_id=1, source_target_pairs={{0,24},{8,0},{16,8},{24,16},{1,25},{9,1},{17,9},{25,17},{2,26},{10... | collective-permute-start | bytes 24584 | tf_op jit(solution)/shard_map/ppermute | solution.py:181
  56.3 5.5 %collective-permute-start.12 = (f32[24,128]{1,0:T(8,128)S(1)}, f32[24,128]{1,0:T(8,128)S(1)}, u32[]{:S(2)}, u32[]{:S(2)}) collective-permute-start(f32[24,128]{1,0:T(8,128)S(1)} %get-tuple-element.81), channel_id=1, source_target_pairs={{0,2},{2,4},{4,6},{6,0},{1,3},{3,5},{5,7},{7,1},{8,10},{10,12},{12... | collective-permute-start | bytes 36872 | tf_op jit(solution)/shard_map/ppermute | solution.py:184
  56.4 5.5 %collective-permute-start.13 = (f32[24,128]{1,0:T(8,128)S(1)}, f32[24,128]{1,0:T(8,128)S(1)}, u32[]{:S(2)}, u32[]{:S(2)}) collective-permute-start(f32[24,128]{1,0:T(8,128)S(1)} %get-tuple-element.82), channel_id=1, source_target_pairs={{0,6},{2,0},{4,2},{6,4},{1,7},{3,1},{5,3},{7,5},{8,14},{10,8},{12,... | collective-permute-start | bytes 36872 | tf_op jit(solution)/shard_map/ppermute | solution.py:185
  61.9 4.1 %collective-permute-start.14 = (f32[56,128]{1,0:T(8,128)S(1)}, f32[56,128]{1,0:T(8,128)S(1)}, u32[]{:S(2)}, u32[]{:S(2)}) collective-permute-start(f32[56,128]{1,0:T(8,128)S(1)} %get-tuple-element.84), channel_id=1, source_target_pairs={{0,1},{1,0},{2,3},{3,2},{4,5},{5,4},{6,7},{7,6},{8,9},{9,8},{10,11... | collective-permute-start | bytes 86024 | tf_op jit(solution)/shard_map/ppermute | solution.py:188

commit v4 on v3

--- a/solution.py
+++ b/solution.py
@@ -426,7 +426,7 @@
                             pair_block(s, c, yz, cell, source_x - x, j, e, source, low, high, kernel)
             return carry
 
-        lax.fori_loop(begin, end, along_x, 0)
+        lax.fori_loop(begin, end, along_x, 0, unroll=True)
 
     def first(own, after, kernel, low, high, left, done, halves, targets):
         done[...] = after[...]
@@ -516,8 +516,8 @@
             apply_line(s, c, s.ny * s.half - 1, gains, kernel, sums)
             return carry
 
-        lax.fori_loop(0, combos_x(s), functools.partial(along_x, True), 0)
-        lax.fori_loop(combos_x(s), combos_x(s) + 2, functools.partial(along_x, False), 0)
+        lax.fori_loop(0, combos_x(s), functools.partial(along_x, True), 0, unroll=True)
+        lax.fori_loop(combos_x(s), combos_x(s) + 2, functools.partial(along_x, False), 0, unroll=2)
 
         flow, weight = flow_of(s, sums, conduct_own[...], temp_own[...])
         flow_out[...] = flow
@@ -636,7 +636,7 @@
     started = start_kernel(s)(*[pltpu.with_memory_space_constraint(a, pltpu.HBM) for a in arguments])
     made = []
     own_bytes = 4 * slots * rounded_up(FIELDS * s.cells)
-    parts = (0, 2 * combos_x(s) // 7, 5 * combos_x(s) // 7, combos_x(s))
+    parts = (0, combos_x(s) // 7, 4 * combos_x(s) // 7, combos_x(s))
 
     def during(phase, after):
         begin, end = parts[phase], parts[phase + 1]

time: 71.6 us -> 69 us (0.964)
  Pallas kernels: 36.1 us -> 33.8 us
    pallas_call x1, Pallas kernels: 15.4 us -> 13.3 us  [local(): outer_kernel(s, ROOM - own_bytes)(kernel, low, high, own, *messages)]
    pallas_call x1, Pallas kernels: 3.61 us -> 2.5 us  [during(): inner_kernel(s, ROOM - own_bytes - 4096, begin, end)(started[0], after)]
    pallas_call x2, Pallas kernels: 5.56 us -> 6.56 us  [during(): made[0], done = inner_kernel(s, ROOM, begin, end)(*made, after)]
  transfers between devices with their start and end apart: 15 -> 15, of which waited for: 7 -> 8; matrix products, arithmetic and copies ran while one was open for 0% -> 0% of each run, Pallas kernels for 13% -> 13%
where the time goes in v4:
time: 69 us; the launch traced here: 68.9 us
  Pallas kernels  33.8 us (49%)
  starting transfers between devices  23 us (33%)
  waiting for transfers between devices  11.7 us (17%)
    pallas_call x1, Pallas kernels, local(): outer_kernel(s, ROOM - own_bytes)(kernel, low, high, own, *messages)  13.3 us
    ppermute x3, starting transfers between devices, exchange(): y1 = lax.ppermute(down, 'gy', route('gy', -1))  8.85 us
    pallas_call x2, Pallas kernels, during(): made[0], done = inner_kernel(s, ROOM, begin, end)(*made, after)  6.56 us
    pallas_call x1, Pallas kernels, local(): next_kernel(s, ROOM, True)  5.48 us
    ppermute x3, starting transfers between devices, exchange(): x1 = lax.ppermute(down, 'gx', route('gx', -1))  5.44 us
    ppermute x3, waiting for transfers between devices, exchange(): lax.ppermute(m, 'gz', route('gz', d))  5.42 us
    pallas_call x1, Pallas kernels, local(): next_kernel(s, ROOM, False)(kernel, volume, scaled, conduct_own, *arrived)  4.86 us
    ppermute x3, starting transfers between devices, exchange(): lax.ppermute(m, 'gz', route('gz', d))  4.72 us
  transfers between devices with their start and end apart: 15, of which 8 were waited for; matrix products, arithmetic and copies ran while one was open for 0% of the time, Pallas kernels for 13%

profile of v4, /device:TPU:0, one launch (start us, length us, event | category | flops | bytes accessed | tf_op | source)
XLA Modules:
  0.0 68.9 jit_solution(8306808338922256937)
XLA Ops:
  0.0 0.9 %start.1 = (f32[180,128]{1,0:T(8,128)S(1)}, f32[1,128]{1,0:T(1,128)S(1)}, f32[64,128]{1,0:T(8,128)S(1)}, f32[64,128]{1,0:T(8,128)S(1)}) custom-call(s32[3,3,4]{2,1,0:T(4,128)} %counts_in.1, f32[3,3,3,4,128]{4,3,2,1,0:T(4,128)} %placements_in.1, f32[3,3,4,128]{3,2,1,0:T(4,128)} %mass_in.1, f32[3,3,4,128]{3,2,1,0:T(4,128)} %temp_in.1), custom_call_target="tpu_custom_call" | custom-call | tf_op jit(solution)/shard_map/start/pallas_call | solution.py:636
  1.4 2.0 %collective-permute-start.1 = (f32[64,128]{1,0:T(8,128)S(1)}, f32[64,128]{1,0:T(8,128)S(1)}, u32[]{:S(2)}, u32[]{:S(2)}) collective-permute-start(f32[64,128]{1,0:T(8,128)S(1)} %get-tuple-element.52), channel_id=1, source_target_pairs={{0,24},{8,0},{16,8},{24,16},{1,25},{9,1},{17,9},{25,17},{2,26},{10... | collective-permute-start | bytes 98312 | tf_op jit(solution)/shard_map/ppermute | solution.py:181
  3.4 2.5 %inner_first.1 = (bf16[9,6,1152,256]{3,2,1,0:T(8,128)(2,1)S(1)}, bf16[324,16,128]{2,1,0:T(8,128)(2,1)S(1)}, bf16[108,16,128]{2,1,0:T(8,128)(2,1)S(1)}, bf16[18,128,128]{2,1,0:T(8,128)(2,1)S(1)}, f32[1,128]{1,0:T(1,128)S(1)}) custom-call(f32[180,128]{1,0:T(8,128)S(1)} %get-tuple-element.45.own, f32[1,128]{1,0:T(1,128)S(1)} %get-tuple-element.46.after.top), custom_call_target="tpu_custom_call" | custom-call | tf_op jit(solution)/shard_map/inner_first/pallas_call | solution.py:644
  6.0 2.4 %collective-permute-start.2 = (f32[104,128]{1,0:T(8,128)S(1)}, f32[104,128]{1,0:T(8,128)S(1)}, u32[]{:S(2)}, u32[]{:S(2)}) collective-permute-start(f32[104,128]{1,0:T(8,128)S(1)} %get-tuple-element.56), channel_id=1, source_target_pairs={{0,2},{2,4},{4,6},{6,0},{1,3},{3,5},{5,7},{7,1},{8,10},{10,12},{12... | collective-permute-start | bytes 159752 | tf_op jit(solution)/shard_map/ppermute | solution.py:184
  8.4 2.1 %collective-permute-start.3 = (f32[104,128]{1,0:T(8,128)S(1)}, f32[104,128]{1,0:T(8,128)S(1)}, u32[]{:S(2)}, u32[]{:S(2)}) collective-permute-start(f32[104,128]{1,0:T(8,128)S(1)} %get-tuple-element.57), channel_id=1, source_target_pairs={{0,6},{2,0},{4,2},{6,4},{1,7},{3,1},{5,3},{7,5},{8,14},{10,8},{12,... | collective-permute-start | bytes 159752 | tf_op jit(solution)/shard_map/ppermute | solution.py:185
  10.5 3.1 %inner_second.2 = (bf16[9,6,1152,256]{3,2,1,0:T(8,128)(2,1)S(1)}, f32[1,128]{1,0:T(1,128)S(1)}) custom-call(bf16[9,6,1152,256]{3,2,1,0:T(8,128)(2,1)S(1)} %get-tuple-element.47.kernel_in, bf16[324,16,128]{2,1,0:T(8,128)(2,1)S(1)} %get-tuple-element.48.low, bf16[108,16,128]{2,1,0:T(8,128)(2,1)S(1)} %get-tuple-element.49.high, ...), custom_call_target="tpu_custom_call", output_to_operand_aliasing={{0}: (0, {})} | custom-call | tf_op jit(solution)/shard_map/inner_second/pallas_call | solution.py:647
  13.8 1.7 %collective-permute-start.4 = (f32[256,128]{1,0:T(8,128)S(1)}, f32[256,128]{1,0:T(8,128)S(1)}, u32[]{:S(2)}, u32[]{:S(2)}) collective-permute-start(f32[256,128]{1,0:T(8,128)S(1)} %get-tuple-element.61), channel_id=1, source_target_pairs={{0,1},{1,0},{2,3},{3,2},{4,5},{5,4},{6,7},{7,6},{8,9},{9,8},{10,11... | collective-permute-start | bytes 393224 | tf_op jit(solution)/shard_map/ppermute | solution.py:188
  15.4 3.5 %inner_second.3 = (bf16[9,6,1152,256]{3,2,1,0:T(8,128)(2,1)S(1)}, f32[1,128]{1,0:T(1,128)}) custom-call(bf16[9,6,1152,256]{3,2,1,0:T(8,128)(2,1)S(1)} %get-tuple-element.55.kernel_in, bf16[324,16,128]{2,1,0:T(8,128)(2,1)S(1)} %get-tuple-element.48.low, bf16[108,16,128]{2,1,0:T(8,128)(2,1)S(1)} %get-tuple-element.49.high, ...), custom_call_target="tpu_custom_call", output_to_operand_aliasing={{0}: (0, {})} | custom-call | tf_op jit(solution)/shard_map/inner_second/pallas_call | solution.py:647
  19.6 13.3 %outer_and_first_flow.1 = (bf16[9,6,1152,256]{3,2,1,0:T(8,128)(2,1)S(1)}, f32[36,128]{1,0:T(8,128)S(1)}, f32[150,128]{1,0:T(8,128)S(1)}, f32[150,128]{1,0:T(8,12...) custom-call(bf16[9,6,1152,256]{3,2,1,0:T(8,128)(2,1)S(1)} %get-tuple, ...), custom_call_target="tpu_custom_call", output_to_operand_aliasing={{0}: (0, {})} | custom-call | tf_op jit(solution)/shard_map/outer_and_first_flow/pallas_call | solution.py:652
  32.9 1.7 %collective-permute-start.6 = (f32[16,128]{1,0:T(8,128)S(1)}, f32[16,128]{1,0:T(8,128)S(1)}, u32[]{:S(2)}, u32[]{:S(2)}) collective-permute-start(f32[16,128]{1,0:T(8,128)S(1)} %get-tuple-element.70), channel_id=1, source_target_pairs={{0,24},{8,0},{16,8},{24,16},{1,25},{9,1},{17,9},{25,17},{2,26},{10... | collective-permute-start | bytes 24584 | tf_op jit(solution)/shard_map/ppermute | solution.py:181
  34.6 1.3 %collective-permute-done.5.before.x0.rest_2_ = f32[16,128]{1,0:T(8,128)S(1)} collective-permute-done((f32[16,128]{1,0:T(8,128)S(1)}, f32[16,128]{1,0:T(8,128)S(1)}, u32[]{:S(2)}, u32[]{:S(2)}) %collective-permute-start.5) | collective-permute-done | bytes 8224 | tf_op jit(solution)/shard_map/ppermute | solution.py:180
  36.0 0.9 %collective-permute-start.7 = (f32[24,128]{1,0:T(8,128)S(1)}, f32[24,128]{1,0:T(8,128)S(1)}, u32[]{:S(2)}, u32[]{:S(2)}) collective-permute-start(f32[24,128]{1,0:T(8,128)S(1)} %get-tuple-element.72), channel_id=1, source_target_pairs={{0,2},{2,4},{4,6},{6,0},{1,3},{3,5},{5,7},{7,1},{8,10},{10,12},{12... | collective-permute-start | bytes 36872 | tf_op jit(solution)/shard_map/ppermute | solution.py:184
  36.9 2.9 %collective-permute-start.8 = (f32[24,128]{1,0:T(8,128)S(1)}, f32[24,128]{1,0:T(8,128)S(1)}, u32[]{:S(2)}, u32[]{:S(2)}) collective-permute-start(f32[24,128]{1,0:T(8,128)S(1)} %get-tuple-element.73), channel_id=1, source_target_pairs={{0,6},{2,0},{4,2},{6,4},{1,7},{3,1},{5,3},{7,5},{8,14},{10,8},{12,... | collective-permute-start | bytes 36872 | tf_op jit(solution)/shard_map/ppermute | solution.py:185
  39.9 1.8 %collective-permute-done.7.y0.rest_4_ = f32[24,128]{1,0:T(8,128)S(1)} collective-permute-done((f32[24,128]{1,0:T(8,128)S(1)}, f32[24,128]{1,0:T(8,128)S(1)}, u32[]{:S(2)}, u32[]{:S(2)}) %collective-permute-start.7) | collective-permute-done | bytes 12320 | tf_op jit(solution)/shard_map/ppermute | solution.py:184
  41.7 1.5 %collective-permute-start.9 = (f32[56,128]{1,0:T(8,128)S(1)}, f32[56,128]{1,0:T(8,128)S(1)}, u32[]{:S(2)}, u32[]{:S(2)}) collective-permute-start(f32[56,128]{1,0:T(8,128)S(1)} %get-tuple-element.75), channel_id=1, source_target_pairs={{0,1},{1,0},{2,3},{3,2},{4,5},{5,4},{6,7},{7,6},{8,9},{9,8},{10,11... | collective-permute-start | bytes 86024 | tf_op jit(solution)/shard_map/ppermute | solution.py:188
  43.2 2.4 %collective-permute-done.9.rest_6_ = f32[56,128]{1,0:T(8,128)S(1)} collective-permute-done((f32[56,128]{1,0:T(8,128)S(1)}, f32[56,128]{1,0:T(8,128)S(1)}, u32[]{:S(2)}, u32[]{:S(2)}) %collective-permute-start.9) | collective-permute-done | bytes 28704 | tf_op jit(solution)/shard_map/ppermute | solution.py:188
  45.6 4.9 %next_flow.1 = (f32[36,128]{1,0:T(8,128)S(1)}, f32[1,128]{1,0:T(1,128)S(1)}, f32[16,128]{1,0:T(8,128)S(1)}, f32[16,128]{1,0:T(8,128)S(1)}) custom-call(bf16[9,6,1152,256]{3,2,1,0:T(8,128)(2,1)S(1)} %get-tuple-element.62.kernel, f32[150,128]{1,0:T(8,128)S(1)} %get-tuple-element.63.volume, f32[150,128]{1,0:T(8,128)S(1)} %get-tuple-element.64.scaled, ...), custom_call_target="tpu_custom_call" | custom-call | tf_op jit(solution)/shard_map/next_flow/pallas_call | solution.py:656
  50.6 1.7 %collective-permute-start.11 = (f32[16,128]{1,0:T(8,128)S(1)}, f32[16,128]{1,0:T(8,128)S(1)}, u32[]{:S(2)}, u32[]{:S(2)}) collective-permute-start(f32[16,128]{1,0:T(8,128)S(1)} %get-tuple-element.79), channel_id=1, source_target_pairs={{0,24},{8,0},{16,8},{24,16},{1,25},{9,1},{17,9},{25,17},{2,26},{10... | collective-permute-start | bytes 24584 | tf_op jit(solution)/shard_map/ppermute | solution.py:181
  52.3 1.3 %collective-permute-done.10.before.x0.rest_4_ = f32[16,128]{1,0:T(8,128)S(1)} collective-permute-done((f32[16,128]{1,0:T(8,128)S(1)}, f32[16,128]{1,0:T(8,128)S(1)}, u32[]{:S(2)}, u32[]{:S(2)}) %collective-permute-start.10) | collective-permute-done | bytes 8224 | tf_op jit(solution)/shard_map/ppermute | solution.py:180
  53.7 3.8 %collective-permute-start.13 = (f32[24,128]{1,0:T(8,128)S(1)}, f32[24,128]{1,0:T(8,128)S(1)}, u32[]{:S(2)}, u32[]{:S(2)}) collective-permute-start(f32[24,128]{1,0:T(8,128)S(1)} %get-tuple-element.82), channel_id=1, source_target_pairs={{0,6},{2,0},{4,2},{6,4},{1,7},{3,1},{5,3},{7,5},{8,14},{10,8},{12,... | collective-permute-start | bytes 36872 | tf_op jit(solution)/shard_map/ppermute | solution.py:185
  57.6 1.7 %collective-permute-done.12.y0.rest_6_ = f32[24,128]{1,0:T(8,128)S(1)} collective-permute-done((f32[24,128]{1,0:T(8,128)S(1)}, f32[24,128]{1,0:T(8,128)S(1)}, u32[]{:S(2)}, u32[]{:S(2)}) %collective-permute-start.12) | collective-permute-done | bytes 12320 | tf_op jit(solution)/shard_map/ppermute | solution.py:184
  59.3 1.5 %collective-permute-start.14 = (f32[56,128]{1,0:T(8,128)S(1)}, f32[56,128]{1,0:T(8,128)S(1)}, u32[]{:S(2)}, u32[]{:S(2)}) collective-permute-start(f32[56,128]{1,0:T(8,128)S(1)} %get-tuple-element.84), channel_id=1, source_target_pairs={{0,1},{1,0},{2,3},{3,2},{4,5},{5,4},{6,7},{7,6},{8,9},{9,8},{10,11... | collective-permute-start | bytes 86024 | tf_op jit(solution)/shard_map/ppermute | solution.py:188
  60.8 2.4 %collective-permute-done.14.rest_8_ = f32[56,128]{1,0:T(8,128)S(1)} collective-permute-done((f32[56,128]{1,0:T(8,128)S(1)}, f32[56,128]{1,0:T(8,128)S(1)}, u32[]{:S(2)}, u32[]{:S(2)}) %collective-permute-start.14) | collective-permute-done | bytes 28704 | tf_op jit(solution)/shard_map/ppermute | solution.py:188
  63.2 5.5 %last_flow.1 = f32[3,3,4,128]{3,2,1,0:T(4,128)} custom-call(bf16[9,6,1152,256]{3,2,1,0:T(8,128)(2,1)S(1)} %get-tuple-element.62.kernel, f32[150,128]{1,0:T(8,128)S(1)} %get-tuple-element.63.volume, f32[150,128]{1,0:T(8,128)S(1)} %get-tuple-element.64.scaled, f32[36,128]{1,0:T(8,128)S(1)} %get-tuple-element.65.conduct_own, ...), custom_call_target="tpu_custom_call" | custom-call | tf_op jit(solution)/shard_map/last_flow/pallas_call | solution.py:658
  (19 shorter events, 1.8 us)
Async XLA Ops:
  0.9 5.0 %collective-permute-start = (f32[64,128]{1,0:T(8,128)S(1)}, f32[64,128]{1,0:T(8,128)S(1)}, u32[]{:S(2)}, u32[]{:S(2)}) collective-permute-start(f32[64,128]{1,0:T(8,128)S(1)} %get-tuple-element.51), channel_id=1, source_target_pairs={{0,8},{8,16},{16,24},{24,0},{1,9},{9,17},{17,25},{25,1},{2,10},{10... | collective-permute-start | bytes 98312 | tf_op jit(solution)/shard_map/ppermute | solution.py:180
  1.4 4.5 %collective-permute-start.1 = (f32[64,128]{1,0:T(8,128)S(1)}, f32[64,128]{1,0:T(8,128)S(1)}, u32[]{:S(2)}, u32[]{:S(2)}) collective-permute-start(f32[64,128]{1,0:T(8,128)S(1)} %get-tuple-element.52), channel_id=1, source_target_pairs={{0,24},{8,0},{16,8},{24,16},{1,25},{9,1},{17,9},{25,17},{2,26},{10... | collective-permute-start | bytes 98312 | tf_op jit(solution)/shard_map/ppermute | solution.py:181
  6.0 7.5 %collective-permute-start.2 = (f32[104,128]{1,0:T(8,128)S(1)}, f32[104,128]{1,0:T(8,128)S(1)}, u32[]{:S(2)}, u32[]{:S(2)}) collective-permute-start(f32[104,128]{1,0:T(8,128)S(1)} %get-tuple-element.56), channel_id=1, source_target_pairs={{0,2},{2,4},{4,6},{6,0},{1,3},{3,5},{5,7},{7,1},{8,10},{10,12},{12... | collective-permute-start | bytes 159752 | tf_op jit(solution)/shard_map/ppermute | solution.py:184
  8.4 5.3 %collective-permute-start.3 = (f32[104,128]{1,0:T(8,128)S(1)}, f32[104,128]{1,0:T(8,128)S(1)}, u32[]{:S(2)}, u32[]{:S(2)}) collective-permute-start(f32[104,128]{1,0:T(8,128)S(1)} %get-tuple-element.57), channel_id=1, source_target_pairs={{0,6},{2,0},{4,2},{6,4},{1,7},{3,1},{5,3},{7,5},{8,14},{10,8},{12,... | collective-permute-start | bytes 159752 | tf_op jit(solution)/shard_map/ppermute | solution.py:185
  13.8 5.8 %collective-permute-start.4 = (f32[256,128]{1,0:T(8,128)S(1)}, f32[256,128]{1,0:T(8,128)S(1)}, u32[]{:S(2)}, u32[]{:S(2)}) collective-permute-start(f32[256,128]{1,0:T(8,128)S(1)} %get-tuple-element.61), channel_id=1, source_target_pairs={{0,1},{1,0},{2,3},{3,2},{4,5},{5,4},{6,7},{7,6},{8,9},{9,8},{10,11... | collective-permute-start | bytes 393224 | tf_op jit(solution)/shard_map/ppermute | solution.py:188
  32.8 3.1 %collective-permute-start.5 = (f32[16,128]{1,0:T(8,128)S(1)}, f32[16,128]{1,0:T(8,128)S(1)}, u32[]{:S(2)}, u32[]{:S(2)}) collective-permute-start(f32[16,128]{1,0:T(8,128)S(1)} %get-tuple-element.69), channel_id=1, source_target_pairs={{0,8},{8,16},{16,24},{24,0},{1,9},{9,17},{17,25},{25,1},{2,10},{10... | collective-permute-start | bytes 24584 | tf_op jit(solution)/shard_map/ppermute | solution.py:180
  32.9 3.1 %collective-permute-start.6 = (f32[16,128]{1,0:T(8,128)S(1)}, f32[16,128]{1,0:T(8,128)S(1)}, u32[]{:S(2)}, u32[]{:S(2)}) collective-permute-start(f32[16,128]{1,0:T(8,128)S(1)} %get-tuple-element.70), channel_id=1, source_target_pairs={{0,24},{8,0},{16,8},{24,16},{1,25},{9,1},{17,9},{25,17},{2,26},{10... | collective-permute-start | bytes 24584 | tf_op jit(solution)/shard_map/ppermute | solution.py:181
  36.0 5.7 %collective-permute-start.7 = (f32[24,128]{1,0:T(8,128)S(1)}, f32[24,128]{1,0:T(8,128)S(1)}, u32[]{:S(2)}, u32[]{:S(2)}) collective-permute-start(f32[24,128]{1,0:T(8,128)S(1)} %get-tuple-element.72), channel_id=1, source_target_pairs={{0,2},{2,4},{4,6},{6,0},{1,3},{3,5},{5,7},{7,1},{8,10},{10,12},{12... | collective-permute-start | bytes 36872 | tf_op jit(solution)/shard_map/ppermute | solution.py:184
  36.9 4.7 %collective-permute-start.8 = (f32[24,128]{1,0:T(8,128)S(1)}, f32[24,128]{1,0:T(8,128)S(1)}, u32[]{:S(2)}, u32[]{:S(2)}) collective-permute-start(f32[24,128]{1,0:T(8,128)S(1)} %get-tuple-element.73), channel_id=1, source_target_pairs={{0,6},{2,0},{4,2},{6,4},{1,7},{3,1},{5,3},{7,5},{8,14},{10,8},{12,... | collective-permute-start | bytes 36872 | tf_op jit(solution)/shard_map/ppermute | solution.py:185
  41.7 3.9 %collective-permute-start.9 = (f32[56,128]{1,0:T(8,128)S(1)}, f32[56,128]{1,0:T(8,128)S(1)}, u32[]{:S(2)}, u32[]{:S(2)}) collective-permute-start(f32[56,128]{1,0:T(8,128)S(1)} %get-tuple-element.75), channel_id=1, source_target_pairs={{0,1},{1,0},{2,3},{3,2},{4,5},{5,4},{6,7},{7,6},{8,9},{9,8},{10,11... | collective-permute-start | bytes 86024 | tf_op jit(solution)/shard_map/ppermute | solution.py:188
  50.5 3.1 %collective-permute-start.10 = (f32[16,128]{1,0:T(8,128)S(1)}, f32[16,128]{1,0:T(8,128)S(1)}, u32[]{:S(2)}, u32[]{:S(2)}) collective-permute-start(f32[16,128]{1,0:T(8,128)S(1)} %get-tuple-element.78), channel_id=1, source_target_pairs={{0,8},{8,16},{16,24},{24,0},{1,9},{9,17},{17,25},{25,1},{2,10},{10... | collective-permute-start | bytes 24584 | tf_op jit(solution)/shard_map/ppermute | solution.py:180
  50.6 3.1 %collective-permute-start.11 = (f32[16,128]{1,0:T(8,128)S(1)}, f32[16,128]{1,0:T(8,128)S(1)}, u32[]{:S(2)}, u32[]{:S(2)}) collective-permute-start(f32[16,128]{1,0:T(8,128)S(1)} %get-tuple-element.79), channel_id=1, source_target_pairs={{0,24},{8,0},{16,8},{24,16},{1,25},{9,1},{17,9},{25,17},{2,26},{10... | collective-permute-start | bytes 24584 | tf_op jit(solution)/shard_map/ppermute | solution.py:181
  53.7 5.5 %collective-permute-start.12 = (f32[24,128]{1,0:T(8,128)S(1)}, f32[24,128]{1,0:T(8,128)S(1)}, u32[]{:S(2)}, u32[]{:S(2)}) collective-permute-start(f32[24,128]{1,0:T(8,128)S(1)} %get-tuple-element.81), channel_id=1, source_target_pairs={{0,2},{2,4},{4,6},{6,0},{1,3},{3,5},{5,7},{7,1},{8,10},{10,12},{12... | collective-permute-start | bytes 36872 | tf_op jit(solution)/shard_map/ppermute | solution.py:184
  53.7 5.5 %collective-permute-start.13 = (f32[24,128]{1,0:T(8,128)S(1)}, f32[24,128]{1,0:T(8,128)S(1)}, u32[]{:S(2)}, u32[]{:S(2)}) collective-permute-start(f32[24,128]{1,0:T(8,128)S(1)} %get-tuple-element.82), channel_id=1, source_target_pairs={{0,6},{2,0},{4,2},{6,4},{1,7},{3,1},{5,3},{7,5},{8,14},{10,8},{12,... | collective-permute-start | bytes 36872 | tf_op jit(solution)/shard_map/ppermute | solution.py:185
  59.3 3.9 %collective-permute-start.14 = (f32[56,128]{1,0:T(8,128)S(1)}, f32[56,128]{1,0:T(8,128)S(1)}, u32[]{:S(2)}, u32[]{:S(2)}) collective-permute-start(f32[56,128]{1,0:T(8,128)S(1)} %get-tuple-element.84), channel_id=1, source_target_pairs={{0,1},{1,0},{2,3},{3,2},{4,5},{5,4},{6,7},{7,6},{8,9},{9,8},{10,11... | collective-permute-start | bytes 86024 | tf_op jit(solution)/shard_map/ppermute | solution.py:188

commit v5 on v4

--- a/solution.py
+++ b/solution.py
@@ -174,8 +174,9 @@
         )
 
     def exchange(self, own, top, up, down, during=None):
-        def beside(phase, top):
-            return () if during is None else (during(phase, top),)
+        def beside(phase, top, *messages):
+            done = None if during is None else during(phase, top, *messages)
+            return () if done is None else (done,)
 
         x0 = lax.ppermute(up, "gx", route("gx", 1))
         x1 = lax.ppermute(down, "gx", route("gx", -1))
@@ -186,7 +187,7 @@
         waits = beside(1, top)
         *messages, top = self.z_packer(len(waits))(own, top, x0, x1, y0, y1, *waits)
         z = [lax.ppermute(m, "gz", route("gz", d)) for m, d in zip(messages, (1, -1))]
-        beside(2, top)
+        beside(2, top, own, x0, x1, y0, y1)
         return (own, top, x0, x1, y0, y1, *z)
 
     def lay_out(self, halo, own, x0, x1, y0, y1, z):
@@ -302,13 +303,20 @@
     )
 
 
-def apply_line(s, c, yz, gains, kernel, sums):
+def apply_line(s, c, yz, gains, kernel, sums, chosen=None):
     x, source_x = line(s, c)
     y, zp = yz // s.half, yz % s.half
-    parts = [
-        gain_pair(gains, (source_x * s.py + y + j) * s.pz + 2 * zp + e) for j in range(3) for e in range(3)
-    ]
-    total = jnp.dot(jnp.concatenate(parts, axis=1), kernel[c, yz], preferred_element_type=jnp.float32)
+    blocks = [(j, e) for j in range(3) for e in range(3) if chosen is None or chosen(s, zp, e)]
+    if not blocks:
+        return
+    parts = [gain_pair(gains, (source_x * s.py + y + j) * s.pz + 2 * zp + e) for j, e in blocks]
+    if len(blocks) == 9:
+        right = kernel[c, yz]
+    else:
+        right = jnp.concatenate(
+            [kernel[c, yz, (j * 3 + e) * s.slots : (j * 3 + e + 1) * s.slots, :] for j, e in blocks], axis=0
+        )
+    total = jnp.dot(jnp.concatenate(parts, axis=1), right, preferred_element_type=jnp.float32)
     add_sums(s, total, 2 * (x * s.ny * s.half + yz), sums)
 
 
@@ -401,6 +409,10 @@
 
 def inner_z(s, zp, e):
     return 0 <= 2 * zp + e - 1 and 2 * zp + e < s.nz
+
+
+def outer_z(s, zp, e):
+    return not inner_z(s, zp, e)
 
 
 def combos_x(s):
@@ -552,12 +564,43 @@
     )
 
 
+def part_kernel(s, room):
+    slots = s.slots
+    faces = Faces(s, 1)
+
+    def body(kernel, volume, scaled, after, own, x0, x1, y0, y1, sums, temp, gains):
+        faces.put_own(temp, own)
+        faces.put_x(temp, x0, x1)
+        faces.put_y(temp, y0, y1)
+        none = jnp.zeros((1, slots), jnp.float32)
+        for column in range(s.columns):
+            for z in (0, s.pz - 1):
+                temp[column * s.pz + z : column * s.pz + z + 1, :] = none
+        source_rows(s, volume, scaled, temp, gains)
+        sums[...] = jnp.zeros_like(sums)
+
+        def along_x(c, carry):
+            for yz in range(s.ny * s.half):
+                apply_line(s, c, yz, gains, kernel, sums, inner_z)
+            return carry
+
+        lax.fori_loop(0, combos_x(s) + 2, along_x, 0, unroll=3)
+
+    return pl.pallas_call(
+        body,
+        out_shape=f32(s.cells * 8, slots),
+        scratch_shapes=[faces.halo_shape, pltpu.VMEM((s.padded, 8, slots), jnp.float32)],
+        compiler_params=pltpu.CompilerParams(vmem_limit_bytes=room),
+        name="part_flow",
+    )
+
+
 def next_kernel(s, room, last):
     slots = s.slots
     faces = Faces(s, 1)
     arrivals = len(faces.z_messages())
 
-    def body(kernel, volume, scaled, conduct_own, *rest):
+    def body(kernel, volume, scaled, conduct_own, part, *rest):
         if last:
             temp_own, flow1, *rest = rest
         own, top, x0, x1, y0, y1, *rest = rest
@@ -570,11 +613,11 @@
         most = faces.latest_top(top, z)
         source_rows(s, volume, scaled, temp, gains)
 
-        sums[...] = jnp.zeros_like(sums)
+        sums[...] = part[...]
 
         def along_x(c, carry):
             for yz in range(s.ny * s.half):
-                apply_line(s, c, yz, gains, kernel, sums)
+                apply_line(s, c, yz, gains, kernel, sums, outer_z)
             return carry
 
         lax.fori_loop(0, combos_x(s) + 2, along_x, 0, unroll=3)
@@ -638,7 +681,7 @@
     own_bytes = 4 * slots * rounded_up(FIELDS * s.cells)
     parts = (0, combos_x(s) // 7, 4 * combos_x(s) // 7, combos_x(s))
 
-    def during(phase, after):
+    def during(phase, after, *_):
         begin, end = parts[phase], parts[phase + 1]
         if phase == 0:
             *outs, done = inner_kernel(s, ROOM - own_bytes - 4096, begin, end)(started[0], after)
@@ -652,10 +695,18 @@
     kernel, flow1, volume, scaled, conduct_own, temp_own, top, up, down = outer_kernel(s, ROOM - own_bytes)(
         kernel, low, high, own, *messages
     )
-    arrived = faces.exchange(flow1, top, up, down)
-    flow2, top, up, down = next_kernel(s, ROOM, False)(kernel, volume, scaled, conduct_own, *arrived)
-    arrived = faces.exchange(flow2, top, up, down)
-    (final,) = next_kernel(s, ROOM, True)(kernel, volume, scaled, conduct_own, temp_own, flow1, *arrived)
+    sums = []
+
+    def apply_part(phase, after, *messages):
+        if phase == 2:
+            sums.append(part_kernel(s, ROOM)(kernel, volume, scaled, after, *messages))
+
+    arrived = faces.exchange(flow1, top, up, down, apply_part)
+    flow2, top, up, down = next_kernel(s, ROOM, False)(kernel, volume, scaled, conduct_own, sums[0], *arrived)
+    arrived = faces.exchange(flow2, top, up, down, apply_part)
+    (final,) = next_kernel(s, ROOM, True)(
+        kernel, volume, scaled, conduct_own, sums[1], temp_own, flow1, *arrived
+    )
     if not covered():
         top, flow3 = lax.optimization_barrier((arrived[1], final))
         step = step_factor / lax.pmax(jnp.max(top), AXES)

time: 69 us -> 64.6 us (0.936)
  waiting for transfers between devices: 11.7 us -> 6.92 us
  Pallas kernels: 33.8 us -> 35.1 us
  starting transfers between devices: 23 us -> 22.1 us
    ppermute x3, waiting for transfers between devices: 5.42 us -> 0.62 us  [exchange(): lax.ppermute(m, 'gz', route('gz', d))]
    pallas_call x1 -> x3, Pallas kernels: 4.86 us -> 8.93 us  [the longest x2 6.83 us: apply_part(): sums.append(part_kernel(s, ROOM)(kernel, volume, scaled, after, *messages))]
    pallas_call x1, Pallas kernels: 5.48 us -> 2.73 us  [local(): next_kernel(s, ROOM, True)]
    ppermute x3, starting transfers between devices: 4.72 us -> 3.81 us  [exchange(): lax.ppermute(m, 'gz', route('gz', d))]
  transfers between devices with their start and end apart: 15 -> 15, of which waited for: 8 -> 6; matrix products, arithmetic and copies ran while one was open for 0% -> 0% of each run, Pallas kernels for 13% -> 25%
where the time goes in v5:
time: 64.6 us; the launch traced here: 64.5 us
  Pallas kernels  35.1 us (54%)
  starting transfers between devices  22.1 us (34%)
  waiting for transfers between devices  6.92 us (11%)
    pallas_call x1, Pallas kernels, local(): outer_kernel(s, ROOM - own_bytes)(kernel, low, high, own, *messages)  13.3 us
    ppermute x3, starting transfers between devices, exchange(): y1 = lax.ppermute(down, 'gy', route('gy', -1))  8.85 us
    pallas_call x2, Pallas kernels, apply_part(): sums.append(part_kernel(s, ROOM)(kernel, volume, scaled, after, *messages))  6.83 us
    pallas_call x2, Pallas kernels, during(): made[0], done = inner_kernel(s, ROOM, begin, end)(*made, after)  6.56 us
    ppermute x3, starting transfers between devices, exchange(): x1 = lax.ppermute(down, 'gx', route('gx', -1))  5.44 us
    ppermute x3, starting transfers between devices, exchange(): lax.ppermute(m, 'gz', route('gz', d))  3.81 us
    ppermute x3, waiting for transfers between devices, exchange(): y0 = lax.ppermute(up, 'gy', route('gy', 1))  3.46 us
    ppermute x3, starting transfers between devices, exchange(): y0 = lax.ppermute(up, 'gy', route('gy', 1))  3.37 us
  transfers between devices with their start and end apart: 15, of which 6 were waited for; matrix products, arithmetic and copies ran while one was open for 0% of the time, Pallas kernels for 25%

profile of v5, /device:TPU:0, one launch (start us, length us, event | category | flops | bytes accessed | tf_op | source)
XLA Modules:
  0.0 64.5 jit_solution(16326002620056117654)
XLA Ops:
  0.0 0.9 %start.1 = (f32[180,128]{1,0:T(8,128)S(1)}, f32[1,128]{1,0:T(1,128)S(1)}, f32[64,128]{1,0:T(8,128)S(1)}, f32[64,128]{1,0:T(8,128)S(1)}) custom-call(s32[3,3,4]{2,1,0:T(4,128)} %counts_in.1, f32[3,3,3,4,128]{4,3,2,1,0:T(4,128)} %placements_in.1, f32[3,3,4,128]{3,2,1,0:T(4,128)} %mass_in.1, f32[3,3,4,128]{3,2,1,0:T(4,128)} %temp_in.1), custom_call_target="tpu_custom_call" | custom-call | tf_op jit(solution)/shard_map/start/pallas_call | solution.py:679
  1.4 2.0 %collective-permute-start.1 = (f32[64,128]{1,0:T(8,128)S(1)}, f32[64,128]{1,0:T(8,128)S(1)}, u32[]{:S(2)}, u32[]{:S(2)}) collective-permute-start(f32[64,128]{1,0:T(8,128)S(1)} %get-tuple-element.52), channel_id=1, source_target_pairs={{0,24},{8,0},{16,8},{24,16},{1,25},{9,1},{17,9},{25,17},{2,26},{10... | collective-permute-start | bytes 98312 | tf_op jit(solution)/shard_map/ppermute | solution.py:182
  3.4 2.5 %inner_first.1 = (bf16[9,6,1152,256]{3,2,1,0:T(8,128)(2,1)S(1)}, bf16[324,16,128]{2,1,0:T(8,128)(2,1)S(1)}, bf16[108,16,128]{2,1,0:T(8,128)(2,1)S(1)}, bf16[18,128,128]{2,1,0:T(8,128)(2,1)S(1)}, f32[1,128]{1,0:T(1,128)S(1)}) custom-call(f32[180,128]{1,0:T(8,128)S(1)} %get-tuple-element.45.own, f32[1,128]{1,0:T(1,128)S(1)} %get-tuple-element.46.after.top), custom_call_target="tpu_custom_call" | custom-call | tf_op jit(solution)/shard_map/inner_first/pallas_call | solution.py:687
  6.0 2.4 %collective-permute-start.2 = (f32[104,128]{1,0:T(8,128)S(1)}, f32[104,128]{1,0:T(8,128)S(1)}, u32[]{:S(2)}, u32[]{:S(2)}) collective-permute-start(f32[104,128]{1,0:T(8,128)S(1)} %get-tuple-element.56), channel_id=1, source_target_pairs={{0,2},{2,4},{4,6},{6,0},{1,3},{3,5},{5,7},{7,1},{8,10},{10,12},{12... | collective-permute-start | bytes 159752 | tf_op jit(solution)/shard_map/ppermute | solution.py:185
  8.4 2.1 %collective-permute-start.3 = (f32[104,128]{1,0:T(8,128)S(1)}, f32[104,128]{1,0:T(8,128)S(1)}, u32[]{:S(2)}, u32[]{:S(2)}) collective-permute-start(f32[104,128]{1,0:T(8,128)S(1)} %get-tuple-element.57), channel_id=1, source_target_pairs={{0,6},{2,0},{4,2},{6,4},{1,7},{3,1},{5,3},{7,5},{8,14},{10,8},{12,... | collective-permute-start | bytes 159752 | tf_op jit(solution)/shard_map/ppermute | solution.py:186
  10.5 3.1 %inner_second.2 = (bf16[9,6,1152,256]{3,2,1,0:T(8,128)(2,1)S(1)}, f32[1,128]{1,0:T(1,128)S(1)}) custom-call(bf16[9,6,1152,256]{3,2,1,0:T(8,128)(2,1)S(1)} %get-tuple-element.47.kernel_in, bf16[324,16,128]{2,1,0:T(8,128)(2,1)S(1)} %get-tuple-element.48.low, bf16[108,16,128]{2,1,0:T(8,128)(2,1)S(1)} %get-tuple-element.49.high, ...), custom_call_target="tpu_custom_call", output_to_operand_aliasing={{0}: (0, {})} | custom-call | tf_op jit(solution)/shard_map/inner_second/pallas_call | solution.py:690
  13.8 1.7 %collective-permute-start.4 = (f32[256,128]{1,0:T(8,128)S(1)}, f32[256,128]{1,0:T(8,128)S(1)}, u32[]{:S(2)}, u32[]{:S(2)}) collective-permute-start(f32[256,128]{1,0:T(8,128)S(1)} %get-tuple-element.61), channel_id=1, source_target_pairs={{0,1},{1,0},{2,3},{3,2},{4,5},{5,4},{6,7},{7,6},{8,9},{9,8},{10,11... | collective-permute-start | bytes 393224 | tf_op jit(solution)/shard_map/ppermute | solution.py:189
  15.4 3.5 %inner_second.3 = (bf16[9,6,1152,256]{3,2,1,0:T(8,128)(2,1)S(1)}, f32[1,128]{1,0:T(1,128)}) custom-call(bf16[9,6,1152,256]{3,2,1,0:T(8,128)(2,1)S(1)} %get-tuple-element.55.kernel_in, bf16[324,16,128]{2,1,0:T(8,128)(2,1)S(1)} %get-tuple-element.48.low, bf16[108,16,128]{2,1,0:T(8,128)(2,1)S(1)} %get-tuple-element.49.high, ...), custom_call_target="tpu_custom_call", output_to_operand_aliasing={{0}: (0, {})} | custom-call | tf_op jit(solution)/shard_map/inner_second/pallas_call | solution.py:690
  19.6 13.3 %outer_and_first_flow.1 = (bf16[9,6,1152,256]{3,2,1,0:T(8,128)(2,1)S(1)}, f32[36,128]{1,0:T(8,128)S(1)}, f32[150,128]{1,0:T(8,128)S(1)}, f32[150,128]{1,0:T(8,12...) custom-call(bf16[9,6,1152,256]{3,2,1,0:T(8,128)(2,1)S(1)} %get-tuple, ...), custom_call_target="tpu_custom_call", output_to_operand_aliasing={{0}: (0, {})} | custom-call | tf_op jit(solution)/shard_map/outer_and_first_flow/pallas_call | solution.py:695
  32.9 1.7 %collective-permute-start.6 = (f32[16,128]{1,0:T(8,128)S(1)}, f32[16,128]{1,0:T(8,128)S(1)}, u32[]{:S(2)}, u32[]{:S(2)}) collective-permute-start(f32[16,128]{1,0:T(8,128)S(1)} %get-tuple-element.69), channel_id=1, source_target_pairs={{0,24},{8,0},{16,8},{24,16},{1,25},{9,1},{17,9},{25,17},{2,26},{10... | collective-permute-start | bytes 24584 | tf_op jit(solution)/shard_map/ppermute | solution.py:182
  34.6 1.3 %collective-permute-done.5.before.x0.rest_2_ = f32[16,128]{1,0:T(8,128)S(1)} collective-permute-done((f32[16,128]{1,0:T(8,128)S(1)}, f32[16,128]{1,0:T(8,128)S(1)}, u32[]{:S(2)}, u32[]{:S(2)}) %collective-permute-start.5) | collective-permute-done | bytes 8224 | tf_op jit(solution)/shard_map/ppermute | solution.py:181
  36.0 0.9 %collective-permute-start.7 = (f32[24,128]{1,0:T(8,128)S(1)}, f32[24,128]{1,0:T(8,128)S(1)}, u32[]{:S(2)}, u32[]{:S(2)}) collective-permute-start(f32[24,128]{1,0:T(8,128)S(1)} %get-tuple-element.71), channel_id=1, source_target_pairs={{0,2},{2,4},{4,6},{6,0},{1,3},{3,5},{5,7},{7,1},{8,10},{10,12},{12... | collective-permute-start | bytes 36872 | tf_op jit(solution)/shard_map/ppermute | solution.py:185
  36.9 2.9 %collective-permute-start.8 = (f32[24,128]{1,0:T(8,128)S(1)}, f32[24,128]{1,0:T(8,128)S(1)}, u32[]{:S(2)}, u32[]{:S(2)}) collective-permute-start(f32[24,128]{1,0:T(8,128)S(1)} %get-tuple-element.72), channel_id=1, source_target_pairs={{0,6},{2,0},{4,2},{6,4},{1,7},{3,1},{5,3},{7,5},{8,14},{10,8},{12,... | collective-permute-start | bytes 36872 | tf_op jit(solution)/shard_map/ppermute | solution.py:186
  39.9 1.8 %collective-permute-done.7.y0.rest_4_ = f32[24,128]{1,0:T(8,128)S(1)} collective-permute-done((f32[24,128]{1,0:T(8,128)S(1)}, f32[24,128]{1,0:T(8,128)S(1)}, u32[]{:S(2)}, u32[]{:S(2)}) %collective-permute-start.7) | collective-permute-done | bytes 12320 | tf_op jit(solution)/shard_map/ppermute | solution.py:185
  41.7 1.5 %collective-permute-start.9 = (f32[56,128]{1,0:T(8,128)S(1)}, f32[56,128]{1,0:T(8,128)S(1)}, u32[]{:S(2)}, u32[]{:S(2)}) collective-permute-start(f32[56,128]{1,0:T(8,128)S(1)} %get-tuple-element.74), channel_id=1, source_target_pairs={{0,1},{1,0},{2,3},{3,2},{4,5},{5,4},{6,7},{7,6},{8,9},{9,8},{10,11... | collective-permute-start | bytes 86024 | tf_op jit(solution)/shard_map/ppermute | solution.py:189
  43.2 3.4 %part_flow.2.part = f32[288,128]{1,0:T(8,128)S(1)} custom-call(bf16[9,6,1152,256]{3,2,1,0:T(8,128)(2,1)S(1)} %get-tuple-element.62.kernel, f32[150,128]{1,0:T(8,128)S(1)} %get-tuple-element.63.volume, f32[150,128]{1,0:T(8,128)S(1)} %get-tuple-element.64.scaled, f32[1,128]{1,0:T(1,128)S(1)} %get-tuple-element.73.after.rest_1_, ...), custom_call_target="tpu_custom_call" | custom-call | tf_op jit(solution)/shard_map/part_flow/pallas_call | solution.py:702
  46.6 2.1 %next_flow.1 = (f32[36,128]{1,0:T(8,128)S(1)}, f32[1,128]{1,0:T(1,128)S(1)}, f32[16,128]{1,0:T(8,128)S(1)}, f32[16,128]{1,0:T(8,128)S(1)}) custom-call(bf16[9,6,1152,256]{3,2,1,0:T(8,128)(2,1)S(1)} %get-tuple-element.62.kernel, f32[150,128]{1,0:T(8,128)S(1)} %get-tuple-element.63.volume, f32[150,128]{1,0:T(8,128)S(1)} %get-tuple-element.64.scaled, ...), custom_call_target="tpu_custom_call" | custom-call | tf_op jit(solution)/shard_map/next_flow/pallas_call | solution.py:705
  48.8 1.7 %collective-permute-start.11 = (f32[16,128]{1,0:T(8,128)S(1)}, f32[16,128]{1,0:T(8,128)S(1)}, u32[]{:S(2)}, u32[]{:S(2)}) collective-permute-start(f32[16,128]{1,0:T(8,128)S(1)} %get-tuple-element.78), channel_id=1, source_target_pairs={{0,24},{8,0},{16,8},{24,16},{1,25},{9,1},{17,9},{25,17},{2,26},{10... | collective-permute-start | bytes 24584 | tf_op jit(solution)/shard_map/ppermute | solution.py:182
  50.5 1.3 %collective-permute-done.10.before.x0.rest_4_ = f32[16,128]{1,0:T(8,128)S(1)} collective-permute-done((f32[16,128]{1,0:T(8,128)S(1)}, f32[16,128]{1,0:T(8,128)S(1)}, u32[]{:S(2)}, u32[]{:S(2)}) %collective-permute-start.10) | collective-permute-done | bytes 8224 | tf_op jit(solution)/shard_map/ppermute | solution.py:181
  52.0 3.8 %collective-permute-start.13 = (f32[24,128]{1,0:T(8,128)S(1)}, f32[24,128]{1,0:T(8,128)S(1)}, u32[]{:S(2)}, u32[]{:S(2)}) collective-permute-start(f32[24,128]{1,0:T(8,128)S(1)} %get-tuple-element.81), channel_id=1, source_target_pairs={{0,6},{2,0},{4,2},{6,4},{1,7},{3,1},{5,3},{7,5},{8,14},{10,8},{12,... | collective-permute-start | bytes 36872 | tf_op jit(solution)/shard_map/ppermute | solution.py:186
  55.8 1.7 %collective-permute-done.12.y0.rest_6_ = f32[24,128]{1,0:T(8,128)S(1)} collective-permute-done((f32[24,128]{1,0:T(8,128)S(1)}, f32[24,128]{1,0:T(8,128)S(1)}, u32[]{:S(2)}, u32[]{:S(2)}) %collective-permute-start.12) | collective-permute-done | bytes 12320 | tf_op jit(solution)/shard_map/ppermute | solution.py:185
  57.5 0.6 collective-permute-start.14
  58.1 3.4 %part_flow.3.part = f32[288,128]{1,0:T(8,128)S(1)} custom-call(bf16[9,6,1152,256]{3,2,1,0:T(8,128)(2,1)S(1)} %get-tuple-element.62.kernel, f32[150,128]{1,0:T(8,128)S(1)} %get-tuple-element.63.volume, f32[150,128]{1,0:T(8,128)S(1)} %get-tuple-element.64.scaled, f32[1,128]{1,0:T(1,128)S(1)} %get-tuple-element.82.after.rest_3_, ...), custom_call_target="tpu_custom_call" | custom-call | tf_op jit(solution)/shard_map/part_flow/pallas_call | solution.py:702
  61.6 2.7 %last_flow.1 = f32[3,3,4,128]{3,2,1,0:T(4,128)} custom-call(bf16[9,6,1152,256]{3,2,1,0:T(8,128)(2,1)S(1)} %get-tuple-element.62.kernel, f32[150,128]{1,0:T(8,128)S(1)} %get-tuple-element.63.volume, f32[150,128]{1,0:T(8,128)S(1)} %get-tuple-element.64.scaled, f32[36,128]{1,0:T(8,128)S(1)} %get-tuple-element.65.conduct_own, f32[288,128]{1,0:T(8,128)S(1)} %part_flow.3.part, ...), custom_call_target="tpu_custom_call" | custom-call | tf_op jit(solution)/shard_map/last_flow/pallas_call | solution.py:707
  (21 shorter events, 1.8 us)
Async XLA Ops:
  0.9 5.0 %collective-permute-start = (f32[64,128]{1,0:T(8,128)S(1)}, f32[64,128]{1,0:T(8,128)S(1)}, u32[]{:S(2)}, u32[]{:S(2)}) collective-permute-start(f32[64,128]{1,0:T(8,128)S(1)} %get-tuple-element.51), channel_id=1, source_target_pairs={{0,8},{8,16},{16,24},{24,0},{1,9},{9,17},{17,25},{25,1},{2,10},{10... | collective-permute-start | bytes 98312 | tf_op jit(solution)/shard_map/ppermute | solution.py:181
  1.4 4.5 %collective-permute-start.1 = (f32[64,128]{1,0:T(8,128)S(1)}, f32[64,128]{1,0:T(8,128)S(1)}, u32[]{:S(2)}, u32[]{:S(2)}) collective-permute-start(f32[64,128]{1,0:T(8,128)S(1)} %get-tuple-element.52), channel_id=1, source_target_pairs={{0,24},{8,0},{16,8},{24,16},{1,25},{9,1},{17,9},{25,17},{2,26},{10... | collective-permute-start | bytes 98312 | tf_op jit(solution)/shard_map/ppermute | solution.py:182
  6.0 7.5 %collective-permute-start.2 = (f32[104,128]{1,0:T(8,128)S(1)}, f32[104,128]{1,0:T(8,128)S(1)}, u32[]{:S(2)}, u32[]{:S(2)}) collective-permute-start(f32[104,128]{1,0:T(8,128)S(1)} %get-tuple-element.56), channel_id=1, source_target_pairs={{0,2},{2,4},{4,6},{6,0},{1,3},{3,5},{5,7},{7,1},{8,10},{10,12},{12... | collective-permute-start | bytes 159752 | tf_op jit(solution)/shard_map/ppermute | solution.py:185
  8.4 5.3 %collective-permute-start.3 = (f32[104,128]{1,0:T(8,128)S(1)}, f32[104,128]{1,0:T(8,128)S(1)}, u32[]{:S(2)}, u32[]{:S(2)}) collective-permute-start(f32[104,128]{1,0:T(8,128)S(1)} %get-tuple-element.57), channel_id=1, source_target_pairs={{0,6},{2,0},{4,2},{6,4},{1,7},{3,1},{5,3},{7,5},{8,14},{10,8},{12,... | collective-permute-start | bytes 159752 | tf_op jit(solution)/shard_map/ppermute | solution.py:186
  13.8 5.8 %collective-permute-start.4 = (f32[256,128]{1,0:T(8,128)S(1)}, f32[256,128]{1,0:T(8,128)S(1)}, u32[]{:S(2)}, u32[]{:S(2)}) collective-permute-start(f32[256,128]{1,0:T(8,128)S(1)} %get-tuple-element.61), channel_id=1, source_target_pairs={{0,1},{1,0},{2,3},{3,2},{4,5},{5,4},{6,7},{7,6},{8,9},{9,8},{10,11... | collective-permute-start | bytes 393224 | tf_op jit(solution)/shard_map/ppermute | solution.py:189
  32.8 3.1 %collective-permute-start.5 = (f32[16,128]{1,0:T(8,128)S(1)}, f32[16,128]{1,0:T(8,128)S(1)}, u32[]{:S(2)}, u32[]{:S(2)}) collective-permute-start(f32[16,128]{1,0:T(8,128)S(1)} %get-tuple-element.68), channel_id=1, source_target_pairs={{0,8},{8,16},{16,24},{24,0},{1,9},{9,17},{17,25},{25,1},{2,10},{10... | collective-permute-start | bytes 24584 | tf_op jit(solution)/shard_map/ppermute | solution.py:181
  32.9 3.1 %collective-permute-start.6 = (f32[16,128]{1,0:T(8,128)S(1)}, f32[16,128]{1,0:T(8,128)S(1)}, u32[]{:S(2)}, u32[]{:S(2)}) collective-permute-start(f32[16,128]{1,0:T(8,128)S(1)} %get-tuple-element.69), channel_id=1, source_target_pairs={{0,24},{8,0},{16,8},{24,16},{1,25},{9,1},{17,9},{25,17},{2,26},{10... | collective-permute-start | bytes 24584 | tf_op jit(solution)/shard_map/ppermute | solution.py:182
  36.0 5.7 %collective-permute-start.7 = (f32[24,128]{1,0:T(8,128)S(1)}, f32[24,128]{1,0:T(8,128)S(1)}, u32[]{:S(2)}, u32[]{:S(2)}) collective-permute-start(f32[24,128]{1,0:T(8,128)S(1)} %get-tuple-element.71), channel_id=1, source_target_pairs={{0,2},{2,4},{4,6},{6,0},{1,3},{3,5},{5,7},{7,1},{8,10},{10,12},{12... | collective-permute-start | bytes 36872 | tf_op jit(solution)/shard_map/ppermute | solution.py:185
  36.9 4.7 %collective-permute-start.8 = (f32[24,128]{1,0:T(8,128)S(1)}, f32[24,128]{1,0:T(8,128)S(1)}, u32[]{:S(2)}, u32[]{:S(2)}) collective-permute-start(f32[24,128]{1,0:T(8,128)S(1)} %get-tuple-element.72), channel_id=1, source_target_pairs={{0,6},{2,0},{4,2},{6,4},{1,7},{3,1},{5,3},{7,5},{8,14},{10,8},{12,... | collective-permute-start | bytes 36872 | tf_op jit(solution)/shard_map/ppermute | solution.py:186
  41.7 4.9 %collective-permute-start.9 = (f32[56,128]{1,0:T(8,128)S(1)}, f32[56,128]{1,0:T(8,128)S(1)}, u32[]{:S(2)}, u32[]{:S(2)}) collective-permute-start(f32[56,128]{1,0:T(8,128)S(1)} %get-tuple-element.74), channel_id=1, source_target_pairs={{0,1},{1,0},{2,3},{3,2},{4,5},{5,4},{6,7},{7,6},{8,9},{9,8},{10,11... | collective-permute-start | bytes 86024 | tf_op jit(solution)/shard_map/ppermute | solution.py:189
  48.7 3.1 %collective-permute-start.10 = (f32[16,128]{1,0:T(8,128)S(1)}, f32[16,128]{1,0:T(8,128)S(1)}, u32[]{:S(2)}, u32[]{:S(2)}) collective-permute-start(f32[16,128]{1,0:T(8,128)S(1)} %get-tuple-element.77), channel_id=1, source_target_pairs={{0,8},{8,16},{16,24},{24,0},{1,9},{9,17},{17,25},{25,1},{2,10},{10... | collective-permute-start | bytes 24584 | tf_op jit(solution)/shard_map/ppermute | solution.py:181
  48.8 3.1 %collective-permute-start.11 = (f32[16,128]{1,0:T(8,128)S(1)}, f32[16,128]{1,0:T(8,128)S(1)}, u32[]{:S(2)}, u32[]{:S(2)}) collective-permute-start(f32[16,128]{1,0:T(8,128)S(1)} %get-tuple-element.78), channel_id=1, source_target_pairs={{0,24},{8,0},{16,8},{24,16},{1,25},{9,1},{17,9},{25,17},{2,26},{10... | collective-permute-start | bytes 24584 | tf_op jit(solution)/shard_map/ppermute | solution.py:182
  51.9 5.5 %collective-permute-start.12 = (f32[24,128]{1,0:T(8,128)S(1)}, f32[24,128]{1,0:T(8,128)S(1)}, u32[]{:S(2)}, u32[]{:S(2)}) collective-permute-start(f32[24,128]{1,0:T(8,128)S(1)} %get-tuple-element.80), channel_id=1, source_target_pairs={{0,2},{2,4},{4,6},{6,0},{1,3},{3,5},{5,7},{7,1},{8,10},{10,12},{12... | collective-permute-start | bytes 36872 | tf_op jit(solution)/shard_map/ppermute | solution.py:185
  52.0 5.5 %collective-permute-start.13 = (f32[24,128]{1,0:T(8,128)S(1)}, f32[24,128]{1,0:T(8,128)S(1)}, u32[]{:S(2)}, u32[]{:S(2)}) collective-permute-start(f32[24,128]{1,0:T(8,128)S(1)} %get-tuple-element.81), channel_id=1, source_target_pairs={{0,6},{2,0},{4,2},{6,4},{1,7},{3,1},{5,3},{7,5},{8,14},{10,8},{12,... | collective-permute-start | bytes 36872 | tf_op jit(solution)/shard_map/ppermute | solution.py:186
  57.5 4.0 %collective-permute-start.14 = (f32[56,128]{1,0:T(8,128)S(1)}, f32[56,128]{1,0:T(8,128)S(1)}, u32[]{:S(2)}, u32[]{:S(2)}) collective-permute-start(f32[56,128]{1,0:T(8,128)S(1)} %get-tuple-element.84), channel_id=1, source_target_pairs={{0,1},{1,0},{2,3},{3,2},{4,5},{5,4},{6,7},{7,6},{8,9},{9,8},{10,11... | collective-permute-start | bytes 86024 | tf_op jit(solution)/shard_map/ppermute | solution.py:189

commit v6 on v5

--- a/solution.py
+++ b/solution.py
@@ -584,7 +584,7 @@
                 apply_line(s, c, yz, gains, kernel, sums, inner_z)
             return carry
 
-        lax.fori_loop(0, combos_x(s) + 2, along_x, 0, unroll=3)
+        lax.fori_loop(0, combos_x(s) + 2, along_x, 0, unroll=True)
 
     return pl.pallas_call(
         body,
@@ -620,7 +620,7 @@
                 apply_line(s, c, yz, gains, kernel, sums, outer_z)
             return carry
 
-        lax.fori_loop(0, combos_x(s) + 2, along_x, 0, unroll=3)
+        lax.fori_loop(0, combos_x(s) + 2, along_x, 0, unroll=True)
         flow, _ = flow_of(s, sums, conduct_own[...], own[...])
         if last and covered():
             rows, block, arrived = rest

time: 64.6 us -> 63.6 us (0.985)
  Pallas kernels: 35.1 us -> 33.9 us
  transfers between devices with their start and end apart: 15 -> 15, of which waited for: 6 -> 6; matrix products, arithmetic and copies ran while one was open for 0% -> 0% of each run, Pallas kernels for 25% -> 24%
where the time goes in v6:
time: 63.6 us; the launch traced here: 63.4 us
  Pallas kernels  33.9 us (53%)
  starting transfers between devices  22.3 us (35%)
  waiting for transfers between devices  6.93 us (11%)
    pallas_call x1, Pallas kernels, local(): outer_kernel(s, ROOM - own_bytes)(kernel, low, high, own, *messages)  13.3 us
    ppermute x3, starting transfers between devices, exchange(): y1 = lax.ppermute(down, 'gy', route('gy', -1))  8.85 us
    pallas_call x2, Pallas kernels, during(): made[0], done = inner_kernel(s, ROOM, begin, end)(*made, after)  6.56 us
    pallas_call x2, Pallas kernels, apply_part(): sums.append(part_kernel(s, ROOM)(kernel, volume, scaled, after, *messages))  6.26 us
    ppermute x3, starting transfers between devices, exchange(): x1 = lax.ppermute(down, 'gx', route('gx', -1))  5.44 us
    ppermute x3, starting transfers between devices, exchange(): lax.ppermute(m, 'gz', route('gz', d))  3.98 us
    ppermute x3, waiting for transfers between devices, exchange(): y0 = lax.ppermute(up, 'gy', route('gy', 1))  3.46 us
    ppermute x3, starting transfers between devices, exchange(): y0 = lax.ppermute(up, 'gy', route('gy', 1))  3.37 us
  transfers between devices with their start and end apart: 15, of which 6 were waited for; matrix products, arithmetic and copies ran while one was open for 0% of the time, Pallas kernels for 24%

profile of v6, /device:TPU:0, one launch (start us, length us, event | category | flops | bytes accessed | tf_op | source)
XLA Modules:
  0.0 63.4 jit_solution(3734420288610853851)
XLA Ops:
  0.0 0.9 %start.1 = (f32[180,128]{1,0:T(8,128)S(1)}, f32[1,128]{1,0:T(1,128)S(1)}, f32[64,128]{1,0:T(8,128)S(1)}, f32[64,128]{1,0:T(8,128)S(1)}) custom-call(s32[3,3,4]{2,1,0:T(4,128)} %counts_in.1, f32[3,3,3,4,128]{4,3,2,1,0:T(4,128)} %placements_in.1, f32[3,3,4,128]{3,2,1,0:T(4,128)} %mass_in.1, f32[3,3,4,128]{3,2,1,0:T(4,128)} %temp_in.1), custom_call_target="tpu_custom_call" | custom-call | tf_op jit(solution)/shard_map/start/pallas_call | solution.py:679
  1.4 2.0 %collective-permute-start.1 = (f32[64,128]{1,0:T(8,128)S(1)}, f32[64,128]{1,0:T(8,128)S(1)}, u32[]{:S(2)}, u32[]{:S(2)}) collective-permute-start(f32[64,128]{1,0:T(8,128)S(1)} %get-tuple-element.52), channel_id=1, source_target_pairs={{0,24},{8,0},{16,8},{24,16},{1,25},{9,1},{17,9},{25,17},{2,26},{10... | collective-permute-start | bytes 98312 | tf_op jit(solution)/shard_map/ppermute | solution.py:182
  3.4 2.5 %inner_first.1 = (bf16[9,6,1152,256]{3,2,1,0:T(8,128)(2,1)S(1)}, bf16[324,16,128]{2,1,0:T(8,128)(2,1)S(1)}, bf16[108,16,128]{2,1,0:T(8,128)(2,1)S(1)}, bf16[18,128,128]{2,1,0:T(8,128)(2,1)S(1)}, f32[1,128]{1,0:T(1,128)S(1)}) custom-call(f32[180,128]{1,0:T(8,128)S(1)} %get-tuple-element.45.own, f32[1,128]{1,0:T(1,128)S(1)} %get-tuple-element.46.after.top), custom_call_target="tpu_custom_call" | custom-call | tf_op jit(solution)/shard_map/inner_first/pallas_call | solution.py:687
  6.0 2.4 %collective-permute-start.2 = (f32[104,128]{1,0:T(8,128)S(1)}, f32[104,128]{1,0:T(8,128)S(1)}, u32[]{:S(2)}, u32[]{:S(2)}) collective-permute-start(f32[104,128]{1,0:T(8,128)S(1)} %get-tuple-element.56), channel_id=1, source_target_pairs={{0,2},{2,4},{4,6},{6,0},{1,3},{3,5},{5,7},{7,1},{8,10},{10,12},{12... | collective-permute-start | bytes 159752 | tf_op jit(solution)/shard_map/ppermute | solution.py:185
  8.4 2.1 %collective-permute-start.3 = (f32[104,128]{1,0:T(8,128)S(1)}, f32[104,128]{1,0:T(8,128)S(1)}, u32[]{:S(2)}, u32[]{:S(2)}) collective-permute-start(f32[104,128]{1,0:T(8,128)S(1)} %get-tuple-element.57), channel_id=1, source_target_pairs={{0,6},{2,0},{4,2},{6,4},{1,7},{3,1},{5,3},{7,5},{8,14},{10,8},{12,... | collective-permute-start | bytes 159752 | tf_op jit(solution)/shard_map/ppermute | solution.py:186
  10.5 3.1 %inner_second.2 = (bf16[9,6,1152,256]{3,2,1,0:T(8,128)(2,1)S(1)}, f32[1,128]{1,0:T(1,128)S(1)}) custom-call(bf16[9,6,1152,256]{3,2,1,0:T(8,128)(2,1)S(1)} %get-tuple-element.47.kernel_in, bf16[324,16,128]{2,1,0:T(8,128)(2,1)S(1)} %get-tuple-element.48.low, bf16[108,16,128]{2,1,0:T(8,128)(2,1)S(1)} %get-tuple-element.49.high, ...), custom_call_target="tpu_custom_call", output_to_operand_aliasing={{0}: (0, {})} | custom-call | tf_op jit(solution)/shard_map/inner_second/pallas_call | solution.py:690
  13.8 1.7 %collective-permute-start.4 = (f32[256,128]{1,0:T(8,128)S(1)}, f32[256,128]{1,0:T(8,128)S(1)}, u32[]{:S(2)}, u32[]{:S(2)}) collective-permute-start(f32[256,128]{1,0:T(8,128)S(1)} %get-tuple-element.61), channel_id=1, source_target_pairs={{0,1},{1,0},{2,3},{3,2},{4,5},{5,4},{6,7},{7,6},{8,9},{9,8},{10,11... | collective-permute-start | bytes 393224 | tf_op jit(solution)/shard_map/ppermute | solution.py:189
  15.4 3.5 %inner_second.3 = (bf16[9,6,1152,256]{3,2,1,0:T(8,128)(2,1)S(1)}, f32[1,128]{1,0:T(1,128)}) custom-call(bf16[9,6,1152,256]{3,2,1,0:T(8,128)(2,1)S(1)} %get-tuple-element.55.kernel_in, bf16[324,16,128]{2,1,0:T(8,128)(2,1)S(1)} %get-tuple-element.48.low, bf16[108,16,128]{2,1,0:T(8,128)(2,1)S(1)} %get-tuple-element.49.high, ...), custom_call_target="tpu_custom_call", output_to_operand_aliasing={{0}: (0, {})} | custom-call | tf_op jit(solution)/shard_map/inner_second/pallas_call | solution.py:690
  19.6 13.3 %outer_and_first_flow.1 = (bf16[9,6,1152,256]{3,2,1,0:T(8,128)(2,1)S(1)}, f32[36,128]{1,0:T(8,128)S(1)}, f32[150,128]{1,0:T(8,128)S(1)}, f32[150,128]{1,0:T(8,12...) custom-call(bf16[9,6,1152,256]{3,2,1,0:T(8,128)(2,1)S(1)} %get-tuple, ...), custom_call_target="tpu_custom_call", output_to_operand_aliasing={{0}: (0, {})} | custom-call | tf_op jit(solution)/shard_map/outer_and_first_flow/pallas_call | solution.py:695
  32.9 1.7 %collective-permute-start.6 = (f32[16,128]{1,0:T(8,128)S(1)}, f32[16,128]{1,0:T(8,128)S(1)}, u32[]{:S(2)}, u32[]{:S(2)}) collective-permute-start(f32[16,128]{1,0:T(8,128)S(1)} %get-tuple-element.69), channel_id=1, source_target_pairs={{0,24},{8,0},{16,8},{24,16},{1,25},{9,1},{17,9},{25,17},{2,26},{10... | collective-permute-start | bytes 24584 | tf_op jit(solution)/shard_map/ppermute | solution.py:182
  34.6 1.3 %collective-permute-done.5.before.x0.rest_2_ = f32[16,128]{1,0:T(8,128)S(1)} collective-permute-done((f32[16,128]{1,0:T(8,128)S(1)}, f32[16,128]{1,0:T(8,128)S(1)}, u32[]{:S(2)}, u32[]{:S(2)}) %collective-permute-start.5) | collective-permute-done | bytes 8224 | tf_op jit(solution)/shard_map/ppermute | solution.py:181
  36.0 0.9 %collective-permute-start.7 = (f32[24,128]{1,0:T(8,128)S(1)}, f32[24,128]{1,0:T(8,128)S(1)}, u32[]{:S(2)}, u32[]{:S(2)}) collective-permute-start(f32[24,128]{1,0:T(8,128)S(1)} %get-tuple-element.71), channel_id=1, source_target_pairs={{0,2},{2,4},{4,6},{6,0},{1,3},{3,5},{5,7},{7,1},{8,10},{10,12},{12... | collective-permute-start | bytes 36872 | tf_op jit(solution)/shard_map/ppermute | solution.py:185
  36.9 2.9 %collective-permute-start.8 = (f32[24,128]{1,0:T(8,128)S(1)}, f32[24,128]{1,0:T(8,128)S(1)}, u32[]{:S(2)}, u32[]{:S(2)}) collective-permute-start(f32[24,128]{1,0:T(8,128)S(1)} %get-tuple-element.72), channel_id=1, source_target_pairs={{0,6},{2,0},{4,2},{6,4},{1,7},{3,1},{5,3},{7,5},{8,14},{10,8},{12,... | collective-permute-start | bytes 36872 | tf_op jit(solution)/shard_map/ppermute | solution.py:186
  39.9 1.8 %collective-permute-done.7.y0.rest_4_ = f32[24,128]{1,0:T(8,128)S(1)} collective-permute-done((f32[24,128]{1,0:T(8,128)S(1)}, f32[24,128]{1,0:T(8,128)S(1)}, u32[]{:S(2)}, u32[]{:S(2)}) %collective-permute-start.7) | collective-permute-done | bytes 12320 | tf_op jit(solution)/shard_map/ppermute | solution.py:185
  41.7 1.5 %collective-permute-start.9 = (f32[56,128]{1,0:T(8,128)S(1)}, f32[56,128]{1,0:T(8,128)S(1)}, u32[]{:S(2)}, u32[]{:S(2)}) collective-permute-start(f32[56,128]{1,0:T(8,128)S(1)} %get-tuple-element.74), channel_id=1, source_target_pairs={{0,1},{1,0},{2,3},{3,2},{4,5},{5,4},{6,7},{7,6},{8,9},{9,8},{10,11... | collective-permute-start | bytes 86024 | tf_op jit(solution)/shard_map/ppermute | solution.py:189
  43.2 3.1 %part_flow.2.part = f32[288,128]{1,0:T(8,128)S(1)} custom-call(bf16[9,6,1152,256]{3,2,1,0:T(8,128)(2,1)S(1)} %get-tuple-element.62.kernel, f32[150,128]{1,0:T(8,128)S(1)} %get-tuple-element.63.volume, f32[150,128]{1,0:T(8,128)S(1)} %get-tuple-element.64.scaled, f32[1,128]{1,0:T(1,128)S(1)} %get-tuple-element.73.after.rest_1_, ...), custom_call_target="tpu_custom_call" | custom-call | tf_op jit(solution)/shard_map/part_flow/pallas_call | solution.py:702
  46.4 1.8 %next_flow.1 = (f32[36,128]{1,0:T(8,128)S(1)}, f32[1,128]{1,0:T(1,128)S(1)}, f32[16,128]{1,0:T(8,128)S(1)}, f32[16,128]{1,0:T(8,128)S(1)}) custom-call(bf16[9,6,1152,256]{3,2,1,0:T(8,128)(2,1)S(1)} %get-tuple-element.62.kernel, f32[150,128]{1,0:T(8,128)S(1)} %get-tuple-element.63.volume, f32[150,128]{1,0:T(8,128)S(1)} %get-tuple-element.64.scaled, ...), custom_call_target="tpu_custom_call" | custom-call | tf_op jit(solution)/shard_map/next_flow/pallas_call | solution.py:705
  48.2 1.7 %collective-permute-start.11 = (f32[16,128]{1,0:T(8,128)S(1)}, f32[16,128]{1,0:T(8,128)S(1)}, u32[]{:S(2)}, u32[]{:S(2)}) collective-permute-start(f32[16,128]{1,0:T(8,128)S(1)} %get-tuple-element.78), channel_id=1, source_target_pairs={{0,24},{8,0},{16,8},{24,16},{1,25},{9,1},{17,9},{25,17},{2,26},{10... | collective-permute-start | bytes 24584 | tf_op jit(solution)/shard_map/ppermute | solution.py:182
  49.9 1.3 %collective-permute-done.10.before.x0.rest_4_ = f32[16,128]{1,0:T(8,128)S(1)} collective-permute-done((f32[16,128]{1,0:T(8,128)S(1)}, f32[16,128]{1,0:T(8,128)S(1)}, u32[]{:S(2)}, u32[]{:S(2)}) %collective-permute-start.10) | collective-permute-done | bytes 8224 | tf_op jit(solution)/shard_map/ppermute | solution.py:181
  51.4 3.8 %collective-permute-start.13 = (f32[24,128]{1,0:T(8,128)S(1)}, f32[24,128]{1,0:T(8,128)S(1)}, u32[]{:S(2)}, u32[]{:S(2)}) collective-permute-start(f32[24,128]{1,0:T(8,128)S(1)} %get-tuple-element.81), channel_id=1, source_target_pairs={{0,6},{2,0},{4,2},{6,4},{1,7},{3,1},{5,3},{7,5},{8,14},{10,8},{12,... | collective-permute-start | bytes 36872 | tf_op jit(solution)/shard_map/ppermute | solution.py:186
  55.2 1.7 %collective-permute-done.12.y0.rest_6_ = f32[24,128]{1,0:T(8,128)S(1)} collective-permute-done((f32[24,128]{1,0:T(8,128)S(1)}, f32[24,128]{1,0:T(8,128)S(1)}, u32[]{:S(2)}, u32[]{:S(2)}) %collective-permute-start.12) | collective-permute-done | bytes 12320 | tf_op jit(solution)/shard_map/ppermute | solution.py:185
  56.9 0.8 %collective-permute-start.14 = (f32[56,128]{1,0:T(8,128)S(1)}, f32[56,128]{1,0:T(8,128)S(1)}, u32[]{:S(2)}, u32[]{:S(2)}) collective-permute-start(f32[56,128]{1,0:T(8,128)S(1)} %get-tuple-element.84), channel_id=1, source_target_pairs={{0,1},{1,0},{2,3},{3,2},{4,5},{5,4},{6,7},{7,6},{8,9},{9,8},{10,11... | collective-permute-start | bytes 86024 | tf_op jit(solution)/shard_map/ppermute | solution.py:189
  57.7 3.1 %part_flow.3.part = f32[288,128]{1,0:T(8,128)S(1)} custom-call(bf16[9,6,1152,256]{3,2,1,0:T(8,128)(2,1)S(1)} %get-tuple-element.62.kernel, f32[150,128]{1,0:T(8,128)S(1)} %get-tuple-element.63.volume, f32[150,128]{1,0:T(8,128)S(1)} %get-tuple-element.64.scaled, f32[1,128]{1,0:T(1,128)S(1)} %get-tuple-element.82.after.rest_3_, ...), custom_call_target="tpu_custom_call" | custom-call | tf_op jit(solution)/shard_map/part_flow/pallas_call | solution.py:702
  60.8 2.4 %last_flow.1 = f32[3,3,4,128]{3,2,1,0:T(4,128)} custom-call(bf16[9,6,1152,256]{3,2,1,0:T(8,128)(2,1)S(1)} %get-tuple-element.62.kernel, f32[150,128]{1,0:T(8,128)S(1)} %get-tuple-element.63.volume, f32[150,128]{1,0:T(8,128)S(1)} %get-tuple-element.64.scaled, f32[36,128]{1,0:T(8,128)S(1)} %get-tuple-element.65.conduct_own, f32[288,128]{1,0:T(8,128)S(1)} %part_flow.3.part, ...), custom_call_target="tpu_custom_call" | custom-call | tf_op jit(solution)/shard_map/last_flow/pallas_call | solution.py:707
  (21 shorter events, 1.8 us)
Async XLA Ops:
  0.9 5.0 %collective-permute-start = (f32[64,128]{1,0:T(8,128)S(1)}, f32[64,128]{1,0:T(8,128)S(1)}, u32[]{:S(2)}, u32[]{:S(2)}) collective-permute-start(f32[64,128]{1,0:T(8,128)S(1)} %get-tuple-element.51), channel_id=1, source_target_pairs={{0,8},{8,16},{16,24},{24,0},{1,9},{9,17},{17,25},{25,1},{2,10},{10... | collective-permute-start | bytes 98312 | tf_op jit(solution)/shard_map/ppermute | solution.py:181
  1.4 4.5 %collective-permute-start.1 = (f32[64,128]{1,0:T(8,128)S(1)}, f32[64,128]{1,0:T(8,128)S(1)}, u32[]{:S(2)}, u32[]{:S(2)}) collective-permute-start(f32[64,128]{1,0:T(8,128)S(1)} %get-tuple-element.52), channel_id=1, source_target_pairs={{0,24},{8,0},{16,8},{24,16},{1,25},{9,1},{17,9},{25,17},{2,26},{10... | collective-permute-start | bytes 98312 | tf_op jit(solution)/shard_map/ppermute | solution.py:182
  6.0 7.5 %collective-permute-start.2 = (f32[104,128]{1,0:T(8,128)S(1)}, f32[104,128]{1,0:T(8,128)S(1)}, u32[]{:S(2)}, u32[]{:S(2)}) collective-permute-start(f32[104,128]{1,0:T(8,128)S(1)} %get-tuple-element.56), channel_id=1, source_target_pairs={{0,2},{2,4},{4,6},{6,0},{1,3},{3,5},{5,7},{7,1},{8,10},{10,12},{12... | collective-permute-start | bytes 159752 | tf_op jit(solution)/shard_map/ppermute | solution.py:185
  8.4 5.3 %collective-permute-start.3 = (f32[104,128]{1,0:T(8,128)S(1)}, f32[104,128]{1,0:T(8,128)S(1)}, u32[]{:S(2)}, u32[]{:S(2)}) collective-permute-start(f32[104,128]{1,0:T(8,128)S(1)} %get-tuple-element.57), channel_id=1, source_target_pairs={{0,6},{2,0},{4,2},{6,4},{1,7},{3,1},{5,3},{7,5},{8,14},{10,8},{12,... | collective-permute-start | bytes 159752 | tf_op jit(solution)/shard_map/ppermute | solution.py:186
  13.8 5.8 %collective-permute-start.4 = (f32[256,128]{1,0:T(8,128)S(1)}, f32[256,128]{1,0:T(8,128)S(1)}, u32[]{:S(2)}, u32[]{:S(2)}) collective-permute-start(f32[256,128]{1,0:T(8,128)S(1)} %get-tuple-element.61), channel_id=1, source_target_pairs={{0,1},{1,0},{2,3},{3,2},{4,5},{5,4},{6,7},{7,6},{8,9},{9,8},{10,11... | collective-permute-start | bytes 393224 | tf_op jit(solution)/shard_map/ppermute | solution.py:189
  32.8 3.1 %collective-permute-start.5 = (f32[16,128]{1,0:T(8,128)S(1)}, f32[16,128]{1,0:T(8,128)S(1)}, u32[]{:S(2)}, u32[]{:S(2)}) collective-permute-start(f32[16,128]{1,0:T(8,128)S(1)} %get-tuple-element.68), channel_id=1, source_target_pairs={{0,8},{8,16},{16,24},{24,0},{1,9},{9,17},{17,25},{25,1},{2,10},{10... | collective-permute-start | bytes 24584 | tf_op jit(solution)/shard_map/ppermute | solution.py:181
  32.9 3.1 %collective-permute-start.6 = (f32[16,128]{1,0:T(8,128)S(1)}, f32[16,128]{1,0:T(8,128)S(1)}, u32[]{:S(2)}, u32[]{:S(2)}) collective-permute-start(f32[16,128]{1,0:T(8,128)S(1)} %get-tuple-element.69), channel_id=1, source_target_pairs={{0,24},{8,0},{16,8},{24,16},{1,25},{9,1},{17,9},{25,17},{2,26},{10... | collective-permute-start | bytes 24584 | tf_op jit(solution)/shard_map/ppermute | solution.py:182
  36.0 5.7 %collective-permute-start.7 = (f32[24,128]{1,0:T(8,128)S(1)}, f32[24,128]{1,0:T(8,128)S(1)}, u32[]{:S(2)}, u32[]{:S(2)}) collective-permute-start(f32[24,128]{1,0:T(8,128)S(1)} %get-tuple-element.71), channel_id=1, source_target_pairs={{0,2},{2,4},{4,6},{6,0},{1,3},{3,5},{5,7},{7,1},{8,10},{10,12},{12... | collective-permute-start | bytes 36872 | tf_op jit(solution)/shard_map/ppermute | solution.py:185
  36.9 4.7 %collective-permute-start.8 = (f32[24,128]{1,0:T(8,128)S(1)}, f32[24,128]{1,0:T(8,128)S(1)}, u32[]{:S(2)}, u32[]{:S(2)}) collective-permute-start(f32[24,128]{1,0:T(8,128)S(1)} %get-tuple-element.72), channel_id=1, source_target_pairs={{0,6},{2,0},{4,2},{6,4},{1,7},{3,1},{5,3},{7,5},{8,14},{10,8},{12,... | collective-permute-start | bytes 36872 | tf_op jit(solution)/shard_map/ppermute | solution.py:186
  41.7 4.7 %collective-permute-start.9 = (f32[56,128]{1,0:T(8,128)S(1)}, f32[56,128]{1,0:T(8,128)S(1)}, u32[]{:S(2)}, u32[]{:S(2)}) collective-permute-start(f32[56,128]{1,0:T(8,128)S(1)} %get-tuple-element.74), channel_id=1, source_target_pairs={{0,1},{1,0},{2,3},{3,2},{4,5},{5,4},{6,7},{7,6},{8,9},{9,8},{10,11... | collective-permute-start | bytes 86024 | tf_op jit(solution)/shard_map/ppermute | solution.py:189
  48.2 3.1 %collective-permute-start.10 = (f32[16,128]{1,0:T(8,128)S(1)}, f32[16,128]{1,0:T(8,128)S(1)}, u32[]{:S(2)}, u32[]{:S(2)}) collective-permute-start(f32[16,128]{1,0:T(8,128)S(1)} %get-tuple-element.77), channel_id=1, source_target_pairs={{0,8},{8,16},{16,24},{24,0},{1,9},{9,17},{17,25},{25,1},{2,10},{10... | collective-permute-start | bytes 24584 | tf_op jit(solution)/shard_map/ppermute | solution.py:181
  48.2 3.1 %collective-permute-start.11 = (f32[16,128]{1,0:T(8,128)S(1)}, f32[16,128]{1,0:T(8,128)S(1)}, u32[]{:S(2)}, u32[]{:S(2)}) collective-permute-start(f32[16,128]{1,0:T(8,128)S(1)} %get-tuple-element.78), channel_id=1, source_target_pairs={{0,24},{8,0},{16,8},{24,16},{1,25},{9,1},{17,9},{25,17},{2,26},{10... | collective-permute-start | bytes 24584 | tf_op jit(solution)/shard_map/ppermute | solution.py:182
  51.3 5.5 %collective-permute-start.12 = (f32[24,128]{1,0:T(8,128)S(1)}, f32[24,128]{1,0:T(8,128)S(1)}, u32[]{:S(2)}, u32[]{:S(2)}) collective-permute-start(f32[24,128]{1,0:T(8,128)S(1)} %get-tuple-element.80), channel_id=1, source_target_pairs={{0,2},{2,4},{4,6},{6,0},{1,3},{3,5},{5,7},{7,1},{8,10},{10,12},{12... | collective-permute-start | bytes 36872 | tf_op jit(solution)/shard_map/ppermute | solution.py:185
  51.4 5.5 %collective-permute-start.13 = (f32[24,128]{1,0:T(8,128)S(1)}, f32[24,128]{1,0:T(8,128)S(1)}, u32[]{:S(2)}, u32[]{:S(2)}) collective-permute-start(f32[24,128]{1,0:T(8,128)S(1)} %get-tuple-element.81), channel_id=1, source_target_pairs={{0,6},{2,0},{4,2},{6,4},{1,7},{3,1},{5,3},{7,5},{8,14},{10,8},{12,... | collective-permute-start | bytes 36872 | tf_op jit(solution)/shard_map/ppermute | solution.py:186
  56.9 3.9 %collective-permute-start.14 = (f32[56,128]{1,0:T(8,128)S(1)}, f32[56,128]{1,0:T(8,128)S(1)}, u32[]{:S(2)}, u32[]{:S(2)}) collective-permute-start(f32[56,128]{1,0:T(8,128)S(1)} %get-tuple-element.84), channel_id=1, source_target_pairs={{0,1},{1,0},{2,3},{3,2},{4,5},{5,4},{6,7},{7,6},{8,9},{9,8},{10,11... | collective-permute-start | bytes 86024 | tf_op jit(solution)/shard_map/ppermute | solution.py:189
